TPU v7x, 8 devices: a whole 2x2x1 slice. The times are simulated.
8 devices in a mesh: replica: 2 (over z, y), stage: 4 (over x, core).
Axes of the slice: x: 2, y: 2, z: 1, core: 2. Of those that a mesh axis runs over, the one named last changes fastest.
Arguments:
- x_dec: bfloat16 [8, 8, 576], P('replica'), parts along dimension 0
- x_pre: bfloat16 [8, 64, 576], P('replica'), parts along dimension 0
- dec_len: int32 [8, 8], P('replica'), parts along dimension 0
- pre_len: int32 [2], P('replica'), parts along dimension 0
- g_attn: bfloat16 [4, 576], P('stage')
- w_q: bfloat16 [4, 576, 576], P('stage')
- w_k: bfloat16 [4, 576, 192], P('stage')
- w_v: bfloat16 [4, 576, 192], P('stage')
- w_o: bfloat16 [4, 576, 576], P('stage')
- g_mlp: bfloat16 [4, 576], P('stage')
- w_gate: bfloat16 [4, 576, 1536], P('stage')
- w_up: bfloat16 [4, 576, 1536], P('stage')
- w_down: bfloat16 [4, 1536, 576], P('stage')
- g_final: bfloat16 [576], replicated
- w_head: bfloat16 [576, 1024], replicated
- k_dec: bfloat16 [4, 8, 8, 512, 3, 64], P('stage', 'replica'), parts along dimension 1
- v_dec: bfloat16 [4, 8, 8, 512, 3, 64], P('stage', 'replica'), parts along dimension 1
- k_pre: bfloat16 [4, 1024, 3, 64], P('stage', 'replica'), parts along dimension 1
- v_pre: bfloat16 [4, 1024, 3, 64], P('stage', 'replica'), parts along dimension 1
Outputs:
- output 1: float32 [8, 9, 1024], P('replica'), parts along dimension 0
- output 2: bfloat16 [4, 8, 8, 512, 3, 64], P('stage', 'replica'), parts along dimension 1
- output 3: bfloat16 [4, 8, 8, 512, 3, 64], P('stage', 'replica'), parts along dimension 1
- output 4: bfloat16 [4, 1024, 3, 64], P('stage', 'replica'), parts along dimension 1
- output 5: bfloat16 [4, 1024, 3, 64], P('stage', 'replica'), parts along dimension 1
There are 2 independent parts. A program takes and returns all parts, laid end to end along the dimension named above; an argument that names none is the same for every part.
All inputs are finite; a program needn't handle non-finite values.
Results may differ from a plain program's by a relative error of at most 0.0189117.
Values are sent between devices in bfloat16 or wider.
A program may use at most 1 GiB of HBM per device.

v0:
```python
import jax
import jax.numpy as jnp
from jax import lax
from jax.sharding import PartitionSpec as P

NORM_EPS = 1e-6
ROPE_BASE = 10000.0


def rms_norm(acts, gain):
    acts_f = acts.astype(jnp.float32)
    inv_rms = lax.rsqrt(jnp.mean(acts_f * acts_f, axis=-1, keepdims=True) + NORM_EPS)
    return (acts_f * inv_rms * gain.astype(jnp.float32)).astype(jnp.bfloat16)


def rotate(proj, positions):
    head_dim = proj.shape[-1]
    half_dim = head_dim // 2
    inv_freq = ROPE_BASE ** (-jnp.arange(half_dim, dtype=jnp.float32) * (2.0 / head_dim))
    angles = positions.astype(jnp.float32)[:, None, None] * inv_freq
    cosine = jnp.cos(angles)
    sine_v = jnp.sin(angles)
    first_h = proj[..., :half_dim]
    second_h = proj[..., half_dim:]
    return jnp.concatenate([first_h * cosine - second_h * sine_v, second_h * cosine + first_h * sine_v], axis=-1)


def project(normed, positions, wq_l, wk_l, wv_l, kv_count, head_dim):
    n_rows = normed.shape[0]
    q_heads = wq_l.shape[1] // head_dim
    q_proj = jnp.dot(normed, wq_l, preferred_element_type=jnp.float32).reshape(n_rows, q_heads, head_dim)
    k_proj = jnp.dot(normed, wk_l, preferred_element_type=jnp.float32).reshape(n_rows, kv_count, head_dim)
    q_grp = rotate(q_proj, positions).astype(jnp.bfloat16).reshape(n_rows, kv_count, q_heads // kv_count, head_dim)
    k_new = rotate(k_proj, positions).astype(jnp.bfloat16)
    v_new = jnp.dot(normed, wv_l, preferred_element_type=jnp.float32).astype(jnp.bfloat16).reshape(n_rows, kv_count, head_dim)
    return q_grp, k_new, v_new


def attend(q_grp, keys_in, values_in, valid, score_form, mix_form):
    att_scale = q_grp.shape[-1] ** -0.5
    scores = jnp.einsum(score_form, q_grp, keys_in, preferred_element_type=jnp.float32) * att_scale
    probs = jax.nn.softmax(jnp.where(valid, scores, -1e30), axis=-1).astype(jnp.bfloat16)
    mixed = jnp.einsum(mix_form, probs, values_in, preferred_element_type=jnp.float32)
    return mixed.astype(jnp.bfloat16).reshape(q_grp.shape[0], -1)


def finish(acts, attn_out, wo_l, g_ffn, wg_l, wu_l, wd_l):
    acts = (acts.astype(jnp.float32) + jnp.dot(attn_out, wo_l, preferred_element_type=jnp.float32)).astype(jnp.bfloat16)
    normed = rms_norm(acts, g_ffn)
    gate_f = jnp.dot(normed, wg_l, preferred_element_type=jnp.float32)
    up_proj = jnp.dot(normed, wu_l, preferred_element_type=jnp.float32)
    hidden_act = (jax.nn.silu(gate_f) * up_proj).astype(jnp.bfloat16)
    return (acts.astype(jnp.float32) + jnp.dot(hidden_act, wd_l, preferred_element_type=jnp.float32)).astype(jnp.bfloat16)


def run_stages(src_rows, n_keep, keep_fn, stage_fn, caches, fwd_perm):
    n_micro, n_rows, hidden = src_rows.shape
    stage_idx = lax.axis_index('stage')
    n_ticks = n_micro + len(fwd_perm)

    def tick_fn(tick_idx, loop_carry):
        in_rows, collect, cache_state = loop_carry
        micro_idx = tick_idx - stage_idx
        active = (micro_idx >= 0) & (micro_idx < n_micro)
        micro_c = jnp.clip(micro_idx, 0, n_micro - 1)

        def compute(carry_in):
            rows_in, collect_in, caches_in = carry_in
            first_in = lax.dynamic_index_in_dim(src_rows, micro_c, 0, keepdims=False)
            acts = jnp.where(stage_idx == 0, first_in, rows_in)
            acts, caches_out = stage_fn(acts, micro_c, caches_in)
            collect_out = lax.dynamic_update_slice(collect_in, keep_fn(acts)[None], (micro_c, 0, 0))
            return acts, collect_out, caches_out

        sent_rows, collect, cache_state = lax.cond(active, compute, lambda carry_in: carry_in, (in_rows, collect, cache_state))
        return lax.ppermute(sent_rows, 'stage', fwd_perm), collect, cache_state

    init_carry = (jnp.zeros((n_rows, hidden), src_rows.dtype), jnp.zeros((n_micro, n_keep, hidden), src_rows.dtype), caches)
    last_carry = lax.fori_loop(0, n_ticks, tick_fn, init_carry)
    return last_carry[1], last_carry[2]


def solution(mesh):
    n_stages = mesh.shape['stage']
    fwd_perm = [(src_idx, src_idx + 1) for src_idx in range(n_stages - 1)]
    part_spec = P('replica')
    layer_spec = P('stage')
    cache_spec = P('stage', 'replica')
    in_specs = (part_spec,) * 4 + (layer_spec,) * 9 + (P(), P()) + (cache_spec,) * 4
    out_specs = (part_spec,) + (cache_spec,) * 4

    def device_fn(x_dec, x_pre, dec_len, pre_len, g_attn, w_q, w_k, w_v, w_o, g_mlp, w_gate, w_up, w_down, g_final, w_head, k_dec, v_dec, k_pre, v_pre):
        n_micro, dec_rows, hidden = x_dec.shape
        seg_len = x_pre.shape[1]
        local_layers, cache_len, kv_count, head_dim = k_pre.shape
        stage_idx = lax.axis_index('stage')
        cache_pos = jnp.arange(cache_len)

        def stage_fn(acts, micro_c, caches):
            kd_all, vd_all, kp_all, vp_all = caches
            dec_pos = lax.dynamic_index_in_dim(dec_len, micro_c, 0, keepdims=False)
            pre_begin = pre_len[0] + micro_c * seg_len
            pre_pos = pre_begin + jnp.arange(seg_len)
            positions = jnp.concatenate([dec_pos, pre_pos])
            hit = (cache_pos[None, :] == dec_pos[:, None])[:, :, None, None]
            dec_valid = (cache_pos[None, :] <= dec_pos[:, None])[:, None, None, :]
            pre_valid = (cache_pos[None, :] <= pre_pos[:, None])[:, None, None, :]
            for layer_idx in range(local_layers):
                normed = rms_norm(acts, g_attn[layer_idx])
                q_grp, k_new, v_new = project(normed, positions, w_q[layer_idx], w_k[layer_idx], w_v[layer_idx], kv_count, head_dim)
                kd_m = jnp.where(hit, k_new[:dec_rows, None], lax.dynamic_index_in_dim(kd_all[layer_idx], micro_c, 0, keepdims=False))
                vd_m = jnp.where(hit, v_new[:dec_rows, None], lax.dynamic_index_in_dim(vd_all[layer_idx], micro_c, 0, keepdims=False))
                kd_all = lax.dynamic_update_slice(kd_all, kd_m[None, None], (layer_idx, micro_c, 0, 0, 0, 0))
                vd_all = lax.dynamic_update_slice(vd_all, vd_m[None, None], (layer_idx, micro_c, 0, 0, 0, 0))
                kp_all = lax.dynamic_update_slice(kp_all, k_new[None, dec_rows:], (layer_idx, pre_begin, 0, 0))
                vp_all = lax.dynamic_update_slice(vp_all, v_new[None, dec_rows:], (layer_idx, pre_begin, 0, 0))
                attn_out = jnp.concatenate([
                    attend(q_grp[:dec_rows], kd_m, vd_m, dec_valid, 'bkgd,bskd->bkgs', 'bkgs,bskd->bkgd'),
                    attend(q_grp[dec_rows:], kp_all[layer_idx], vp_all[layer_idx], pre_valid, 'ikgd,skd->ikgs', 'ikgs,skd->ikgd')], axis=0)
                acts = finish(acts, attn_out, w_o[layer_idx], g_mlp[layer_idx], w_gate[layer_idx], w_up[layer_idx], w_down[layer_idx])
            return acts, (kd_all, vd_all, kp_all, vp_all)

        def keep_rows(acts):
            return jnp.concatenate([acts[:dec_rows], acts[-1:]], axis=0)

        src_rows = jnp.concatenate([x_dec, x_pre], axis=1)
        collect, caches = run_stages(src_rows, dec_rows + 1, keep_rows, stage_fn, (k_dec, v_dec, k_pre, v_pre), fwd_perm)
        last_rows = lax.psum(jnp.where(stage_idx == n_stages - 1, collect, jnp.zeros_like(collect)), 'stage')
        final_h = rms_norm(last_rows, g_final)
        logits = jnp.dot(final_h.reshape(-1, hidden), w_head, preferred_element_type=jnp.float32).reshape(n_micro, dec_rows + 1, -1)
        return (logits,) + caches

    return jax.shard_map(device_fn, mesh=mesh, in_specs=in_specs, out_specs=out_specs, check_vma=False)
```

profile of v0, /device:TPU:7, one launch (start us, length us, event | category | flops | bytes accessed | tf_op | source)
XLA Modules:
  0.0 335.8 jit_solution(9233997881058872508)
XLA Ops:
  0.7 6.4 %copy.90 = bf16[1,4,8,512,3,64]{3,5,4,2,1,0:T(8,128)(2,1)} copy(bf16[1,4,8,512,3,64]{3,5,4,2,1,0:T(8,128)(2,1)} %param.38) | data formatting | bytes 12582912
  7.1 2.9 copy.91
  11.4 2.3 copy.42
  13.7 2.4 copy.40
  16.1 1.6 pad_maximum_fusion.2
  19.8 302.1 %while.25 = (s32[]{:T(128)}, bf16[72,576]{1,0:T(8,128)(2,1)}, bf16[4,9,576]{2,1,0:T(8,128)(2,1)}, bf16[1,4,8,512,3,64]{3,5,4,2,1,0:T(8,128)(2,1)}, bf16[1,4,8,51...) while((s32[]{:T(128)}, bf16[72,576]{1,0:T(8,128)(2,1)}, ...), condition=%wide.region_9.10_spmd.clone.clone, body=%wide.region_0.9_spmd.clone.clone.sunk | while | flops 602316864 | bytes 27632996 | solution.py:79
  20.4 1.3 collective-permute-start
  21.7 2.1 collective-permute-done
  25.0 1.3 collective-permute-start
  26.3 4.6 %collective-permute-done = bf16[72,576]{1,0:T(8,128)(2,1)S(1)} collective-permute-done((bf16[72,576]{1,0:T(8,128)(2,1)}, bf16[72,576]{1,0:T(8,128)(2,1)S(1)}, u32[]{:S(2)}, u32[]{:S(2)}) %collective-permute-start) | collective-permute-done | bytes 82976 | tf_op jit(solution)/shard_map/while/body/eval_jaxpr/ppermute | solution.py:76
  33.4 112.2 %collective-permute-done = bf16[72,576]{1,0:T(8,128)(2,1)S(1)} collective-permute-done((bf16[72,576]{1,0:T(8,128)(2,1)}, bf16[72,576]{1,0:T(8,128)(2,1)S(1)}, u32[]{:S(2)}, u32[]{:S(2)}) %collective-permute-start) | collective-permute-done | bytes 82976 | tf_op jit(solution)/shard_map/while/body/eval_jaxpr/ppermute | solution.py:76
  146.8 37.5 %conditional.4 = ((bf16[72,576]{1,0:T(8,128)(2,1)}, bf16[4,9,576]{2,1,0:T(8,128)(2,1)}, bf16[1,4,8,512,3,64]{3,5,4,2,1,0:T(8,128)(2,1)}, bf16[1,4,8,512,3,64]{3,...) conditional(s32[]{:T(128)} %convert_element_type.153, ...), branch_computations={%region_1.1_spmd, %region_2.8_spmd} | conditional | flops 602316864 | bytes 27132768 | solution.py:75
  147.9 1.3 convert_reduce_fusion
  149.2 1.5 fusion.62
  155.8 1.4 broadcast_compare_fusion.2
  157.2 3.2 fusion.101
  161.4 2.1 fusion.38
  163.5 3.5 %select_dynamic-update-slice_fusion = (bf16[1,4,8,512,3,64]{3,5,4,2,1,0:T(8,128)(2,1)}, bf16[1,4,8,512,3,64]{3,5,4,2,1,0:T(8,128)(2,1)}) fusion(bf16[1,4,8,512,3,64]{3,5,4,2,1,0:T(8,128)(2,1)} %get-tuple-element.442, s32[]{:T(128)S(6)} %min.9, pred[8,512]{1,0:T(8,128)(4,1)S(1)} %get-tuple-element.699, bf16[8,3,64]{2,1,0:T(4,128)(2,1)S(1)} %broadcast_in_dim.98, ...), kind=kLoop, calls=%fused_computation.14 | loop fusion | flops 1572864 | bytes 6301700 | tf_op jit(solution)/shard_map/while/body/eval_jaxpr/cond/branch_1_fun/dynamic_update_slice | solution.py:114
  167.9 2.0 dynamic_update_slice.16
  170.2 2.5 fusion.98
  172.8 2.0 dynamic_update_slice.15
  174.9 1.9 convolution_convert_fusion
  178.5 3.7 %fusion.33 = bf16[72,576]{1,0:T(8,128)(2,1)} fusion(f32[72,576]{1,0:T(8,128)S(1)} %get-tuple-element.705, bf16[1,1536,576]{2,1,0:T(8,128)(2,1)} %get-tuple-element.450, bf16[1,576,1536]{2,1,0:T(8,128)(2,1)} %get-tuple-element.449, f32[72,1536]{1,0:T(8,128)} %fusion.8, f32[576]{0:T(1024)S(1)} %copy-done.10, f32[72]{0:T(128)S(1)} %add_rsqrt_fusion), kind=kOutput, calls=%fused_computation.35 | convolution fusion | flops 255674880 | bytes 4232736 | tf_op jit(solution)/shard_map/while/body/eval_jaxpr/cond/branch_1_fun/dot_general | solution.py:53
  185.6 4.6 %collective-permute-done = bf16[72,576]{1,0:T(8,128)(2,1)S(1)} collective-permute-done((bf16[72,576]{1,0:T(8,128)(2,1)}, bf16[72,576]{1,0:T(8,128)(2,1)S(1)}, u32[]{:S(2)}, u32[]{:S(2)}) %collective-permute-start) | collective-permute-done | bytes 82976 | tf_op jit(solution)/shard_map/while/body/eval_jaxpr/ppermute | solution.py:76
  191.4 37.5 %conditional.4 = ((bf16[72,576]{1,0:T(8,128)(2,1)}, bf16[4,9,576]{2,1,0:T(8,128)(2,1)}, bf16[1,4,8,512,3,64]{3,5,4,2,1,0:T(8,128)(2,1)}, bf16[1,4,8,512,3,64]{3,...) conditional(s32[]{:T(128)} %convert_element_type.153, ...), branch_computations={%region_1.1_spmd, %region_2.8_spmd} | conditional | flops 602316864 | bytes 27132768 | solution.py:75
  192.5 1.3 convert_reduce_fusion
  193.8 1.5 fusion.62
  200.4 1.4 broadcast_compare_fusion.2
  201.8 3.2 fusion.101
  206.0 2.1 fusion.38
  208.1 3.5 %select_dynamic-update-slice_fusion = (bf16[1,4,8,512,3,64]{3,5,4,2,1,0:T(8,128)(2,1)}, bf16[1,4,8,512,3,64]{3,5,4,2,1,0:T(8,128)(2,1)}) fusion(bf16[1,4,8,512,3,64]{3,5,4,2,1,0:T(8,128)(2,1)} %get-tuple-element.442, s32[]{:T(128)S(6)} %min.9, pred[8,512]{1,0:T(8,128)(4,1)S(1)} %get-tuple-element.699, bf16[8,3,64]{2,1,0:T(4,128)(2,1)S(1)} %broadcast_in_dim.98, ...), kind=kLoop, calls=%fused_computation.14 | loop fusion | flops 1572864 | bytes 6301700 | tf_op jit(solution)/shard_map/while/body/eval_jaxpr/cond/branch_1_fun/dynamic_update_slice | solution.py:114
  212.5 2.0 dynamic_update_slice.16
  214.8 2.5 fusion.98
  217.4 2.0 dynamic_update_slice.15
  219.5 1.9 convolution_convert_fusion
  223.1 3.7 %fusion.33 = bf16[72,576]{1,0:T(8,128)(2,1)} fusion(f32[72,576]{1,0:T(8,128)S(1)} %get-tuple-element.705, bf16[1,1536,576]{2,1,0:T(8,128)(2,1)} %get-tuple-element.450, bf16[1,576,1536]{2,1,0:T(8,128)(2,1)} %get-tuple-element.449, f32[72,1536]{1,0:T(8,128)} %fusion.8, f32[576]{0:T(1024)S(1)} %copy-done.10, f32[72]{0:T(128)S(1)} %add_rsqrt_fusion), kind=kOutput, calls=%fused_computation.35 | convolution fusion | flops 255674880 | bytes 4232736 | tf_op jit(solution)/shard_map/while/body/eval_jaxpr/cond/branch_1_fun/dot_general | solution.py:53
  230.2 4.6 %collective-permute-done = bf16[72,576]{1,0:T(8,128)(2,1)S(1)} collective-permute-done((bf16[72,576]{1,0:T(8,128)(2,1)}, bf16[72,576]{1,0:T(8,128)(2,1)S(1)}, u32[]{:S(2)}, u32[]{:S(2)}) %collective-permute-start) | collective-permute-done | bytes 82976 | tf_op jit(solution)/shard_map/while/body/eval_jaxpr/ppermute | solution.py:76
  236.0 37.5 %conditional.4 = ((bf16[72,576]{1,0:T(8,128)(2,1)}, bf16[4,9,576]{2,1,0:T(8,128)(2,1)}, bf16[1,4,8,512,3,64]{3,5,4,2,1,0:T(8,128)(2,1)}, bf16[1,4,8,512,3,64]{3,...) conditional(s32[]{:T(128)} %convert_element_type.153, ...), branch_computations={%region_1.1_spmd, %region_2.8_spmd} | conditional | flops 602316864 | bytes 27132768 | solution.py:75
  237.1 1.3 convert_reduce_fusion
  238.4 1.5 fusion.62
  245.0 1.4 broadcast_compare_fusion.2
  246.4 3.2 fusion.101
  250.6 2.1 fusion.38
  252.7 3.5 %select_dynamic-update-slice_fusion = (bf16[1,4,8,512,3,64]{3,5,4,2,1,0:T(8,128)(2,1)}, bf16[1,4,8,512,3,64]{3,5,4,2,1,0:T(8,128)(2,1)}) fusion(bf16[1,4,8,512,3,64]{3,5,4,2,1,0:T(8,128)(2,1)} %get-tuple-element.442, s32[]{:T(128)S(6)} %min.9, pred[8,512]{1,0:T(8,128)(4,1)S(1)} %get-tuple-element.699, bf16[8,3,64]{2,1,0:T(4,128)(2,1)S(1)} %broadcast_in_dim.98, ...), kind=kLoop, calls=%fused_computation.14 | loop fusion | flops 1572864 | bytes 6301700 | tf_op jit(solution)/shard_map/while/body/eval_jaxpr/cond/branch_1_fun/dynamic_update_slice | solution.py:114
  257.1 2.0 dynamic_update_slice.16
  259.4 2.5 fusion.98
  262.0 2.0 dynamic_update_slice.15
  264.1 1.9 convolution_convert_fusion
  267.7 3.7 %fusion.33 = bf16[72,576]{1,0:T(8,128)(2,1)} fusion(f32[72,576]{1,0:T(8,128)S(1)} %get-tuple-element.705, bf16[1,1536,576]{2,1,0:T(8,128)(2,1)} %get-tuple-element.450, bf16[1,576,1536]{2,1,0:T(8,128)(2,1)} %get-tuple-element.449, f32[72,1536]{1,0:T(8,128)} %fusion.8, f32[576]{0:T(1024)S(1)} %copy-done.10, f32[72]{0:T(128)S(1)} %add_rsqrt_fusion), kind=kOutput, calls=%fused_computation.35 | convolution fusion | flops 255674880 | bytes 4232736 | tf_op jit(solution)/shard_map/while/body/eval_jaxpr/cond/branch_1_fun/dot_general | solution.py:53
  274.8 4.6 %collective-permute-done = bf16[72,576]{1,0:T(8,128)(2,1)S(1)} collective-permute-done((bf16[72,576]{1,0:T(8,128)(2,1)}, bf16[72,576]{1,0:T(8,128)(2,1)S(1)}, u32[]{:S(2)}, u32[]{:S(2)}) %collective-permute-start) | collective-permute-done | bytes 82976 | tf_op jit(solution)/shard_map/while/body/eval_jaxpr/ppermute | solution.py:76
  280.6 37.5 %conditional.4 = ((bf16[72,576]{1,0:T(8,128)(2,1)}, bf16[4,9,576]{2,1,0:T(8,128)(2,1)}, bf16[1,4,8,512,3,64]{3,5,4,2,1,0:T(8,128)(2,1)}, bf16[1,4,8,512,3,64]{3,...) conditional(s32[]{:T(128)} %convert_element_type.153, ...), branch_computations={%region_1.1_spmd, %region_2.8_spmd} | conditional | flops 602316864 | bytes 27132768 | solution.py:75
  281.7 1.3 convert_reduce_fusion
  283.0 1.5 fusion.62
  289.6 1.4 broadcast_compare_fusion.2
  291.1 3.2 fusion.101
  295.2 2.1 fusion.38
  297.3 3.5 %select_dynamic-update-slice_fusion = (bf16[1,4,8,512,3,64]{3,5,4,2,1,0:T(8,128)(2,1)}, bf16[1,4,8,512,3,64]{3,5,4,2,1,0:T(8,128)(2,1)}) fusion(bf16[1,4,8,512,3,64]{3,5,4,2,1,0:T(8,128)(2,1)} %get-tuple-element.442, s32[]{:T(128)S(6)} %min.9, pred[8,512]{1,0:T(8,128)(4,1)S(1)} %get-tuple-element.699, bf16[8,3,64]{2,1,0:T(4,128)(2,1)S(1)} %broadcast_in_dim.98, ...), kind=kLoop, calls=%fused_computation.14 | loop fusion | flops 1572864 | bytes 6301700 | tf_op jit(solution)/shard_map/while/body/eval_jaxpr/cond/branch_1_fun/dynamic_update_slice | solution.py:114
  301.7 2.0 dynamic_update_slice.16
  304.0 2.5 fusion.98
  306.6 2.0 dynamic_update_slice.15
  308.7 1.9 convolution_convert_fusion
  312.3 3.7 %fusion.33 = bf16[72,576]{1,0:T(8,128)(2,1)} fusion(f32[72,576]{1,0:T(8,128)S(1)} %get-tuple-element.705, bf16[1,1536,576]{2,1,0:T(8,128)(2,1)} %get-tuple-element.450, bf16[1,576,1536]{2,1,0:T(8,128)(2,1)} %get-tuple-element.449, f32[72,1536]{1,0:T(8,128)} %fusion.8, f32[576]{0:T(1024)S(1)} %copy-done.10, f32[72]{0:T(128)S(1)} %add_rsqrt_fusion), kind=kOutput, calls=%fused_computation.35 | convolution fusion | flops 255674880 | bytes 4232736 | tf_op jit(solution)/shard_map/while/body/eval_jaxpr/cond/branch_1_fun/dot_general | solution.py:53
  319.4 1.9 collective-permute-done
  322.8 11.0 %psum.7 = bf16[4,9,576]{2,1,0:T(8,128)(2,1)S(1)} all-reduce(bf16[4,9,576]{2,1,0:T(8,128)(2,1)S(1)} %broadcast_select_fusion), channel_id=1, replica_groups=mesh['replica'=2,'stage'=4] {'stage'}, use_global_device_ids=true, to_apply=%region_10.11 | all-reduce | flops 20736 | bytes 82944 | tf_op jit(solution)/shard_map/psum | solution.py:128
  (265 shorter events, 66.8 us)
Async XLA Ops:
  0.6 334.0 %copy-start = (bf16[576,1024]{1,0:T(8,128)(2,1)S(1)}, bf16[576,1024]{1,0:T(8,128)(2,1)}, u32[]{:S(2)}) copy-start(bf16[576,1024]{1,0:T(8,128)(2,1)} %param.37) | copy-start | bytes 3538948
  0.6 6.5 %copy-start.5 = (bf16[1,4,8,512,3,64]{3,5,4,2,1,0:T(8,128)(2,1)S(1)}, bf16[1,4,8,512,3,64]{3,5,4,2,1,0:T(8,128)(2,1)}, u32[]{:S(2)}) copy-start(bf16[1,4,8,512,3,64]{3,5,4,2,1,0:T(8,128)(2,1)} %param.39) | copy-start | bytes 18874372
  7.1 2.9 copy-start.13
  7.1 3.6 %copy-start.14 = (bf16[1,512,3,64]{1,3,2,0:T(8,128)(2,1)S(1)}, bf16[1,512,3,64]{1,3,2,0:T(8,128)(2,1)}, u32[]{:S(2)}) copy-start(bf16[1,512,3,64]{1,3,2,0:T(8,128)(2,1)} %param.41) | copy-start | bytes 589828
  7.1 4.3 %copy-start.8 = (bf16[1,1536,576]{1,2,0:T(8,128)(2,1)S(1)}, bf16[1,1536,576]{1,2,0:T(8,128)(2,1)}, u32[]{:S(2)}) copy-start(bf16[1,1536,576]{1,2,0:T(8,128)(2,1)} %param.35) | copy-start | bytes 5308420
  11.4 4.7 %copy-start.11 = (bf16[4,64,576]{2,1,0:T(8,128)(2,1)S(1)}, bf16[4,64,576]{2,1,0:T(8,128)(2,1)}, u32[]{:S(2)}) copy-start(bf16[4,64,576]{2,1,0:T(8,128)(2,1)} %param.24) | copy-start | bytes 884740
  13.7 4.0 %copy-start.12 = (bf16[1,576,192]{1,2,0:T(8,128)(2,1)S(1)}, bf16[1,576,192]{1,2,0:T(8,128)(2,1)}, u32[]{:S(2)}) copy-start(bf16[1,576,192]{1,2,0:T(8,128)(2,1)} %param.30) | copy-start | bytes 663556
  13.7 6.1 %copy-start.1 = (bf16[1,576,1536]{2,1,0:T(8,128)(2,1)S(1)}, bf16[1,576,1536]{2,1,0:T(8,128)(2,1)}, u32[]{:S(2)}) copy-start(bf16[1,576,1536]{2,1,0:T(8,128)(2,1)} %param.33) | copy-start | bytes 5308420
  20.4 3.4 collective-permute-start
  25.0 5.9 %collective-permute-start = (bf16[72,576]{1,0:T(8,128)(2,1)}, bf16[72,576]{1,0:T(8,128)(2,1)S(1)}, u32[]{:S(2)}, u32[]{:S(2)}) collective-permute-start(bf16[72,576]{1,0:T(8,128)(2,1)} %get-tuple-element.835), channel_id=1, source_target_pairs={{0,1},{1,2},{2,3},{4,5},{5,6},{6,7}} | collective-permute-start | bytes 248840 | tf_op jit(solution)/shard_map/while/body/eval_jaxpr/ppermute | solution.py:76
  32.1 113.4 %collective-permute-start = (bf16[72,576]{1,0:T(8,128)(2,1)}, bf16[72,576]{1,0:T(8,128)(2,1)S(1)}, u32[]{:S(2)}, u32[]{:S(2)}) collective-permute-start(bf16[72,576]{1,0:T(8,128)(2,1)} %get-tuple-element.835), channel_id=1, source_target_pairs={{0,1},{1,2},{2,3},{4,5},{5,6},{6,7}} | collective-permute-start | bytes 248840 | tf_op jit(solution)/shard_map/while/body/eval_jaxpr/ppermute | solution.py:76
  147.9 5.9 %copy-start.15 = (f32[72]{0:T(128)}, f32[72]{0:T(128)S(1)}, u32[]{:S(2)}) copy-start(f32[72]{0:T(128)S(1)} %add_rsqrt_fusion.1) | copy-start | bytes 868 | tf_op jit(solution)/shard_map/while/body/eval_jaxpr/cond
  151.4 2.4 copy-start.17
  152.9 0.8 copy-start.7
  157.2 3.2 copy-start.4
  157.2 3.2 copy-start.16
  160.7 0.6 copy-start.6
  163.5 6.6 %copy-start.9 = (s32[512]{0:T(512)S(1)}, s32[512]{0:T(512)}, u32[]{:S(2)}) copy-start(s32[512]{0:T(512)} %get-tuple-element.444) | copy-start | bytes 6148 | tf_op jit(solution)/shard_map/while/body/eval_jaxpr/cond
  163.5 6.6 %copy-start.18 = (s32[64]{0:T(128)S(1)}, s32[64]{0:T(128)}, u32[]{:S(2)}) copy-start(s32[64]{0:T(128)} %copy-done.17) | copy-start | bytes 772 | tf_op jit(solution)/shard_map/while/body/eval_jaxpr/cond
  167.0 5.7 %slice-start = ((bf16[72,192]{1,0:T(8,128)(2,1)}), bf16[64,192]{1,0:T(8,128)(2,1)S(1)}, s32[]{:S(2)}) async-start(bf16[72,192]{1,0:T(8,128)(2,1)} %copy-done.6), calls=%async_computation | async-start | bytes 65536 | tf_op jit(solution)/shard_map/while/body/eval_jaxpr/cond/branch_1_fun/slice | solution.py:116
  174.8 1.9 copy-start.2
  174.9 1.9 copy-start.3
  174.9 2.4 copy-start.10
  184.3 5.9 %collective-permute-start = (bf16[72,576]{1,0:T(8,128)(2,1)}, bf16[72,576]{1,0:T(8,128)(2,1)S(1)}, u32[]{:S(2)}, u32[]{:S(2)}) collective-permute-start(bf16[72,576]{1,0:T(8,128)(2,1)} %get-tuple-element.835), channel_id=1, source_target_pairs={{0,1},{1,2},{2,3},{4,5},{5,6},{6,7}} | collective-permute-start | bytes 248840 | tf_op jit(solution)/shard_map/while/body/eval_jaxpr/ppermute | solution.py:76
  192.5 5.9 %copy-start.15 = (f32[72]{0:T(128)}, f32[72]{0:T(128)S(1)}, u32[]{:S(2)}) copy-start(f32[72]{0:T(128)S(1)} %add_rsqrt_fusion.1) | copy-start | bytes 868 | tf_op jit(solution)/shard_map/while/body/eval_jaxpr/cond
  196.0 2.4 copy-start.17
  196.7 0.6 copy-start.19
  197.5 0.8 copy-start.7
  201.8 3.2 copy-start.4
  201.8 3.2 copy-start.16
  205.3 0.6 copy-start.6
  208.1 6.6 %copy-start.9 = (s32[512]{0:T(512)S(1)}, s32[512]{0:T(512)}, u32[]{:S(2)}) copy-start(s32[512]{0:T(512)} %get-tuple-element.444) | copy-start | bytes 6148 | tf_op jit(solution)/shard_map/while/body/eval_jaxpr/cond
  208.1 6.6 %copy-start.18 = (s32[64]{0:T(128)S(1)}, s32[64]{0:T(128)}, u32[]{:S(2)}) copy-start(s32[64]{0:T(128)} %copy-done.17) | copy-start | bytes 772 | tf_op jit(solution)/shard_map/while/body/eval_jaxpr/cond
  211.6 5.7 %slice-start = ((bf16[72,192]{1,0:T(8,128)(2,1)}), bf16[64,192]{1,0:T(8,128)(2,1)S(1)}, s32[]{:S(2)}) async-start(bf16[72,192]{1,0:T(8,128)(2,1)} %copy-done.6), calls=%async_computation | async-start | bytes 65536 | tf_op jit(solution)/shard_map/while/body/eval_jaxpr/cond/branch_1_fun/slice | solution.py:116
  219.4 1.9 copy-start.2
  219.4 1.9 copy-start.3
  219.5 2.4 copy-start.10
  228.9 5.9 %collective-permute-start = (bf16[72,576]{1,0:T(8,128)(2,1)}, bf16[72,576]{1,0:T(8,128)(2,1)S(1)}, u32[]{:S(2)}, u32[]{:S(2)}) collective-permute-start(bf16[72,576]{1,0:T(8,128)(2,1)} %get-tuple-element.835), channel_id=1, source_target_pairs={{0,1},{1,2},{2,3},{4,5},{5,6},{6,7}} | collective-permute-start | bytes 248840 | tf_op jit(solution)/shard_map/while/body/eval_jaxpr/ppermute | solution.py:76
  237.1 5.9 %copy-start.15 = (f32[72]{0:T(128)}, f32[72]{0:T(128)S(1)}, u32[]{:S(2)}) copy-start(f32[72]{0:T(128)S(1)} %add_rsqrt_fusion.1) | copy-start | bytes 868 | tf_op jit(solution)/shard_map/while/body/eval_jaxpr/cond
  240.6 2.4 copy-start.17
  242.1 0.8 copy-start.7
  246.4 3.2 copy-start.4
  246.4 3.2 copy-start.16
  249.9 0.6 copy-start.6
  252.7 6.6 %copy-start.9 = (s32[512]{0:T(512)S(1)}, s32[512]{0:T(512)}, u32[]{:S(2)}) copy-start(s32[512]{0:T(512)} %get-tuple-element.444) | copy-start | bytes 6148 | tf_op jit(solution)/shard_map/while/body/eval_jaxpr/cond
  252.7 6.6 %copy-start.18 = (s32[64]{0:T(128)S(1)}, s32[64]{0:T(128)}, u32[]{:S(2)}) copy-start(s32[64]{0:T(128)} %copy-done.17) | copy-start | bytes 772 | tf_op jit(solution)/shard_map/while/body/eval_jaxpr/cond
  256.3 5.7 %slice-start = ((bf16[72,192]{1,0:T(8,128)(2,1)}), bf16[64,192]{1,0:T(8,128)(2,1)S(1)}, s32[]{:S(2)}) async-start(bf16[72,192]{1,0:T(8,128)(2,1)} %copy-done.6), calls=%async_computation | async-start | bytes 65536 | tf_op jit(solution)/shard_map/while/body/eval_jaxpr/cond/branch_1_fun/slice | solution.py:116
  264.1 1.9 copy-start.2
  264.1 1.9 copy-start.3
  264.1 2.4 copy-start.10
  273.5 5.9 %collective-permute-start = (bf16[72,576]{1,0:T(8,128)(2,1)}, bf16[72,576]{1,0:T(8,128)(2,1)S(1)}, u32[]{:S(2)}, u32[]{:S(2)}) collective-permute-start(bf16[72,576]{1,0:T(8,128)(2,1)} %get-tuple-element.835), channel_id=1, source_target_pairs={{0,1},{1,2},{2,3},{4,5},{5,6},{6,7}} | collective-permute-start | bytes 248840 | tf_op jit(solution)/shard_map/while/body/eval_jaxpr/ppermute | solution.py:76
  281.7 5.9 %copy-start.15 = (f32[72]{0:T(128)}, f32[72]{0:T(128)S(1)}, u32[]{:S(2)}) copy-start(f32[72]{0:T(128)S(1)} %add_rsqrt_fusion.1) | copy-start | bytes 868 | tf_op jit(solution)/shard_map/while/body/eval_jaxpr/cond
  285.2 2.4 copy-start.17
  286.7 0.8 copy-start.7
  291.1 3.2 copy-start.4
  291.1 3.2 copy-start.16
  294.5 0.6 copy-start.6
  297.3 6.6 %copy-start.9 = (s32[512]{0:T(512)S(1)}, s32[512]{0:T(512)}, u32[]{:S(2)}) copy-start(s32[512]{0:T(512)} %get-tuple-element.444) | copy-start | bytes 6148 | tf_op jit(solution)/shard_map/while/body/eval_jaxpr/cond
  297.3 6.6 %copy-start.18 = (s32[64]{0:T(128)S(1)}, s32[64]{0:T(128)}, u32[]{:S(2)}) copy-start(s32[64]{0:T(128)} %copy-done.17) | copy-start | bytes 772 | tf_op jit(solution)/shard_map/while/body/eval_jaxpr/cond
  300.9 5.7 %slice-start = ((bf16[72,192]{1,0:T(8,128)(2,1)}), bf16[64,192]{1,0:T(8,128)(2,1)S(1)}, s32[]{:S(2)}) async-start(bf16[72,192]{1,0:T(8,128)(2,1)} %copy-done.6), calls=%async_computation | async-start | bytes 65536 | tf_op jit(solution)/shard_map/while/body/eval_jaxpr/cond/branch_1_fun/slice | solution.py:116
  308.7 1.9 copy-start.2
  308.7 1.9 copy-start.3
  308.7 2.4 copy-start.10
  318.1 3.2 collective-permute-start
  (3 other events, 1.7 us)
where the time goes:
time: 339 us; the launch traced here: 336 us
  waiting for transfers between devices  134 us (40%)
  matrix products  73.1 us (22%)
  local copies, waits for them, and re-layouts  63.8 us (19%)
  other arithmetic  40.4 us (12%)
  blocking collectives  11 us (3%)
  starting transfers between devices  8.96 us (3%)
  loops' own time  3.48 us (1%)
    ppermute x7, waiting for transfers between devices, tick_fn(): return (lax.ppermute(sent_rows, 'stage', fwd_perm), collect, cache_state)  134 us
    sub x8, matrix products, attend(): jax.nn.softmax(jnp.where(valid, scores, -1e+30), axis=-1)  22.9 us
    unnamed x24, local copies, waits for them, and re-layouts  17.1 us
    dot_general x8, matrix products, attend(): jnp.einsum(mix_form, probs, values_in, preferred_element_type=jnp.float32)  16 us
    dot_general x4, matrix products, finish(): jnp.dot(hidden_act, wd_l, preferred_element_type=jnp.float32)  14.9 us
    dynamic_update_slice x4, other arithmetic, stage_fn(): lax.dynamic_update_slice(vd_all, vd_m[None, None], (layer_idx, micro_c, 0...  14.1 us
    psum x1, blocking collectives, device_fn(): lax.psum(jnp.where(stage_idx == n_stages - 1, collect, jnp.zeros_like(col...  11 us
    ppermute x7, starting transfers between devices, tick_fn(): return (lax.ppermute(sent_rows, 'stage', fwd_perm), collect, cache_state)  8.96 us
  transfers between devices with their start and end apart: 7, of which 7 were waited for; matrix products, arithmetic and copies ran while one was open for 0% of the time, Pallas kernels for 0%

commit v1 on v0

v1 whole, which is shorter than its diff:
```python
import functools

import jax
import jax.numpy as jnp
import numpy as np
from jax import lax
from jax.experimental import pallas as pl
from jax.experimental.pallas import tpu as pltpu
from jax.sharding import PartitionSpec as P

F32 = jnp.float32
BF16 = jnp.bfloat16
MESH = pl.DeviceIdType.MESH
NORM_EPS = 1e-6
ROPE_BASE = 10000.0
NEG = -1e30

HID = 576
NQ = 9
NKV = 3
GRP = 3
HD = 64
HALF = 32
KVW = NKV * HD
FFN = 1536
NM = 4
DR = 8
SEG = 64
CL = 512
VOC = 1024
ND = NM * DR
NP = NM * SEG
LAST = 3
LN = 128


def nt(a, b):
    return lax.dot_general(a, b, (((1,), (1,)), ((), ())), preferred_element_type=F32)


def nn(a, b):
    return jnp.dot(a, b, preferred_element_type=F32)


def rms(x, g):
    inv = lax.rsqrt(jnp.mean(x * x, axis=-1, keepdims=True) + NORM_EPS)
    return (x * inv * g).astype(BF16)


def rope_t(m, cos, sin):
    parts = []
    for j in range(m.shape[0] // HD):
        a = m[j * HD:j * HD + HALF]
        b = m[j * HD + HALF:(j + 1) * HD]
        parts += [a * cos - b * sin, b * cos + a * sin]
    return jnp.concatenate(parts, axis=0)


def lane_iota(shape):
    return lax.broadcasted_iota(jnp.int32, shape, len(shape) - 1)


def pipe_kernel(xd, xp, dlen, plen, ga, wq, wk, wv, wo, gm, wg, wu, wd, gf, wh, kd, vd, kp, vp, ifr,
                kdn, vdn, kpn, vpn, logits,
                xd_s, xp_s, dl_s, pl_s, ga_s, wq_s, wk_s, wv_s, wo_s, gm_s, wg_s, wu_s, wd_s, gf_s, wh_s,
                kd_s, vd_s, kp_s, vp_s, ifr_s,
                wqt_s, cosd_s, sind_s, cosp_s, sinp_s, cosl_s, sinl_s, qa_s, qb_s, self_s, vn_s, oa_s, ob_s,
                kdn_s, vdn_s, ot_s, act_s, x4_s, sd_s, sp_s, fh_s, fr_s, lg_s,
                in_sem, kd_sem, vd_sem, out_sem, sdd, sdp, rcd, rcp, sdf, rcf):
    st = lax.axis_index('stage')
    rep = lax.axis_index('replica')
    order = [(dlen, dl_s), (plen, pl_s), (xd, xd_s), (ga, ga_s), (ifr, ifr_s), (wq, wq_s), (wk, wk_s), (wv, wv_s),
             (kp, kp_s), (vp, vp_s), (wo, wo_s), (gm, gm_s), (wg, wg_s), (wu, wu_s), (wd, wd_s), (xp, xp_s), (gf, gf_s), (wh, wh_s)]
    cps = [pltpu.make_async_copy(a, b, in_sem.at[i]) for i, (a, b) in enumerate(order)]
    by = {id(b): c for (a, b), c in zip(order, cps)}
    kcp = [pltpu.make_async_copy(kd.at[m], kd_s.at[m], kd_sem.at[m]) for m in range(NM)]
    vcp = [pltpu.make_async_copy(vd.at[m], vd_s.at[m], vd_sem.at[m]) for m in range(NM)]

    def ld(ref):
        return by[id(ref)]

    for r in (dl_s, pl_s, ga_s, ifr_s, wq_s, wk_s, wv_s):
        ld(r).start()

    @pl.when(st == 0)
    def _():
        ld(xd_s).start()

    for m in range(NM):
        kcp[m].start()
        vcp[m].start()
    for r in (wo_s, gm_s, wg_s, wu_s, wd_s, kp_s, vp_s):
        ld(r).start()

    @pl.when(st == 0)
    def _():
        ld(xp_s).start()

    ld(gf_s).start()
    ld(wh_s).start()

    bar = pltpu.get_barrier_semaphore()
    for k in range(4):
        @pl.when(st != k)
        def _(k=k):
            pl.semaphore_signal(bar, inc=1, device_id={'stage': k}, device_id_type=MESH)

    ld(dl_s).wait()
    ld(pl_s).wait()
    ld(ifr_s).wait()
    p0 = pl_s[0]
    li = lane_iota((1, LN))
    posd = jnp.zeros((1, LN), jnp.int32)
    for b in range(ND):
        posd = jnp.where(li == b, dl_s[b // DR, b % DR], posd)
    fr = ifr_s[...]
    ang = fr[:, :LN] * posd.astype(F32)
    cosd_s[...] = jnp.cos(ang)
    sind_s[...] = jnp.sin(ang)
    ang = fr * (p0 + lane_iota((1, NP))).astype(F32)
    cosp_s[...] = jnp.cos(ang)
    sinp_s[...] = jnp.sin(ang)
    ang = fr[:, :LN] * (p0 + li * SEG + (SEG - 1)).astype(F32)
    cosl_s[...] = jnp.cos(ang)
    sinl_s[...] = jnp.sin(ang)
    qa_s[...] = jnp.zeros_like(qa_s)
    qb_s[...] = jnp.zeros_like(qb_s)
    ob_s[...] = jnp.zeros_like(ob_s)

    ld(ga_s).wait()
    ld(wq_s).wait()
    wqt_s[...] = wq_s[...].astype(F32).T.astype(BF16)
    ld(wk_s).wait()
    ld(wv_s).wait()
    gat = ga_s[...].astype(F32)

    lgrp = lane_iota((8, KVW)) // HD

    def qkv_dec(h, cos, sin, b0, n):
        hp = jnp.concatenate([h, jnp.zeros((LN - h.shape[0], HID), BF16)], axis=0)
        qt = rope_t(nt(wqt_s[...], hp), cos, sin).astype(BF16).astype(F32)
        kt = rope_t(nt(wk_s[...], hp), cos, sin).astype(BF16).astype(F32)
        vt = nt(wv_s[...], hp).astype(BF16).astype(F32)
        qt = qt * (HD ** -0.5)
        row = lax.broadcasted_iota(jnp.int32, (24, LN), 0)
        sf = jnp.zeros((24, LN), F32)
        for g in range(NKV):
            for r in range(GRP):
                j = g * GRP + r
                s = jnp.sum(qt[j * HD:(j + 1) * HD] * kt[g * HD:(g + 1) * HD], axis=0, keepdims=True)
                sf = jnp.where(row == 8 * g + r, s, sf)
        for r in range(GRP):
            qr = [qt[(g * GRP + r) * HD:(g * GRP + r + 1) * HD] for g in range(NKV)]
            qa_s[pl.ds(b0 * 8 + r, n, stride=8), :] = jnp.concatenate(qr[:2], axis=0).T[:n]
            qb_s[pl.ds(b0 * 8 + r, n, stride=8), :] = jnp.concatenate([qr[2], jnp.zeros((HD, LN), F32)], axis=0).T[:n]
        vn_s[b0:b0 + n, :LN] = vt[:LN].T[:n]
        vn_s[b0:b0 + n, LN:] = jnp.concatenate([vt[LN:], jnp.zeros((HD, LN), F32)], axis=0).T[:n, :HD]
        return kt, vt, sf

    def attn_dec(b, kt, vt, pos, selfcol):
        qb = jnp.concatenate([qa_s[pl.ds(b * 8, 8), :], qb_s[pl.ds(b * 8, 8), :HD]], axis=1)
        lhs = jnp.concatenate([jnp.where(lgrp == g, qb, 0.0) for g in range(NKV)], axis=0).astype(BF16)
        s = nn(lhs, kt)
        s = jnp.where(lane_iota((24, CL)) < pos, s, NEG)
        mx = jnp.maximum(jnp.max(s, axis=-1, keepdims=True), selfcol)
        p = jnp.exp(s - mx)
        ps = jnp.exp(selfcol - mx)
        rl = 1.0 / (jnp.sum(p, axis=-1, keepdims=True) + ps)
        o = nt((p * rl).astype(BF16), vt)
        o = o + (ps * rl).astype(BF16).astype(F32) * vn_s[pl.ds(b, 1), :]
        acc = jnp.where(lgrp == 0, o[0:8], 0.0)
        for g in range(1, NKV):
            acc = jnp.where(lgrp == g, o[8 * g:8 * g + 8], acc)
        oa_s[pl.ds(b * 8, 8), :] = acc[:, :LN]
        ob_s[pl.ds(b * 8, 8), :HD] = acc[:, LN:]

    def self_col(b):
        return jnp.sum(jnp.where(lane_iota((24, LN)) == b, self_s[...], 0.0), axis=-1, keepdims=True)

    def dec_out(b0, n):
        return [jnp.concatenate([oa_s[pl.ds(b0 * 8 + r, n, stride=8), :], ob_s[pl.ds(b0 * 8 + r, n, stride=8), :][:, :HD]], axis=1).astype(BF16)
                for r in range(GRP)]

    def wo_rows(r):
        return jnp.concatenate([wo_s[(g * GRP + r) * HD:(g * GRP + r + 1) * HD, :] for g in range(NKV)], axis=0)

    def mlp(x, rows):
        h2 = rms(x, gm_s[...].astype(F32))
        step = 512
        for c in range(FFN // step):
            gt = nn(h2, wg_s[:, c * step:(c + 1) * step])
            up = nn(h2, wu_s[:, c * step:(c + 1) * step])
            act_s[:rows, c * step:(c + 1) * step] = (gt * (1.0 / (1.0 + jnp.exp(-gt))) * up).astype(BF16)
        return (x + nt(act_s[:rows, :], wd_s[...])).astype(BF16)

    def round32(x):
        return x.astype(BF16).astype(F32)

    def to(k):
        return {'stage': k}

    def hop(src, dst, s_sem, r_sem):
        return pltpu.make_async_remote_copy(src, dst, s_sem, r_sem, device_id=to(jnp.minimum(st + 1, LAST)), device_id_type=MESH)

    @pl.when(st == 0)
    def _():
        ld(xd_s).wait()

    @pl.when(st > 0)
    def _():
        hop(sd_s, xd_s, sdd, rcd).wait_recv()

    hd = rms(xd_s[...].astype(F32), gat)
    ktd, vtd, sfd = qkv_dec(hd, cosd_s[...], sind_s[...], 0, ND)
    self_s[...] = sfd
    kdn_s[...] = ktd
    vdn_s[...] = vtd
    okd = pltpu.make_async_copy(kdn_s, kdn, out_sem.at[0])
    ovd = pltpu.make_async_copy(vdn_s, vdn, out_sem.at[1])
    okd.start()
    ovd.start()

    def dec_loop(m, carry):
        pltpu.make_async_copy(kd.at[m], kd_s.at[m], kd_sem.at[m]).wait()
        pltpu.make_async_copy(vd.at[m], vd_s.at[m], vd_sem.at[m]).wait()
        for i in range(DR):
            b = m * DR + i
            attn_dec(b, kd_s[m, i].reshape(KVW, CL), vd_s[m, i].reshape(KVW, CL), dl_s[m, i], self_col(b))
        return carry

    lax.fori_loop(0, NM, dec_loop, 0)

    for r in (wo_s, gm_s, wg_s, wu_s, wd_s):
        ld(r).wait()
    pl.semaphore_wait(bar, 3)

    @pl.when(st < LAST)
    def _():
        a = dec_out(0, ND)
        y = nn(a[0], wo_rows(0)) + nn(a[1], wo_rows(1)) + nn(a[2], wo_rows(2))
        x1 = round32(xd_s[...].astype(F32) + y)
        sd_s[...] = mlp(x1, ND)
        hop(sd_s, xd_s, sdd, rcd).start()

    @pl.when(st == 0)
    def _():
        ld(xp_s).wait()

    @pl.when(st > 0)
    def _():
        hop(sp_s, xp_s, sdp, rcp).wait_recv()

    ld(kp_s).wait()
    ld(vp_s).wait()
    hp = rms(xp_s[...].astype(F32), gat)
    ktp = rope_t(nt(wk_s[...], hp), cosp_s[...], sinp_s[...]).astype(BF16)
    vtp = nt(wv_s[...], hp).astype(BF16)
    place = jnp.where(lax.broadcasted_iota(jnp.int32, (NP, CL), 0) + p0 == lane_iota((NP, CL)), 1.0, 0.0).astype(BF16)
    lp = lane_iota((KVW, CL)) - p0
    fresh = (lp >= 0) & (lp < NP)
    kpu = jnp.where(fresh, nn(ktp, place), kp_s[...].reshape(KVW, CL).astype(F32))
    vpu = jnp.where(fresh, nn(vtp, place), vp_s[...].reshape(KVW, CL).astype(F32))
    kp_s[...] = kpu.astype(BF16).reshape(NKV, HD, CL)
    vp_s[...] = vpu.astype(BF16).reshape(NKV, HD, CL)
    okp = pltpu.make_async_copy(kp_s, kpn, out_sem.at[2])
    ovp = pltpu.make_async_copy(vp_s, vpn, out_sem.at[3])
    okp.start()
    ovp.start()

    @pl.when(st < LAST)
    def _():
        kfull = kpu.T.astype(BF16)
        vfull = vp_s[...].reshape(KVW, CL)
        qt = (rope_t(nt(wqt_s[...], hp), cosp_s[...], sinp_s[...]).astype(BF16).astype(F32) * (HD ** -0.5)).astype(BF16)
        bias = jnp.where(lax.broadcasted_iota(jnp.int32, (CL, NP), 0) <= lane_iota((CL, NP)) + p0, 0.0, NEG)
        for j in range(NQ):
            g = j // GRP
            parts = []
            if g:
                parts.append(jnp.zeros((g * HD, NP), BF16))
            parts.append(qt[j * HD:(j + 1) * HD])
            if g < NKV - 1:
                parts.append(jnp.zeros(((NKV - 1 - g) * HD, NP), BF16))
            s = nn(kfull, jnp.concatenate(parts, axis=0)) + bias
            p = jnp.exp(s - jnp.max(s, axis=0, keepdims=True))
            pr = (p * (1.0 / jnp.sum(p, axis=0, keepdims=True))).astype(BF16)
            ot_s[j * HD:(j + 1) * HD, :] = nn(vfull[g * HD:(g + 1) * HD], pr)
        x1 = round32(xp_s[...].astype(F32) + nn(ot_s[...].T.astype(BF16), wo_s[...]))
        sp_s[...] = mlp(x1, NP)
        hop(sp_s, xp_s, sdp, rcp).start()

    def bcast(k):
        return pltpu.make_async_remote_copy(fh_s, fr_s, sdf.at[k], rcf, device_id=to(k), device_id_type=MESH)

    ld(gf_s).wait()
    ld(wh_s).wait()

    def head(ref):
        lg_s[...] = nn(ref[...], wh_s[...])

    @pl.when(st == LAST)
    def _():
        x4_s[...] = jnp.zeros_like(x4_s)
        for m in range(NM):
            r0 = m * SEG + SEG - 8
            x4_s[m:m + 1, :] = xp_s[r0:r0 + 8, :].astype(F32)[7:8]
        x4 = x4_s[...]
        h4 = rms(x4, gat)
        h4 = jnp.concatenate([h4, jnp.zeros_like(h4)], axis=0)
        _, _, sf4 = qkv_dec(h4, cosl_s[...], sinl_s[...], ND, 8)
        for m in range(NM):
            col = jnp.sum(jnp.where(lane_iota((24, LN)) == m, sf4, 0.0), axis=-1, keepdims=True)
            attn_dec(ND + m, kp_s[...].reshape(KVW, CL), vp_s[...].reshape(KVW, CL), p0 + m * SEG + SEG - 1, col)
        for m in range(NM, 8):
            oa_s[pl.ds((ND + m) * 8, 8), :] = jnp.zeros((8, LN), F32)
        a = dec_out(0, ND + 8)
        y = nn(a[0], wo_rows(0)) + nn(a[1], wo_rows(1)) + nn(a[2], wo_rows(2))
        x1 = round32(jnp.concatenate([xd_s[...].astype(F32), x4], axis=0) + y)
        x2 = mlp(x1, ND + 8)
        fh = rms(x2.astype(F32), gf_s[...].astype(F32))
        ri = lax.broadcasted_iota(jnp.int32, (ND + 8, ND + 8), 0)
        src = jnp.where(ri < ND, (ri % NM) * DR + ri // NM, ri)
        fh_s[...] = nn(jnp.where(lane_iota((ND + 8, ND + 8)) == src, 1.0, 0.0).astype(BF16), fh).astype(BF16)
        for k in range(LAST):
            bcast(k).start()
        head(fh_s)

    @pl.when(st < LAST)
    def _():
        bcast(0).wait_recv()
        head(fr_s)

    for i in range(DR + 1):
        logits[i] = lg_s[i * NM:(i + 1) * NM, :]

    okd.wait()
    ovd.wait()
    okp.wait()
    ovp.wait()

    @pl.when(st < LAST)
    def _():
        hop(sd_s, xd_s, sdd, rcd).wait_send()
        hop(sp_s, xp_s, sdp, rcp).wait_send()

    @pl.when(st == LAST)
    def _():
        for k in range(LAST):
            bcast(k).wait_send()


def cache_kernel(dlen, kd, vd, kdn, vdn, kpn, vpn, ko, vo, kpo, vpo, ks, vs, kn_s, vn_s, kp_s, vp_s, ksem, vsem, nsem):
    cin = []
    for m in range(NM):
        cin.append((pltpu.make_async_copy(kd.at[m], ks.at[m], ksem.at[m]), pltpu.make_async_copy(vd.at[m], vs.at[m], vsem.at[m])))
    small = [pltpu.make_async_copy(a, b, nsem.at[i]) for i, (a, b) in enumerate(
        [(kdn, kn_s), (vdn, vn_s), (kpn, kp_s), (vpn, vp_s)])]
    for c in small:
        c.start()
    for a, b in cin:
        a.start()
        b.start()
    for c in small:
        c.wait()
    outs = [pltpu.make_async_copy(kp_s, kpo, nsem.at[2]), pltpu.make_async_copy(vp_s, vpo, nsem.at[3])]
    for c in outs:
        c.start()
    lane = lane_iota((HD, LN))
    for m in range(NM):
        for cp, scr, new, out, sem in ((cin[m][0], ks, kn_s, ko, ksem), (cin[m][1], vs, vn_s, vo, vsem)):
            cp.wait()
            for i in range(DR):
                b = m * DR + i
                pos = dlen[m, i]
                sl = pl.ds(pl.multiple_of((pos // LN) * LN, LN), LN)
                for g in range(NKV):
                    col = new[g * HD:(g + 1) * HD, b:b + 1]
                    old = scr[m, i, g, :, sl].astype(F32)
                    scr[m, i, g, :, sl] = jnp.where(lane == pos % LN, col, old).astype(BF16)
            c = pltpu.make_async_copy(scr.at[m], out.at[m], sem.at[m])
            c.start()
            outs.append(c)
    for c in outs:
        c.wait()


ANY = pl.BlockSpec(memory_space=pltpu.HBM)


def solution(mesh):
    part = P('replica')
    layer = P('stage')
    cache = P('stage', 'replica')
    in_specs = (part,) * 4 + (layer,) * 9 + (P(), P()) + (cache,) * 4
    out_specs = (part,) + (cache,) * 4
    inv_freq = np.float32(ROPE_BASE) ** (-np.arange(HALF, dtype=np.float32) * np.float32(2.0 / HD))
    ifr_c = np.broadcast_to(inv_freq[:, None], (HALF, NP)).astype(np.float32)

    def device_fn(x_dec, x_pre, dec_len, pre_len, g_attn, w_q, w_k, w_v, w_o, g_mlp, w_gate, w_up, w_down, g_final, w_head, k_dec, v_dec, k_pre, v_pre):
        kd = jnp.transpose(k_dec[0], (0, 1, 3, 4, 2))
        vd = jnp.transpose(v_dec[0], (0, 1, 3, 4, 2))
        kp = jnp.transpose(k_pre[0], (1, 2, 0))
        vp = jnp.transpose(v_pre[0], (1, 2, 0))
        args = (x_dec.reshape(ND, HID), x_pre.reshape(NP, HID), dec_len, pre_len, g_attn, w_q[0], w_k[0].T, w_v[0].T, w_o[0], g_mlp,
                w_gate[0], w_up[0], w_down[0].T, g_final.reshape(1, HID), w_head, kd, vd, kp, vp, jnp.asarray(ifr_c))
        vm = lambda shape, dt: pltpu.VMEM(shape, dt)
        scratch = [
            vm((ND, HID), BF16), vm((NP, HID), BF16), pltpu.SMEM((NM, DR), jnp.int32), pltpu.SMEM((1,), jnp.int32), vm((1, HID), BF16),
            vm((HID, HID), BF16), vm((KVW, HID), BF16), vm((KVW, HID), BF16), vm((HID, HID), BF16), vm((1, HID), BF16),
            vm((HID, FFN), BF16), vm((HID, FFN), BF16), vm((HID, FFN), BF16), vm((1, HID), BF16), vm((HID, VOC), BF16),
            vm(kd.shape, BF16), vm(vd.shape, BF16), vm(kp.shape, BF16), vm(vp.shape, BF16), vm((HALF, NP), F32),
            vm((HID, HID), BF16), vm((HALF, LN), F32), vm((HALF, LN), F32), vm((HALF, NP), F32), vm((HALF, NP), F32),
            vm((HALF, LN), F32), vm((HALF, LN), F32),
            vm(((ND + 8) * 8, LN), F32), vm(((ND + 8) * 8, LN), F32), vm((24, LN), F32), vm((ND + 8, KVW), F32),
            vm(((ND + 8) * 8, LN), F32), vm(((ND + 8) * 8, LN), F32),
            vm((KVW, LN), F32), vm((KVW, LN), F32), vm((HID, NP), F32), vm((NP, FFN), BF16), vm((8, HID), F32),
            vm((ND, HID), BF16), vm((NP, HID), BF16), vm((ND + 8, HID), BF16), vm((ND + 8, HID), BF16), vm((ND + 8, VOC), F32),
            pltpu.SemaphoreType.DMA((18,)), pltpu.SemaphoreType.DMA((NM,)), pltpu.SemaphoreType.DMA((NM,)), pltpu.SemaphoreType.DMA((4,)),
            pltpu.SemaphoreType.DMA, pltpu.SemaphoreType.DMA, pltpu.SemaphoreType.DMA, pltpu.SemaphoreType.DMA,
            pltpu.SemaphoreType.DMA((3,)), pltpu.SemaphoreType.DMA,
        ]
        kdn, vdn, kpn, vpn, logits = pl.pallas_call(
            pipe_kernel,
            out_shape=(jax.ShapeDtypeStruct((KVW, LN), F32), jax.ShapeDtypeStruct((KVW, LN), F32),
                       jax.ShapeDtypeStruct(kp.shape, BF16), jax.ShapeDtypeStruct(vp.shape, BF16),
                       jax.ShapeDtypeStruct((DR + 1, NM, VOC), F32)),
            in_specs=[ANY] * len(args),
            out_specs=(ANY, ANY, ANY, ANY, pl.BlockSpec(memory_space=pltpu.VMEM)),
            scratch_shapes=scratch,
            name='pipe',
            compiler_params=pltpu.CompilerParams(collective_id=0, has_side_effects=True, vmem_limit_bytes=60 * 1024 * 1024),
        )(*args)
        ko, vo, kpo, vpo = pl.pallas_call(
            cache_kernel,
            out_shape=tuple(jax.ShapeDtypeStruct(a.shape, BF16) for a in (kd, vd, kp, vp)),
            in_specs=[pl.BlockSpec(memory_space=pltpu.SMEM)] + [ANY] * 6,
            out_specs=(ANY,) * 4,
            scratch_shapes=[vm(kd.shape, BF16), vm(vd.shape, BF16), vm((KVW, LN), F32), vm((KVW, LN), F32), vm(kp.shape, BF16), vm(vp.shape, BF16),
                            pltpu.SemaphoreType.DMA((NM,)), pltpu.SemaphoreType.DMA((NM,)), pltpu.SemaphoreType.DMA((4,))],
            name='caches',
            compiler_params=pltpu.CompilerParams(vmem_limit_bytes=40 * 1024 * 1024),
        )(dec_len, kd, vd, kdn, vdn, kpn, vpn)
        back = lambda a: jnp.transpose(a, (0, 1, 4, 2, 3))[None]
        backp = lambda a: jnp.transpose(a, (2, 0, 1))[None]
        return jnp.transpose(logits, (1, 0, 2)), back(ko), back(vo), backp(kpo), backp(vpo)

    return jax.shard_map(device_fn, mesh=mesh, in_specs=in_specs, out_specs=out_specs, check_vma=False)
```

time: 339 us -> 74.3 us (0.22)
  the two profiles are of different devices: /device:TPU:7 before, /device:TPU:5 now
where the time goes in v1:
time: 74.3 us; the launch traced here: 74 us
  Pallas kernels  61.5 us (83%)
  local copies, waits for them, and re-layouts  11.1 us (15%)
  between operations  1.32 us (2%)
    pallas_call x1, Pallas kernels, device_fn(): pl.pallas_call(pipe_kernel, out_shape=(jax.ShapeDtypeStruct((KVW, LN), F3...  54.5 us
    unnamed x17, local copies, waits for them, and re-layouts  9.87 us
    pallas_call x1, Pallas kernels, device_fn(): pl.pallas_call(cache_kernel, out_shape=tuple((jax.ShapeDtypeStruct(a.shap...  7.06 us

profile of v1, /device:TPU:5, one launch (start us, length us, event | category | flops | bytes accessed | tf_op | source)
XLA Modules:
  0.0 74.0 jit_solution(9908042990074898953)
XLA Ops:
  1.3 1.3 %reshape.21.gf = bf16[1,576]{1,0:T(2,128)(2,1)} reshape(bf16[576]{0:T(1024)(128)(2,1)} %param.33) | data formatting | bytes 2304 | tf_op jit(solution)/shard_map/reshape | solution.py:405
  2.5 0.0 copy-start.6
  2.5 54.5 %pipe.1 = (f32[192,128]{1,0:T(8,128)}, f32[192,128]{1,0:T(8,128)}, bf16[3,64,512]{2,1,0:T(8,128)(2,1)}, bf16[3,64,512]{2,1,0:T(8,128)(2,1)}, f32[9,4,1024]{2,1,0:T(4,128)}) custom-call(bf16[32,576]{1,0:T(8,128)(2,1)} %bitcast.55, bf16[256,576]{1,0:T(8,128)(2,1)} %bitcast.49, s32[4,8]{1,0:T(4,128)} %dlen.3, s32[1]{0:T(128)S(6)} %copy.26.plen, ...), custom_call_target="tpu_custom_call" | custom-call | tf_op jit(solution)/shard_map/pipe/pallas_call | solution.py:422
  57.0 0.0 copy-done.6
  57.1 0.0 copy-start
  57.1 2.8 %copy-done = bf16[1,4,8,512,3,64]{3,5,4,2,1,0:T(8,128)(2,1)S(1)} copy-done((bf16[1,4,8,512,3,64]{3,5,4,2,1,0:T(8,128)(2,1)S(1)}, bf16[1,4,8,512,3,64]{3,5,4,2,1,0:T(8,128)(2,1)}, u32[]{:S(2)}) %copy-start) | copy-done | bytes 6291480
  59.8 0.0 copy-start.1
  59.8 2.8 %copy-done.1 = bf16[1,4,8,512,3,64]{3,5,4,2,1,0:T(8,128)(2,1)S(1)} copy-done((bf16[1,4,8,512,3,64]{3,5,4,2,1,0:T(8,128)(2,1)S(1)}, bf16[1,4,8,512,3,64]{3,5,4,2,1,0:T(8,128)(2,1)}, u32[]{:S(2)}) %copy-start.1) | copy-done | bytes 6291480
  62.6 0.0 copy-start.2
  62.6 0.9 %copy-done.2 = bf16[3,64,512]{2,1,0:T(8,128)(2,1)S(1)} copy-done((bf16[3,64,512]{2,1,0:T(8,128)(2,1)S(1)}, bf16[3,64,512]{2,1,0:T(8,128)(2,1)}, u32[]{:S(2)}) %copy-start.2) | copy-done | bytes 196632
  63.6 0.0 copy-start.3
  63.6 0.9 %copy-done.3 = bf16[3,64,512]{2,1,0:T(8,128)(2,1)S(1)} copy-done((bf16[3,64,512]{2,1,0:T(8,128)(2,1)S(1)}, bf16[3,64,512]{2,1,0:T(8,128)(2,1)}, u32[]{:S(2)}) %copy-start.3) | copy-done | bytes 196632
  64.5 0.0 copy-start.4
  64.5 0.9 %copy-done.4 = f32[192,128]{1,0:T(8,128)S(1)} copy-done((f32[192,128]{1,0:T(8,128)S(1)}, f32[192,128]{1,0:T(8,128)}, u32[]{:S(2)}) %copy-start.4) | copy-done | bytes 98328
  65.4 0.0 copy-start.5
  65.4 0.9 %copy-done.5 = f32[192,128]{1,0:T(8,128)S(1)} copy-done((f32[192,128]{1,0:T(8,128)S(1)}, f32[192,128]{1,0:T(8,128)}, u32[]{:S(2)}) %copy-start.5) | copy-done | bytes 98328
  66.3 0.0 copy-start.7
  66.3 7.1 %caches.1 = (bf16[4,8,3,64,512]{4,3,2,1,0:T(8,128)(2,1)}, bf16[4,8,3,64,512]{4,3,2,1,0:T(8,128)(2,1)}, bf16[3,64,512]{2,1,0:T(8,128)(2,1)}, bf16[3,64,512]{2,1,0:T(8,128)(2,1)}) custom-call(s32[4,8]{1,0:T(4,128)S(1)} %copy-done.6, bf16[4,8,3,64,512]{4,3,2,1,0:T(8,128)(2,1)S(1)} %bitcast.41, bf16[4,8,3,64,512]{4,3,2,1,0:T(8,128)(2,1)S(1)} %bitcast.43, ...), custom_call_target="tpu_custom_call" | custom-call | tf_op jit(solution)/shard_map/caches/pallas_call | solution.py:433
  73.3 0.0 copy-done.7
  73.3 0.7 copy.27
Async XLA Ops:
  2.5 54.5 %copy-start.6 = (s32[4,8]{1,0:T(4,128)S(1)}, s32[4,8]{1,0:T(4,128)}, u32[]{:S(2)}) copy-start(s32[4,8]{1,0:T(4,128)} %dlen.3) | copy-start | bytes 388
  57.1 2.8 %copy-start = (bf16[1,4,8,512,3,64]{3,5,4,2,1,0:T(8,128)(2,1)S(1)}, bf16[1,4,8,512,3,64]{3,5,4,2,1,0:T(8,128)(2,1)}, u32[]{:S(2)}) copy-start(bf16[1,4,8,512,3,64]{3,5,4,2,1,0:T(8,128)(2,1)} %param.35) | copy-start | bytes 18874372
  59.8 2.8 %copy-start.1 = (bf16[1,4,8,512,3,64]{3,5,4,2,1,0:T(8,128)(2,1)S(1)}, bf16[1,4,8,512,3,64]{3,5,4,2,1,0:T(8,128)(2,1)}, u32[]{:S(2)}) copy-start(bf16[1,4,8,512,3,64]{3,5,4,2,1,0:T(8,128)(2,1)} %param.36) | copy-start | bytes 18874372
  62.6 0.9 %copy-start.2 = (bf16[3,64,512]{2,1,0:T(8,128)(2,1)S(1)}, bf16[3,64,512]{2,1,0:T(8,128)(2,1)}, u32[]{:S(2)}) copy-start(bf16[3,64,512]{2,1,0:T(8,128)(2,1)} %get-tuple-element.17.kpn) | copy-start | bytes 589828
  63.6 0.9 %copy-start.3 = (bf16[3,64,512]{2,1,0:T(8,128)(2,1)S(1)}, bf16[3,64,512]{2,1,0:T(8,128)(2,1)}, u32[]{:S(2)}) copy-start(bf16[3,64,512]{2,1,0:T(8,128)(2,1)} %get-tuple-element.18.vpn) | copy-start | bytes 589828
  64.5 0.9 %copy-start.4 = (f32[192,128]{1,0:T(8,128)S(1)}, f32[192,128]{1,0:T(8,128)}, u32[]{:S(2)}) copy-start(f32[192,128]{1,0:T(8,128)} %get-tuple-element.15.kdn) | copy-start | bytes 294916
  65.4 0.9 %copy-start.5 = (f32[192,128]{1,0:T(8,128)S(1)}, f32[192,128]{1,0:T(8,128)}, u32[]{:S(2)}) copy-start(f32[192,128]{1,0:T(8,128)} %get-tuple-element.16.vdn) | copy-start | bytes 294916
  66.3 7.1 %copy-start.7 = (f32[9,4,1024]{2,1,0:T(4,128)S(1)}, f32[9,4,1024]{2,1,0:T(4,128)}, u32[]{:S(2)}) copy-start(f32[9,4,1024]{2,1,0:T(4,128)} %get-tuple-element.14) | copy-start | bytes 442372

commit v2 on v1

--- a/solution.py
+++ b/solution.py
@@ -60,17 +60,16 @@
     return lax.broadcasted_iota(jnp.int32, shape, len(shape) - 1)
 
 
-def pipe_kernel(xd, xp, dlen, plen, ga, wq, wk, wv, wo, gm, wg, wu, wd, gf, wh, kd, vd, kp, vp, ifr,
-                kdn, vdn, kpn, vpn, logits,
-                xd_s, xp_s, dl_s, pl_s, ga_s, wq_s, wk_s, wv_s, wo_s, gm_s, wg_s, wu_s, wd_s, gf_s, wh_s,
+def pipe_kernel(xd, xp, dlen, plen, ga, wq, wk, wv, wo, gm, wg, wu, wd, gf, kd, vd, kp, vp, ifr, tok,
+                kdn, vdn, kpn, vpn, fh_o,
+                xd_s, xp_s, dl_s, pl_s, ga_s, wq_s, wk_s, wv_s, wo_s, gm_s, wg_s, wu_s, wd_s, gf_s,
                 kd_s, vd_s, kp_s, vp_s, ifr_s,
                 wqt_s, cosd_s, sind_s, cosp_s, sinp_s, cosl_s, sinl_s, qa_s, qb_s, self_s, vn_s, oa_s, ob_s,
-                kdn_s, vdn_s, ot_s, act_s, x4_s, sd_s, sp_s, fh_s, fr_s, lg_s,
-                in_sem, kd_sem, vd_sem, out_sem, sdd, sdp, rcd, rcp, sdf, rcf):
+                kdn_s, vdn_s, ot_s, act_s, x4_s, sd_s, sp_s, fh_s,
+                in_sem, kd_sem, vd_sem, out_sem, sdd, sdp, rcd, rcp):
     st = lax.axis_index('stage')
-    rep = lax.axis_index('replica')
     order = [(dlen, dl_s), (plen, pl_s), (xd, xd_s), (ga, ga_s), (ifr, ifr_s), (wq, wq_s), (wk, wk_s), (wv, wv_s),
-             (kp, kp_s), (vp, vp_s), (wo, wo_s), (gm, gm_s), (wg, wg_s), (wu, wu_s), (wd, wd_s), (xp, xp_s), (gf, gf_s), (wh, wh_s)]
+             (kp, kp_s), (vp, vp_s), (wo, wo_s), (gm, gm_s), (wg, wg_s), (wu, wu_s), (wd, wd_s), (xp, xp_s), (gf, gf_s)]
     cps = [pltpu.make_async_copy(a, b, in_sem.at[i]) for i, (a, b) in enumerate(order)]
     by = {id(b): c for (a, b), c in zip(order, cps)}
     kcp = [pltpu.make_async_copy(kd.at[m], kd_s.at[m], kd_sem.at[m]) for m in range(NM)]
@@ -97,13 +96,16 @@
         ld(xp_s).start()
 
     ld(gf_s).start()
-    ld(wh_s).start()
 
     bar = pltpu.get_barrier_semaphore()
-    for k in range(4):
-        @pl.when(st != k)
-        def _(k=k):
-            pl.semaphore_signal(bar, inc=1, device_id={'stage': k}, device_id_type=MESH)
+
+    @pl.when(st > 0)
+    def _():
+        pl.semaphore_signal(bar, inc=1, device_id={'stage': jnp.maximum(st - 1, 0)}, device_id_type=MESH)
+
+    @pl.when(st < LAST)
+    def _():
+        pl.semaphore_signal(bar, inc=1, device_id={'stage': jnp.minimum(st + 1, LAST)}, device_id_type=MESH)
 
     ld(dl_s).wait()
     ld(pl_s).wait()
@@ -232,7 +234,14 @@
 
     for r in (wo_s, gm_s, wg_s, wu_s, wd_s):
         ld(r).wait()
-    pl.semaphore_wait(bar, 3)
+
+    @pl.when((st == 0) | (st == LAST))
+    def _():
+        pl.semaphore_wait(bar, 1)
+
+    @pl.when((st > 0) & (st < LAST))
+    def _():
+        pl.semaphore_wait(bar, 2)
 
     @pl.when(st < LAST)
     def _():
@@ -289,14 +298,7 @@
         sp_s[...] = mlp(x1, NP)
         hop(sp_s, xp_s, sdp, rcp).start()
 
-    def bcast(k):
-        return pltpu.make_async_remote_copy(fh_s, fr_s, sdf.at[k], rcf, device_id=to(k), device_id_type=MESH)
-
     ld(gf_s).wait()
-    ld(wh_s).wait()
-
-    def head(ref):
-        lg_s[...] = nn(ref[...], wh_s[...])
 
     @pl.when(st == LAST)
     def _():
@@ -321,17 +323,9 @@
         ri = lax.broadcasted_iota(jnp.int32, (ND + 8, ND + 8), 0)
         src = jnp.where(ri < ND, (ri % NM) * DR + ri // NM, ri)
         fh_s[...] = nn(jnp.where(lane_iota((ND + 8, ND + 8)) == src, 1.0, 0.0).astype(BF16), fh).astype(BF16)
-        for k in range(LAST):
-            bcast(k).start()
-        head(fh_s)
-
-    @pl.when(st < LAST)
-    def _():
-        bcast(0).wait_recv()
-        head(fr_s)
-
-    for i in range(DR + 1):
-        logits[i] = lg_s[i * NM:(i + 1) * NM, :]
+        ofh = pltpu.make_async_copy(fh_s, fh_o, out_sem.at[4])
+        ofh.start()
+        ofh.wait()
 
     okd.wait()
     ovd.wait()
@@ -343,45 +337,166 @@
         hop(sd_s, xd_s, sdd, rcd).wait_send()
         hop(sp_s, xp_s, sdp, rcp).wait_send()
 
+
+def head_kernel(fh, wh, tok, logits, fh_s, fr_s, wh_s, lsem, ssem, rsem):
+    st = lax.axis_index('stage')
+    lfh = pltpu.make_async_copy(fh, fh_s, lsem.at[0])
+    lwh = pltpu.make_async_copy(wh, wh_s, lsem.at[1])
+
     @pl.when(st == LAST)
     def _():
+        lfh.start()
+
+    lwh.start()
+    bar = pltpu.get_barrier_semaphore()
+
+    def send(k):
+        return pltpu.make_async_remote_copy(fh_s, fr_s, ssem.at[k], rsem, device_id={'stage': k}, device_id_type=MESH)
+
+    def head(ref):
+        lwh.wait()
+        lg = nn(ref[...], wh_s[...])
+        for i in range(DR + 1):
+            logits[i] = lg[i * NM:(i + 1) * NM]
+
+    @pl.when(st < LAST)
+    def _():
+        pl.semaphore_signal(bar, inc=1, device_id={'stage': LAST}, device_id_type=MESH)
+
+    @pl.when(st == LAST)
+    def _():
         for k in range(LAST):
-            bcast(k).wait_send()
-
-
-def cache_kernel(dlen, kd, vd, kdn, vdn, kpn, vpn, ko, vo, kpo, vpo, ks, vs, kn_s, vn_s, kp_s, vp_s, ksem, vsem, nsem):
-    cin = []
-    for m in range(NM):
-        cin.append((pltpu.make_async_copy(kd.at[m], ks.at[m], ksem.at[m]), pltpu.make_async_copy(vd.at[m], vs.at[m], vsem.at[m])))
-    small = [pltpu.make_async_copy(a, b, nsem.at[i]) for i, (a, b) in enumerate(
-        [(kdn, kn_s), (vdn, vn_s), (kpn, kp_s), (vpn, vp_s)])]
-    for c in small:
-        c.start()
-    for a, b in cin:
+            pl.semaphore_signal(bar, inc=1, device_id={'stage': k}, device_id_type=MESH)
+        pl.semaphore_wait(bar, LAST)
+        lfh.wait()
+        for k in range(LAST):
+            send(k).start()
+        head(fh_s)
+        for k in range(LAST):
+            send(k).wait_send()
+
+    @pl.when(st < LAST)
+    def _():
+        pl.semaphore_wait(bar, 1)
+        send(0).wait_recv()
+        head(fr_s)
+
+
+def tile_start(pos):
+    return pl.ds(pl.multiple_of((pos // LN) * LN, LN), LN)
+
+
+def copy_all(kd, vd, ko, vo, ks, vs, ksem, vsem, edit):
+    ins = [(pltpu.make_async_copy(kd.at[m], ks.at[m], ksem.at[m]), pltpu.make_async_copy(vd.at[m], vs.at[m], vsem.at[m])) for m in range(NM)]
+    for a, b in ins:
         a.start()
         b.start()
-    for c in small:
+    outs = []
+    for m in range(NM):
+        for c, scr, out, sem, w in ((ins[m][0], ks, ko, ksem, 0), (ins[m][1], vs, vo, vsem, 1)):
+            c.wait()
+            if edit is not None:
+                edit(m, scr, w)
+            o = pltpu.make_async_copy(scr.at[m], out.at[m], sem.at[m])
+            o.start()
+            outs.append(o)
+    for o in outs:
+        o.wait()
+
+
+def pre_kernel(kd, vd, ko, vo, tok, ks, vs, ksem, vsem):
+    st = lax.axis_index('stage')
+    tok[...] = jnp.zeros_like(tok)
+
+    @pl.when(st >= 2)
+    def _():
+        copy_all(kd, vd, ko, vo, ks, vs, ksem, vsem, None)
+
+
+def load_new(srcs, dsts, sem):
+    cs = [pltpu.make_async_copy(a, b, sem.at[i]) for i, (a, b) in enumerate(zip(srcs, dsts))]
+    for c in cs:
+        c.start()
+    return cs
+
+
+def update_tiles(dlen, bk, bv, ko, vo, kpo, vpo, kt, vt, new, cs, ksem, vsem, nsem):
+    lane = lane_iota((HD, LN))
+
+    def cp(hbm, scr, sem, m, i, out):
+        h = hbm.at[m, i, :, :, tile_start(dlen[m, i])]
+        v = scr.at[m, i]
+        return pltpu.make_async_copy(v, h, sem.at[m]) if out else pltpu.make_async_copy(h, v, sem.at[m])
+
+    for m in range(NM):
+        for i in range(DR):
+            cp(bk, kt, ksem, m, i, False).start()
+            cp(bv, vt, vsem, m, i, False).start()
+    for c in cs:
         c.wait()
-    outs = [pltpu.make_async_copy(kp_s, kpo, nsem.at[2]), pltpu.make_async_copy(vp_s, vpo, nsem.at[3])]
-    for c in outs:
-        c.start()
-    lane = lane_iota((HD, LN))
+    po = [pltpu.make_async_copy(new[2], kpo, nsem.at[2]), pltpu.make_async_copy(new[3], vpo, nsem.at[3])]
+    for o in po:
+        o.start()
     for m in range(NM):
-        for cp, scr, new, out, sem in ((cin[m][0], ks, kn_s, ko, ksem), (cin[m][1], vs, vn_s, vo, vsem)):
-            cp.wait()
+        for hbm, scr, sem, nw in ((ko, kt, ksem, new[0]), (vo, vt, vsem, new[1])):
             for i in range(DR):
-                b = m * DR + i
+                cp(hbm, scr, sem, m, i, False).wait()
+            for i in range(DR):
                 pos = dlen[m, i]
-                sl = pl.ds(pl.multiple_of((pos // LN) * LN, LN), LN)
                 for g in range(NKV):
-                    col = new[g * HD:(g + 1) * HD, b:b + 1]
-                    old = scr[m, i, g, :, sl].astype(F32)
-                    scr[m, i, g, :, sl] = jnp.where(lane == pos % LN, col, old).astype(BF16)
-            c = pltpu.make_async_copy(scr.at[m], out.at[m], sem.at[m])
-            c.start()
-            outs.append(c)
-    for c in outs:
-        c.wait()
+                    col = nw[g * HD:(g + 1) * HD, m * DR + i:m * DR + i + 1]
+                    scr[m, i, g] = jnp.where(lane == pos % LN, col, scr[m, i, g].astype(F32)).astype(BF16)
+            for i in range(DR):
+                cp(hbm, scr, sem, m, i, True).start()
+    for m in range(NM):
+        for i in range(DR):
+            cp(ko, kt, ksem, m, i, True).wait()
+            cp(vo, vt, vsem, m, i, True).wait()
+    for o in po:
+        o.wait()
+
+
+def mid_kernel(dlen, kd, vd, bk, bv, kdn, vdn, kpn, vpn, ko, vo, kpo, vpo, tok, ks, vs, kt, vt, kn_s, vn_s, kp_s, vp_s, ksem, vsem, nsem):
+    st = lax.axis_index('stage')
+    tok[...] = jnp.zeros_like(tok)
+    new = (kn_s, vn_s, kp_s, vp_s)
+
+    @pl.when(st < 2)
+    def _():
+        cs = load_new((kdn, vdn, kpn, vpn), new, nsem)
+        for c in cs:
+            c.wait()
+        po = [pltpu.make_async_copy(kp_s, kpo, nsem.at[2]), pltpu.make_async_copy(vp_s, vpo, nsem.at[3])]
+        for o in po:
+            o.start()
+        lane = lane_iota((HD, LN))
+
+        def edit(m, scr, w):
+            for i in range(DR):
+                pos = dlen[m, i]
+                sl = tile_start(pos)
+                for g in range(NKV):
+                    col = new[w][g * HD:(g + 1) * HD, m * DR + i:m * DR + i + 1]
+                    scr[m, i, g, :, sl] = jnp.where(lane == pos % LN, col, scr[m, i, g, :, sl].astype(F32)).astype(BF16)
+
+        copy_all(kd, vd, ko, vo, ks, vs, ksem, vsem, edit)
+        for o in po:
+            o.wait()
+
+    @pl.when(st == 2)
+    def _():
+        cs = load_new((kdn, vdn, kpn, vpn), new, nsem)
+        update_tiles(dlen, bk, bv, ko, vo, kpo, vpo, kt, vt, new, cs, ksem, vsem, nsem)
+
+
+def post_kernel(dlen, kdn, vdn, kpn, vpn, lg, bk, bv, bkp, bvp, ko, vo, kpo, vpo, kt, vt, kn_s, vn_s, kp_s, vp_s, ksem, vsem, nsem):
+    st = lax.axis_index('stage')
+
+    @pl.when(st == LAST)
+    def _():
+        new = (kn_s, vn_s, kp_s, vp_s)
+        cs = load_new((kdn, vdn, kpn, vpn), new, nsem)
+        update_tiles(dlen, bk, bv, ko, vo, kpo, vpo, kt, vt, new, cs, ksem, vsem, nsem)
 
 
 ANY = pl.BlockSpec(memory_space=pltpu.HBM)
@@ -402,44 +517,60 @@
         kp = jnp.transpose(k_pre[0], (1, 2, 0))
         vp = jnp.transpose(v_pre[0], (1, 2, 0))
         args = (x_dec.reshape(ND, HID), x_pre.reshape(NP, HID), dec_len, pre_len, g_attn, w_q[0], w_k[0].T, w_v[0].T, w_o[0], g_mlp,
-                w_gate[0], w_up[0], w_down[0].T, g_final.reshape(1, HID), w_head, kd, vd, kp, vp, jnp.asarray(ifr_c))
+                w_gate[0], w_up[0], w_down[0].T, g_final.reshape(1, HID), kd, vd, kp, vp, jnp.asarray(ifr_c))
         vm = lambda shape, dt: pltpu.VMEM(shape, dt)
         scratch = [
             vm((ND, HID), BF16), vm((NP, HID), BF16), pltpu.SMEM((NM, DR), jnp.int32), pltpu.SMEM((1,), jnp.int32), vm((1, HID), BF16),
             vm((HID, HID), BF16), vm((KVW, HID), BF16), vm((KVW, HID), BF16), vm((HID, HID), BF16), vm((1, HID), BF16),
-            vm((HID, FFN), BF16), vm((HID, FFN), BF16), vm((HID, FFN), BF16), vm((1, HID), BF16), vm((HID, VOC), BF16),
+            vm((HID, FFN), BF16), vm((HID, FFN), BF16), vm((HID, FFN), BF16), vm((1, HID), BF16),
             vm(kd.shape, BF16), vm(vd.shape, BF16), vm(kp.shape, BF16), vm(vp.shape, BF16), vm((HALF, NP), F32),
             vm((HID, HID), BF16), vm((HALF, LN), F32), vm((HALF, LN), F32), vm((HALF, NP), F32), vm((HALF, NP), F32),
             vm((HALF, LN), F32), vm((HALF, LN), F32),
             vm(((ND + 8) * 8, LN), F32), vm(((ND + 8) * 8, LN), F32), vm((24, LN), F32), vm((ND + 8, KVW), F32),
             vm(((ND + 8) * 8, LN), F32), vm(((ND + 8) * 8, LN), F32),
             vm((KVW, LN), F32), vm((KVW, LN), F32), vm((HID, NP), F32), vm((NP, FFN), BF16), vm((8, HID), F32),
-            vm((ND, HID), BF16), vm((NP, HID), BF16), vm((ND + 8, HID), BF16), vm((ND + 8, HID), BF16), vm((ND + 8, VOC), F32),
-            pltpu.SemaphoreType.DMA((18,)), pltpu.SemaphoreType.DMA((NM,)), pltpu.SemaphoreType.DMA((NM,)), pltpu.SemaphoreType.DMA((4,)),
+            vm((ND, HID), BF16), vm((NP, HID), BF16), vm((ND + 8, HID), BF16),
+            pltpu.SemaphoreType.DMA((17,)), pltpu.SemaphoreType.DMA((NM,)), pltpu.SemaphoreType.DMA((NM,)), pltpu.SemaphoreType.DMA((5,)),
             pltpu.SemaphoreType.DMA, pltpu.SemaphoreType.DMA, pltpu.SemaphoreType.DMA, pltpu.SemaphoreType.DMA,
-            pltpu.SemaphoreType.DMA((3,)), pltpu.SemaphoreType.DMA,
         ]
-        kdn, vdn, kpn, vpn, logits = pl.pallas_call(
+        sds = jax.ShapeDtypeStruct
+        big = pltpu.CompilerParams(vmem_limit_bytes=62 * 1024 * 1024)
+        cshape = sds(kd.shape, BF16)
+        pshape = sds(kp.shape, BF16)
+        nsems = [pltpu.SemaphoreType.DMA((NM,)), pltpu.SemaphoreType.DMA((NM,))]
+        tile = vm((NM, DR, NKV, HD, LN), BF16)
+        news = [vm((KVW, LN), F32), vm((KVW, LN), F32), vm(kp.shape, BF16), vm(vp.shape, BF16)]
+        smem = pl.BlockSpec(memory_space=pltpu.SMEM)
+        vmem = pl.BlockSpec(memory_space=pltpu.VMEM)
+        tshape = sds((8, LN), F32)
+        bk, bv, tok = pl.pallas_call(
+            pre_kernel, out_shape=(cshape, cshape, tshape), in_specs=[ANY, ANY], out_specs=(ANY, ANY, vmem),
+            scratch_shapes=[vm(kd.shape, BF16), vm(vd.shape, BF16)] + nsems, name='pre', compiler_params=big)(kd, vd)
+        args = args + (tok,)
+        kdn, vdn, kpn, vpn, fh = pl.pallas_call(
             pipe_kernel,
-            out_shape=(jax.ShapeDtypeStruct((KVW, LN), F32), jax.ShapeDtypeStruct((KVW, LN), F32),
-                       jax.ShapeDtypeStruct(kp.shape, BF16), jax.ShapeDtypeStruct(vp.shape, BF16),
-                       jax.ShapeDtypeStruct((DR + 1, NM, VOC), F32)),
+            out_shape=(sds((KVW, LN), F32), sds((KVW, LN), F32), pshape, pshape, sds((ND + 8, HID), BF16)),
             in_specs=[ANY] * len(args),
-            out_specs=(ANY, ANY, ANY, ANY, pl.BlockSpec(memory_space=pltpu.VMEM)),
+            out_specs=(ANY,) * 5,
             scratch_shapes=scratch,
             name='pipe',
-            compiler_params=pltpu.CompilerParams(collective_id=0, has_side_effects=True, vmem_limit_bytes=60 * 1024 * 1024),
+            compiler_params=pltpu.CompilerParams(collective_id=0, has_side_effects=True, vmem_limit_bytes=62 * 1024 * 1024),
         )(*args)
+        bk, bv, bkp, bvp, tok2 = pl.pallas_call(
+            mid_kernel, out_shape=(cshape, cshape, pshape, pshape, tshape), in_specs=[smem] + [ANY] * 8, out_specs=(ANY,) * 4 + (vmem,),
+            input_output_aliases={3: 0, 4: 1},
+            scratch_shapes=[vm(kd.shape, BF16), vm(vd.shape, BF16), tile, tile] + news + nsems + [pltpu.SemaphoreType.DMA((4,))],
+            name='mid', compiler_params=big)(dec_len, kd, vd, bk, bv, kdn, vdn, kpn, vpn)
+        logits = pl.pallas_call(
+            head_kernel, out_shape=sds((DR + 1, NM, VOC), F32), in_specs=[ANY] * 3, out_specs=vmem,
+            scratch_shapes=[vm((ND + 8, HID), BF16), vm((ND + 8, HID), BF16), vm((HID, VOC), BF16),
+                            pltpu.SemaphoreType.DMA((2,)), pltpu.SemaphoreType.DMA((LAST,)), pltpu.SemaphoreType.DMA],
+            name='head', compiler_params=pltpu.CompilerParams(collective_id=1, has_side_effects=True))(fh, w_head, tok2)
         ko, vo, kpo, vpo = pl.pallas_call(
-            cache_kernel,
-            out_shape=tuple(jax.ShapeDtypeStruct(a.shape, BF16) for a in (kd, vd, kp, vp)),
-            in_specs=[pl.BlockSpec(memory_space=pltpu.SMEM)] + [ANY] * 6,
-            out_specs=(ANY,) * 4,
-            scratch_shapes=[vm(kd.shape, BF16), vm(vd.shape, BF16), vm((KVW, LN), F32), vm((KVW, LN), F32), vm(kp.shape, BF16), vm(vp.shape, BF16),
-                            pltpu.SemaphoreType.DMA((NM,)), pltpu.SemaphoreType.DMA((NM,)), pltpu.SemaphoreType.DMA((4,))],
-            name='caches',
-            compiler_params=pltpu.CompilerParams(vmem_limit_bytes=40 * 1024 * 1024),
-        )(dec_len, kd, vd, kdn, vdn, kpn, vpn)
+            post_kernel, out_shape=(cshape, cshape, pshape, pshape), in_specs=[smem] + [ANY] * 9, out_specs=(ANY,) * 4,
+            input_output_aliases={6: 0, 7: 1, 8: 2, 9: 3},
+            scratch_shapes=[tile, tile] + news + nsems + [pltpu.SemaphoreType.DMA((4,))],
+            name='post', compiler_params=big)(dec_len, kdn, vdn, kpn, vpn, logits, bk, bv, bkp, bvp)
         back = lambda a: jnp.transpose(a, (0, 1, 4, 2, 3))[None]
         backp = lambda a: jnp.transpose(a, (2, 0, 1))[None]
         return jnp.transpose(logits, (1, 0, 2)), back(ko), back(vo), backp(kpo), backp(vpo)

time: 74.3 us -> 65.1 us (0.88)
  the two profiles are of different devices: /device:TPU:5 before, /device:TPU:7 now
where the time goes in v2:
time: 65.1 us; the launch traced here: 64.9 us
  Pallas kernels  61.7 us (95%)
  local copies, waits for them, and re-layouts  1.93 us (3%)
  between operations  1.33 us (2%)
    pallas_call x1, Pallas kernels, device_fn(): pl.pallas_call(pipe_kernel, out_shape=(sds((KVW, LN), F32), sds((KVW, LN)...  41.6 us
    pallas_call x1, Pallas kernels, device_fn(): pl.pallas_call(pre_kernel, out_shape=(cshape, cshape, tshape), in_specs=[...  9.84 us
    pallas_call x1, Pallas kernels, device_fn(): pl.pallas_call(post_kernel, out_shape=(cshape, cshape, pshape, pshape), i...  5.37 us
    pallas_call x1, Pallas kernels, device_fn(): pl.pallas_call(head_kernel, out_shape=sds((DR + 1, NM, VOC), F32), in_spe...  3.21 us
    pallas_call x1, Pallas kernels, device_fn(): pl.pallas_call(mid_kernel, out_shape=(cshape, cshape, pshape, pshape, tsh...  1.6 us

profile of v2, /device:TPU:7, one launch (start us, length us, event | category | flops | bytes accessed | tf_op | source)
XLA Modules:
  0.0 64.9 jit_solution(2767145648473362476)
XLA Ops:
  1.3 1.3 %reshape.21.gf = bf16[1,576]{1,0:T(2,128)(2,1)} reshape(bf16[576]{0:T(1024)(128)(2,1)} %param.33) | data formatting | bytes 2304 | tf_op jit(solution)/shard_map/reshape | solution.py:520
  2.5 9.8 %pre.1 = (bf16[4,8,3,64,512]{4,3,2,1,0:T(8,128)(2,1)}, bf16[4,8,3,64,512]{4,3,2,1,0:T(8,128)(2,1)}, f32[8,128]{1,0:T(8,128)}) custom-call(bf16[4,8,3,64,512]{4,3,2,1,0:T(8,128)(2,1)} %bitcast.40, bf16[4,8,3,64,512]{4,3,2,1,0:T(8,128)(2,1)} %bitcast.43), custom_call_target="tpu_custom_call" | custom-call | tf_op jit(solution)/shard_map/pre/pallas_call | solution.py:546
  12.4 41.6 %pipe.1 = (f32[192,128]{1,0:T(8,128)}, f32[192,128]{1,0:T(8,128)}, bf16[3,64,512]{2,1,0:T(8,128)(2,1)}, bf16[3,64,512]{2,1,0:T(8,128)(2,1)}, bf16[40,576]{1,0:T(8,128)(2,1)}) custom-call(bf16[32,576]{1,0:T(8,128)(2,1)} %bitcast.61, bf16[256,576]{1,0:T(8,128)(2,1)} %bitcast.54, s32[4,8]{1,0:T(4,128)} %dlen.5, s32[1]{0:T(128)S(6)} %copy.38.plen, ...), custom_call_target="tpu_custom_call" | custom-call | tf_op jit(solution)/shard_map/pipe/pallas_call | solution.py:550
  54.0 1.6 %mid.1 = (bf16[4,8,3,64,512]{4,3,2,1,0:T(8,128)(2,1)}, bf16[4,8,3,64,512]{4,3,2,1,0:T(8,128)(2,1)}, bf16[3,64,512]{2,1,0:T(8,128)(2,1)}, bf16[3,64,512]{2,1,0:T(8,128)(2,1)}, f32[8,128]{1,0:T(8,128)}) custom-call(s32[4,8]{1,0:T(4,128)} %dlen.5, bf16[4,8,3,64,512]{4,3,2,1,0:T(8,128)(2,1)} %bitcast.42, ...), custom_call_target="tpu_custom_call", output_to_operand_aliasing={{0}: (3, {}), {1}: (4, {})} | custom-call | tf_op jit(solution)/shard_map/mid/pallas_call | solution.py:559
  55.6 3.2 %head.1.lg = f32[9,4,1024]{2,1,0:T(4,128)} custom-call(bf16[40,576]{1,0:T(8,128)(2,1)} %get-tuple-element.23.fh, bf16[576,1024]{1,0:T(8,128)(2,1)} %wh.1, f32[8,128]{1,0:T(8,128)} %get-tuple-element.30.tok), custom_call_target="tpu_custom_call" | custom-call | tf_op jit(solution)/shard_map/head/pallas_call | solution.py:564
  58.9 0.0 copy-start
  58.9 5.4 %post.1 = (bf16[4,8,3,64,512]{4,3,2,1,0:T(8,128)(2,1)}, bf16[4,8,3,64,512]{4,3,2,1,0:T(8,128)(2,1)}, bf16[3,64,512]{2,1,0:T(8,128)(2,1)}, bf16[3,64,512]{2,1,0:T(8,128)(2,1)}) custom-call(s32[4,8]{1,0:T(4,128)} %dlen.5, f32[192,128]{1,0:T(8,128)} %get-tuple-element.26.kdn, ...), custom_call_target="tpu_custom_call", output_to_operand_aliasing={{0}: (6, {}), {1}: (7, {}), {2}: (8, {}), {3}: (9, {})} | custom-call | tf_op jit(solution)/shard_map/post/pallas_call | solution.py:569
  64.2 0.0 copy-done
  64.3 0.7 %copy.39 = f32[4,9,1024]{2,0,1:T(4,128)} copy(f32[4,9,1024]{2,0,1:T(4,128)S(1)} %bitcast.51) | data formatting | bytes 294912
Async XLA Ops:
  58.9 5.4 %copy-start = (f32[9,4,1024]{2,1,0:T(4,128)S(1)}, f32[9,4,1024]{2,1,0:T(4,128)}, u32[]{:S(2)}) copy-start(f32[9,4,1024]{2,1,0:T(4,128)} %head.1.lg) | copy-start | bytes 442372

commit v3 on v2

--- a/solution.py
+++ b/solution.py
@@ -65,7 +65,7 @@
                 xd_s, xp_s, dl_s, pl_s, ga_s, wq_s, wk_s, wv_s, wo_s, gm_s, wg_s, wu_s, wd_s, gf_s,
                 kd_s, vd_s, kp_s, vp_s, ifr_s,
                 wqt_s, cosd_s, sind_s, cosp_s, sinp_s, cosl_s, sinl_s, qa_s, qb_s, self_s, vn_s, oa_s, ob_s,
-                kdn_s, vdn_s, ot_s, act_s, x4_s, sd_s, sp_s, fh_s,
+                kdn_s, vdn_s, sc_s, ps_s, pb_s, bias_s, ot_s, act_s, x4_s, sd_s, sp_s, fh_s,
                 in_sem, kd_sem, vd_sem, out_sem, sdd, sdp, rcd, rcp):
     st = lax.axis_index('stage')
     order = [(dlen, dl_s), (plen, pl_s), (xd, xd_s), (ga, ga_s), (ifr, ifr_s), (wq, wq_s), (wk, wk_s), (wv, wv_s),
@@ -159,22 +159,24 @@
         vn_s[b0:b0 + n, LN:] = jnp.concatenate([vt[LN:], jnp.zeros((HD, LN), F32)], axis=0).T[:n, :HD]
         return kt, vt, sf
 
-    def attn_dec(b, kt, vt, pos, selfcol):
-        qb = jnp.concatenate([qa_s[pl.ds(b * 8, 8), :], qb_s[pl.ds(b * 8, 8), :HD]], axis=1)
+    def dec_scores(b, kt, slot):
+        qb = jnp.concatenate([qa_s[b * 8:b * 8 + 8, :], qb_s[b * 8:b * 8 + 8, :HD]], axis=1)
         lhs = jnp.concatenate([jnp.where(lgrp == g, qb, 0.0) for g in range(NKV)], axis=0).astype(BF16)
-        s = nn(lhs, kt)
-        s = jnp.where(lane_iota((24, CL)) < pos, s, NEG)
+        sc_s[slot * 24:slot * 24 + 24, :] = nn(lhs, kt)
+
+    def dec_mix(b, vt, pos, selfcol, slot):
+        s = jnp.where(lane_iota((24, CL)) < pos, sc_s[slot * 24:slot * 24 + 24, :], NEG)
         mx = jnp.maximum(jnp.max(s, axis=-1, keepdims=True), selfcol)
         p = jnp.exp(s - mx)
         ps = jnp.exp(selfcol - mx)
         rl = 1.0 / (jnp.sum(p, axis=-1, keepdims=True) + ps)
         o = nt((p * rl).astype(BF16), vt)
-        o = o + (ps * rl).astype(BF16).astype(F32) * vn_s[pl.ds(b, 1), :]
+        o = o + (ps * rl).astype(BF16).astype(F32) * vn_s[b:b + 1, :]
         acc = jnp.where(lgrp == 0, o[0:8], 0.0)
         for g in range(1, NKV):
             acc = jnp.where(lgrp == g, o[8 * g:8 * g + 8], acc)
-        oa_s[pl.ds(b * 8, 8), :] = acc[:, :LN]
-        ob_s[pl.ds(b * 8, 8), :HD] = acc[:, LN:]
+        oa_s[b * 8:b * 8 + 8, :] = acc[:, :LN]
+        ob_s[b * 8:b * 8 + 8, :HD] = acc[:, LN:]
 
     def self_col(b):
         return jnp.sum(jnp.where(lane_iota((24, LN)) == b, self_s[...], 0.0), axis=-1, keepdims=True)
@@ -222,15 +224,21 @@
     okd.start()
     ovd.start()
 
-    def dec_loop(m, carry):
-        pltpu.make_async_copy(kd.at[m], kd_s.at[m], kd_sem.at[m]).wait()
-        pltpu.make_async_copy(vd.at[m], vd_s.at[m], vd_sem.at[m]).wait()
+    def dec_qk(m):
+        for i in range(DR):
+            dec_scores(m * DR + i, kd_s[m, i].reshape(KVW, CL), (m % 2) * DR + i)
+
+    kcp[0].wait()
+    dec_qk(0)
+    for m in range(NM):
+        if m + 1 < NM:
+            kcp[m + 1].wait()
+        vcp[m].wait()
+        if m + 1 < NM:
+            dec_qk(m + 1)
         for i in range(DR):
             b = m * DR + i
-            attn_dec(b, kd_s[m, i].reshape(KVW, CL), vd_s[m, i].reshape(KVW, CL), dl_s[m, i], self_col(b))
-        return carry
-
-    lax.fori_loop(0, NM, dec_loop, 0)
+            dec_mix(b, vd_s[m, i].reshape(KVW, CL), dl_s[m, i], self_col(b), (m % 2) * DR + i)
 
     for r in (wo_s, gm_s, wg_s, wu_s, wd_s):
         ld(r).wait()
@@ -281,8 +289,10 @@
         kfull = kpu.T.astype(BF16)
         vfull = vp_s[...].reshape(KVW, CL)
         qt = (rope_t(nt(wqt_s[...], hp), cosp_s[...], sinp_s[...]).astype(BF16).astype(F32) * (HD ** -0.5)).astype(BF16)
-        bias = jnp.where(lax.broadcasted_iota(jnp.int32, (CL, NP), 0) <= lane_iota((CL, NP)) + p0, 0.0, NEG)
-        for j in range(NQ):
+        bias_s[...] = jnp.where(lax.broadcasted_iota(jnp.int32, (CL, NP), 0) <= lane_iota((CL, NP)) + p0, 0.0, NEG)
+        hi = (CL - LN, CL)
+
+        def scores(j):
             g = j // GRP
             parts = []
             if g:
@@ -290,10 +300,39 @@
             parts.append(qt[j * HD:(j + 1) * HD])
             if g < NKV - 1:
                 parts.append(jnp.zeros(((NKV - 1 - g) * HD, NP), BF16))
-            s = nn(kfull, jnp.concatenate(parts, axis=0)) + bias
-            p = jnp.exp(s - jnp.max(s, axis=0, keepdims=True))
-            pr = (p * (1.0 / jnp.sum(p, axis=0, keepdims=True))).astype(BF16)
-            ot_s[j * HD:(j + 1) * HD, :] = nn(vfull[g * HD:(g + 1) * HD], pr)
+            ps_s[j % 2] = nn(kfull, jnp.concatenate(parts, axis=0))
+
+        def fold(x, op):
+            x = x.reshape(x.shape[0] // 8, 8, x.shape[1])
+            return op(x, axis=0)
+
+        def mix(j):
+            g = j // GRP
+            sl = j % 2
+            ck = 64
+            for h in range(2):
+                ln = slice(h * LN, (h + 1) * LN)
+                mx = jnp.full((8, LN), NEG, F32)
+                for c in range(0, hi[h], ck):
+                    mx = jnp.maximum(mx, fold(ps_s[sl, c:c + ck, ln] + bias_s[c:c + ck, ln], jnp.max))
+                mx = jnp.max(mx, axis=0, keepdims=True)
+                sm = jnp.zeros((8, LN), F32)
+                for c in range(0, hi[h], ck):
+                    p = jnp.exp(ps_s[sl, c:c + ck, ln] + bias_s[c:c + ck, ln] - mx)
+                    ps_s[sl, c:c + ck, ln] = p
+                    sm = sm + fold(p, jnp.sum)
+                rl = 1.0 / jnp.sum(sm, axis=0, keepdims=True)
+                for c in range(0, hi[h], ck):
+                    pb_s[sl, c:c + ck, ln] = (ps_s[sl, c:c + ck, ln] * rl).astype(BF16)
+            ot_s[j * HD:(j + 1) * HD, :] = nn(vfull[g * HD:(g + 1) * HD], pb_s[sl])
+
+        for k in range(2):
+            pb_s[k, CL - LN:, :LN] = jnp.zeros((LN, LN), BF16)
+        scores(0)
+        for j in range(NQ):
+            if j + 1 < NQ:
+                scores(j + 1)
+            mix(j)
         x1 = round32(xp_s[...].astype(F32) + nn(ot_s[...].T.astype(BF16), wo_s[...]))
         sp_s[...] = mlp(x1, NP)
         hop(sp_s, xp_s, sdp, rcp).start()
@@ -311,15 +350,17 @@
         h4 = jnp.concatenate([h4, jnp.zeros_like(h4)], axis=0)
         _, _, sf4 = qkv_dec(h4, cosl_s[...], sinl_s[...], ND, 8)
         for m in range(NM):
+            dec_scores(ND + m, kp_s[...].reshape(KVW, CL), m)
+        for m in range(NM):
             col = jnp.sum(jnp.where(lane_iota((24, LN)) == m, sf4, 0.0), axis=-1, keepdims=True)
-            attn_dec(ND + m, kp_s[...].reshape(KVW, CL), vp_s[...].reshape(KVW, CL), p0 + m * SEG + SEG - 1, col)
+            dec_mix(ND + m, vp_s[...].reshape(KVW, CL), p0 + m * SEG + SEG - 1, col, m)
         for m in range(NM, 8):
             oa_s[pl.ds((ND + m) * 8, 8), :] = jnp.zeros((8, LN), F32)
         a = dec_out(0, ND + 8)
         y = nn(a[0], wo_rows(0)) + nn(a[1], wo_rows(1)) + nn(a[2], wo_rows(2))
         x1 = round32(jnp.concatenate([xd_s[...].astype(F32), x4], axis=0) + y)
         x2 = mlp(x1, ND + 8)
-        fh = rms(x2.astype(F32), gf_s[...].astype(F32))
+        fh = rms(x2.astype(F32), gf_s[...].astype(F32).reshape(1, HID))
         ri = lax.broadcasted_iota(jnp.int32, (ND + 8, ND + 8), 0)
         src = jnp.where(ri < ND, (ri % NM) * DR + ri // NM, ri)
         fh_s[...] = nn(jnp.where(lane_iota((ND + 8, ND + 8)) == src, 1.0, 0.0).astype(BF16), fh).astype(BF16)
@@ -406,7 +447,6 @@
 
 def pre_kernel(kd, vd, ko, vo, tok, ks, vs, ksem, vsem):
     st = lax.axis_index('stage')
-    tok[...] = jnp.zeros_like(tok)
 
     @pl.when(st >= 2)
     def _():
@@ -428,11 +468,12 @@
         v = scr.at[m, i]
         return pltpu.make_async_copy(v, h, sem.at[m]) if out else pltpu.make_async_copy(h, v, sem.at[m])
 
+    cs[4].wait()
     for m in range(NM):
         for i in range(DR):
             cp(bk, kt, ksem, m, i, False).start()
             cp(bv, vt, vsem, m, i, False).start()
-    for c in cs:
+    for c in cs[:4]:
         c.wait()
     po = [pltpu.make_async_copy(new[2], kpo, nsem.at[2]), pltpu.make_async_copy(new[3], vpo, nsem.at[3])]
     for o in po:
@@ -456,14 +497,13 @@
         o.wait()
 
 
-def mid_kernel(dlen, kd, vd, bk, bv, kdn, vdn, kpn, vpn, ko, vo, kpo, vpo, tok, ks, vs, kt, vt, kn_s, vn_s, kp_s, vp_s, ksem, vsem, nsem):
+def mid_kernel(dlen_h, kd, vd, bk, bv, kdn, vdn, kpn, vpn, ko, vo, kpo, vpo, tok, ks, vs, kt, vt, kn_s, vn_s, kp_s, vp_s, dlen, ksem, vsem, nsem):
     st = lax.axis_index('stage')
-    tok[...] = jnp.zeros_like(tok)
     new = (kn_s, vn_s, kp_s, vp_s)
 
     @pl.when(st < 2)
     def _():
-        cs = load_new((kdn, vdn, kpn, vpn), new, nsem)
+        cs = load_new((kdn, vdn, kpn, vpn, dlen_h), new + (dlen,), nsem)
         for c in cs:
             c.wait()
         po = [pltpu.make_async_copy(kp_s, kpo, nsem.at[2]), pltpu.make_async_copy(vp_s, vpo, nsem.at[3])]
@@ -485,17 +525,17 @@
 
     @pl.when(st == 2)
     def _():
-        cs = load_new((kdn, vdn, kpn, vpn), new, nsem)
+        cs = load_new((kdn, vdn, kpn, vpn, dlen_h), new + (dlen,), nsem)
         update_tiles(dlen, bk, bv, ko, vo, kpo, vpo, kt, vt, new, cs, ksem, vsem, nsem)
 
 
-def post_kernel(dlen, kdn, vdn, kpn, vpn, lg, bk, bv, bkp, bvp, ko, vo, kpo, vpo, kt, vt, kn_s, vn_s, kp_s, vp_s, ksem, vsem, nsem):
+def post_kernel(dlen_h, kdn, vdn, kpn, vpn, lg, bk, bv, bkp, bvp, ko, vo, kpo, vpo, kt, vt, kn_s, vn_s, kp_s, vp_s, dlen, ksem, vsem, nsem):
     st = lax.axis_index('stage')
 
     @pl.when(st == LAST)
     def _():
         new = (kn_s, vn_s, kp_s, vp_s)
-        cs = load_new((kdn, vdn, kpn, vpn), new, nsem)
+        cs = load_new((kdn, vdn, kpn, vpn, dlen_h), new + (dlen,), nsem)
         update_tiles(dlen, bk, bv, ko, vo, kpo, vpo, kt, vt, new, cs, ksem, vsem, nsem)
 
 
@@ -517,18 +557,19 @@
         kp = jnp.transpose(k_pre[0], (1, 2, 0))
         vp = jnp.transpose(v_pre[0], (1, 2, 0))
         args = (x_dec.reshape(ND, HID), x_pre.reshape(NP, HID), dec_len, pre_len, g_attn, w_q[0], w_k[0].T, w_v[0].T, w_o[0], g_mlp,
-                w_gate[0], w_up[0], w_down[0].T, g_final.reshape(1, HID), kd, vd, kp, vp, jnp.asarray(ifr_c))
+                w_gate[0], w_up[0], w_down[0].T, g_final, kd, vd, kp, vp, jnp.asarray(ifr_c))
         vm = lambda shape, dt: pltpu.VMEM(shape, dt)
         scratch = [
             vm((ND, HID), BF16), vm((NP, HID), BF16), pltpu.SMEM((NM, DR), jnp.int32), pltpu.SMEM((1,), jnp.int32), vm((1, HID), BF16),
             vm((HID, HID), BF16), vm((KVW, HID), BF16), vm((KVW, HID), BF16), vm((HID, HID), BF16), vm((1, HID), BF16),
-            vm((HID, FFN), BF16), vm((HID, FFN), BF16), vm((HID, FFN), BF16), vm((1, HID), BF16),
+            vm((HID, FFN), BF16), vm((HID, FFN), BF16), vm((HID, FFN), BF16), vm((HID,), BF16),
             vm(kd.shape, BF16), vm(vd.shape, BF16), vm(kp.shape, BF16), vm(vp.shape, BF16), vm((HALF, NP), F32),
             vm((HID, HID), BF16), vm((HALF, LN), F32), vm((HALF, LN), F32), vm((HALF, NP), F32), vm((HALF, NP), F32),
             vm((HALF, LN), F32), vm((HALF, LN), F32),
             vm(((ND + 8) * 8, LN), F32), vm(((ND + 8) * 8, LN), F32), vm((24, LN), F32), vm((ND + 8, KVW), F32),
             vm(((ND + 8) * 8, LN), F32), vm(((ND + 8) * 8, LN), F32),
-            vm((KVW, LN), F32), vm((KVW, LN), F32), vm((HID, NP), F32), vm((NP, FFN), BF16), vm((8, HID), F32),
+            vm((KVW, LN), F32), vm((KVW, LN), F32), vm((2 * DR * 24, CL), F32), vm((2, CL, NP), F32), vm((2, CL, NP), BF16), vm((CL, NP), F32),
+            vm((HID, NP), F32), vm((NP, FFN), BF16), vm((8, HID), F32),
             vm((ND, HID), BF16), vm((NP, HID), BF16), vm((ND + 8, HID), BF16),
             pltpu.SemaphoreType.DMA((17,)), pltpu.SemaphoreType.DMA((NM,)), pltpu.SemaphoreType.DMA((NM,)), pltpu.SemaphoreType.DMA((5,)),
             pltpu.SemaphoreType.DMA, pltpu.SemaphoreType.DMA, pltpu.SemaphoreType.DMA, pltpu.SemaphoreType.DMA,
@@ -539,12 +580,11 @@
         pshape = sds(kp.shape, BF16)
         nsems = [pltpu.SemaphoreType.DMA((NM,)), pltpu.SemaphoreType.DMA((NM,))]
         tile = vm((NM, DR, NKV, HD, LN), BF16)
-        news = [vm((KVW, LN), F32), vm((KVW, LN), F32), vm(kp.shape, BF16), vm(vp.shape, BF16)]
-        smem = pl.BlockSpec(memory_space=pltpu.SMEM)
+        news = [vm((KVW, LN), F32), vm((KVW, LN), F32), vm(kp.shape, BF16), vm(vp.shape, BF16), pltpu.SMEM((NM, DR), jnp.int32)]
         vmem = pl.BlockSpec(memory_space=pltpu.VMEM)
         tshape = sds((8, LN), F32)
         bk, bv, tok = pl.pallas_call(
-            pre_kernel, out_shape=(cshape, cshape, tshape), in_specs=[ANY, ANY], out_specs=(ANY, ANY, vmem),
+            pre_kernel, out_shape=(cshape, cshape, tshape), in_specs=[ANY, ANY], out_specs=(ANY, ANY, ANY),
             scratch_shapes=[vm(kd.shape, BF16), vm(vd.shape, BF16)] + nsems, name='pre', compiler_params=big)(kd, vd)
         args = args + (tok,)
         kdn, vdn, kpn, vpn, fh = pl.pallas_call(
@@ -557,9 +597,9 @@
             compiler_params=pltpu.CompilerParams(collective_id=0, has_side_effects=True, vmem_limit_bytes=62 * 1024 * 1024),
         )(*args)
         bk, bv, bkp, bvp, tok2 = pl.pallas_call(
-            mid_kernel, out_shape=(cshape, cshape, pshape, pshape, tshape), in_specs=[smem] + [ANY] * 8, out_specs=(ANY,) * 4 + (vmem,),
+            mid_kernel, out_shape=(cshape, cshape, pshape, pshape, tshape), in_specs=[ANY] * 9, out_specs=(ANY,) * 5,
             input_output_aliases={3: 0, 4: 1},
-            scratch_shapes=[vm(kd.shape, BF16), vm(vd.shape, BF16), tile, tile] + news + nsems + [pltpu.SemaphoreType.DMA((4,))],
+            scratch_shapes=[vm(kd.shape, BF16), vm(vd.shape, BF16), tile, tile] + news + nsems + [pltpu.SemaphoreType.DMA((5,))],
             name='mid', compiler_params=big)(dec_len, kd, vd, bk, bv, kdn, vdn, kpn, vpn)
         logits = pl.pallas_call(
             head_kernel, out_shape=sds((DR + 1, NM, VOC), F32), in_specs=[ANY] * 3, out_specs=vmem,
@@ -567,9 +607,9 @@
                             pltpu.SemaphoreType.DMA((2,)), pltpu.SemaphoreType.DMA((LAST,)), pltpu.SemaphoreType.DMA],
             name='head', compiler_params=pltpu.CompilerParams(collective_id=1, has_side_effects=True))(fh, w_head, tok2)
         ko, vo, kpo, vpo = pl.pallas_call(
-            post_kernel, out_shape=(cshape, cshape, pshape, pshape), in_specs=[smem] + [ANY] * 9, out_specs=(ANY,) * 4,
+            post_kernel, out_shape=(cshape, cshape, pshape, pshape), in_specs=[ANY] * 10, out_specs=(ANY,) * 4,
             input_output_aliases={6: 0, 7: 1, 8: 2, 9: 3},
-            scratch_shapes=[tile, tile] + news + nsems + [pltpu.SemaphoreType.DMA((4,))],
+            scratch_shapes=[tile, tile] + news + nsems + [pltpu.SemaphoreType.DMA((5,))],
             name='post', compiler_params=big)(dec_len, kdn, vdn, kpn, vpn, logits, bk, bv, bkp, bvp)
         back = lambda a: jnp.transpose(a, (0, 1, 4, 2, 3))[None]
         backp = lambda a: jnp.transpose(a, (2, 0, 1))[None]

time: 65.1 us -> 51.5 us (0.79)
  Pallas kernels: 61.7 us -> 49.3 us
  local copies, waits for them, and re-layouts: 1.93 us -> 0.67 us
    pallas_call x1, Pallas kernels: 41.6 us -> 32.2 us  [device_fn(): pl.pallas_call(pipe_kernel, out_shape=(sds((KVW, LN), F32), sds((KVW, LN)...]
    pallas_call x1, Pallas kernels: 1.6 us -> 0.32 us  [device_fn(): pl.pallas_call(mid_kernel, out_shape=(cshape, cshape, pshape, pshape, tsh...]
    reshape x1 -> x0, local copies, waits for them, and re-layouts: 1.26 us -> none  [device_fn(): g_final.reshape(1, HID)]
    pallas_call x1, Pallas kernels: 5.37 us -> 4.3 us  [device_fn(): pl.pallas_call(post_kernel, out_shape=(cshape, cshape, pshape, pshape), i...]
where the time goes in v3:
time: 51.5 us; the launch traced here: 51.3 us
  Pallas kernels  49.3 us (96%)
  between operations  1.33 us (3%)
  local copies, waits for them, and re-layouts  0.67 us (1%)
    pallas_call x1, Pallas kernels, device_fn(): pl.pallas_call(pipe_kernel, out_shape=(sds((KVW, LN), F32), sds((KVW, LN)...  32.2 us
    pallas_call x1, Pallas kernels, device_fn(): pl.pallas_call(pre_kernel, out_shape=(cshape, cshape, tshape), in_specs=[...  9.26 us
    pallas_call x1, Pallas kernels, device_fn(): pl.pallas_call(post_kernel, out_shape=(cshape, cshape, pshape, pshape), i...  4.3 us
    pallas_call x1, Pallas kernels, device_fn(): pl.pallas_call(head_kernel, out_shape=sds((DR + 1, NM, VOC), F32), in_spe...  3.21 us

profile of v3, /device:TPU:7, one launch (start us, length us, event | category | flops | bytes accessed | tf_op | source)
XLA Modules:
  0.0 51.3 jit_solution(17420284104209935582)
XLA Ops:
  1.3 9.3 %pre.1 = (bf16[4,8,3,64,512]{4,3,2,1,0:T(8,128)(2,1)}, bf16[4,8,3,64,512]{4,3,2,1,0:T(8,128)(2,1)}, f32[8,128]{1,0:T(8,128)}) custom-call(bf16[4,8,3,64,512]{4,3,2,1,0:T(8,128)(2,1)} %bitcast.40, bf16[4,8,3,64,512]{4,3,2,1,0:T(8,128)(2,1)} %bitcast.43), custom_call_target="tpu_custom_call" | custom-call | tf_op jit(solution)/shard_map/pre/pallas_call | solution.py:586
  10.5 32.2 %pipe.1 = (f32[192,128]{1,0:T(8,128)}, f32[192,128]{1,0:T(8,128)}, bf16[3,64,512]{2,1,0:T(8,128)(2,1)}, bf16[3,64,512]{2,1,0:T(8,128)(2,1)}, bf16[40,576]{1,0:T(8,128)(2,1)}) custom-call(bf16[32,576]{1,0:T(8,128)(2,1)} %bitcast.61, bf16[256,576]{1,0:T(8,128)(2,1)} %bitcast.54, s32[4,8]{1,0:T(4,128)} %dlen_h.3, s32[1]{0:T(128)S(6)} %copy.38.plen, ...), custom_call_target="tpu_custom_call" | custom-call | tf_op jit(solution)/shard_map/pipe/pallas_call | solution.py:590
  42.8 0.3 mid.1
  43.1 3.2 %head.1.lg = f32[9,4,1024]{2,1,0:T(4,128)} custom-call(bf16[40,576]{1,0:T(8,128)(2,1)} %get-tuple-element.23.fh, bf16[576,1024]{1,0:T(8,128)(2,1)} %wh.1, f32[8,128]{1,0:T(8,128)} %get-tuple-element.30.tok), custom_call_target="tpu_custom_call" | custom-call | tf_op jit(solution)/shard_map/head/pallas_call | solution.py:604
  46.3 0.0 copy-start
  46.4 4.3 %post.1 = (bf16[4,8,3,64,512]{4,3,2,1,0:T(8,128)(2,1)}, bf16[4,8,3,64,512]{4,3,2,1,0:T(8,128)(2,1)}, bf16[3,64,512]{2,1,0:T(8,128)(2,1)}, bf16[3,64,512]{2,1,0:T(8,128)(2,1)}) custom-call(s32[4,8]{1,0:T(4,128)} %dlen_h.3, f32[192,128]{1,0:T(8,128)} %get-tuple-element.26.kdn, ...), custom_call_target="tpu_custom_call", output_to_operand_aliasing={{0}: (6, {}), {1}: (7, {}), {2}: (8, {}), {3}: (9, {})} | custom-call | tf_op jit(solution)/shard_map/post/pallas_call | solution.py:609
  50.7 0.0 copy-done
  50.7 0.7 %copy.39 = f32[4,9,1024]{2,0,1:T(4,128)} copy(f32[4,9,1024]{2,0,1:T(4,128)S(1)} %bitcast.51) | data formatting | bytes 294912
Async XLA Ops:
  46.3 4.3 %copy-start = (f32[9,4,1024]{2,1,0:T(4,128)S(1)}, f32[9,4,1024]{2,1,0:T(4,128)}, u32[]{:S(2)}) copy-start(f32[9,4,1024]{2,1,0:T(4,128)} %head.1.lg) | copy-start | bytes 442372

commit v4 on v2

v4 whole, which is shorter than its diff:
```python
import functools

import jax
import jax.numpy as jnp
import numpy as np
from jax import lax
from jax.experimental import pallas as pl
from jax.experimental.pallas import tpu as pltpu
from jax.sharding import PartitionSpec as P

F32 = jnp.float32
BF16 = jnp.bfloat16
MESH = pl.DeviceIdType.MESH
NORM_EPS = 1e-6
ROPE_BASE = 10000.0
NEG = -1e30

HID = 576
NQ = 9
NKV = 3
GRP = 3
HD = 64
HALF = 32
KVW = NKV * HD
FFN = 1536
NM = 4
DR = 8
SEG = 64
CL = 512
VOC = 1024
ND = NM * DR
NP = NM * SEG
LAST = 3
LN = 128
CP = 128
CD = 16
CR = CP + CD
ES = CD + 8
FR = ND + 8


def nt(a, b):
    return lax.dot_general(a, b, (((1,), (1,)), ((), ())), preferred_element_type=F32)


def nn(a, b):
    return jnp.dot(a, b, preferred_element_type=F32)


def rms(x, g):
    inv = lax.rsqrt(jnp.mean(x * x, axis=-1, keepdims=True) + NORM_EPS)
    return (x * inv * g).astype(BF16)


def rope_t(m, cos, sin):
    parts = []
    for j in range(m.shape[0] // HD):
        a = m[j * HD:j * HD + HALF]
        b = m[j * HD + HALF:(j + 1) * HD]
        parts += [a * cos - b * sin, b * cos + a * sin]
    return jnp.concatenate(parts, axis=0)


def lane_iota(shape):
    return lax.broadcasted_iota(jnp.int32, shape, len(shape) - 1)


def pipe_kernel(xd, xp, dlen, plen, ga, wq, wk, wv, wo, gm, wg, wu, wd, gf, kd, vd, kp, vp, ifr, tok,
                kdn, vdn, kpn, vpn, fh_o,
                xc_s, dl_s, pl_s, ga_s, wq_s, w3_s, wo_s, gm_s, wg_s, wu_s, wd_s, gf_s,
                kd_s, vd_s, kp_s, vp_s, ifr_s,
                cos_s, sin_s, qt_s, qa_s, qb_s, self_s, vn_s, oa_s, ob_s,
                kdn_s, vdn_s, sc_s, ps_s, pb_s, bias_s, ot_s, act_s, so_s, fh_s,
                in_sem, kd_sem, vd_sem, out_sem, ssem, rsem):
    st = lax.axis_index('stage')
    order = [(dlen, dl_s), (plen, pl_s), (ga, ga_s), (ifr, ifr_s), (wq, wq_s), (wk, w3_s.at[HID:HID + KVW]), (wv, w3_s.at[HID + KVW:]),
             (kp, kp_s), (vp, vp_s), (wo, wo_s), (gm, gm_s), (wg, wg_s), (wu, wu_s), (wd, wd_s), (gf, gf_s),
             (xp.at[0:CP], xc_s.at[0, 0:CP]), (xd.at[0:CD], xc_s.at[0, CP:CR]), (xp.at[CP:2 * CP], xc_s.at[1, 0:CP]), (xd.at[CD:2 * CD], xc_s.at[1, CP:CR])]
    names = ['dl', 'pl', 'ga', 'ifr', 'wq', 'wk', 'wv', 'kp', 'vp', 'wo', 'gm', 'wg', 'wu', 'wd', 'gf', 'p0', 'd0', 'p1', 'd1']
    cps = {n: pltpu.make_async_copy(a, b, in_sem.at[i]) for i, (n, (a, b)) in enumerate(zip(names, order))}
    kcp = [pltpu.make_async_copy(kd.at[m], kd_s.at[m], kd_sem.at[m]) for m in range(NM)]
    vcp = [pltpu.make_async_copy(vd.at[m], vd_s.at[m], vd_sem.at[m]) for m in range(NM)]

    def start(*ns):
        for n in ns:
            cps[n].start()

    def wait(*ns):
        for n in ns:
            cps[n].wait()

    start('dl', 'pl', 'ifr', 'ga', 'wq', 'wk', 'wv')

    @pl.when(st == 0)
    def _():
        start('p0', 'd0')

    bar = pltpu.get_barrier_semaphore()

    @pl.when(st > 0)
    def _():
        pl.semaphore_signal(bar, inc=1, device_id={'stage': jnp.maximum(st - 1, 0)}, device_id_type=MESH)

    @pl.when(st < LAST)
    def _():
        pl.semaphore_signal(bar, inc=1, device_id={'stage': jnp.minimum(st + 1, LAST)}, device_id_type=MESH)

    wait('dl', 'pl', 'ifr')
    p0 = pl_s[0]
    li = lane_iota((1, 2 * LN))
    fr = ifr_s[...]
    for c in range(2):
        pos = p0 + (c * CP) + li
        for k in range(CD):
            pos = jnp.where(li == LN + k, dl_s[2 * c + k // DR, k % DR], pos)
        for k in range(2):
            pos = jnp.where(li == LN + CD + k, p0 + (c * CP + k * SEG + SEG - 1), pos)
        ang = fr * pos.astype(F32)
        cos_s[c] = jnp.cos(ang)
        sin_s[c] = jnp.sin(ang)
    qa_s[...] = jnp.zeros_like(qa_s)
    qb_s[...] = jnp.zeros_like(qb_s)
    ob_s[...] = jnp.zeros_like(ob_s)
    for k in range(2):
        pb_s[k] = jnp.zeros((CL, 2 * LN), BF16)

    start('kp', 'vp')
    for m in range(2):
        kcp[m].start()
        vcp[m].start()
    start('wo', 'gm')
    wait('ga', 'wq')
    w3_s[:HID, :] = wq_s[...].astype(F32).T.astype(BF16)
    wait('wk', 'wv')
    gat = ga_s[...].astype(F32)

    lgrp = lane_iota((8, KVW)) // HD

    def dec_scores(e, kt, slot):
        qb = jnp.concatenate([qa_s[e * 8:e * 8 + 8, :], qb_s[e * 8:e * 8 + 8, :HD]], axis=1)
        lhs = jnp.concatenate([jnp.where(lgrp == g, qb, 0.0) for g in range(NKV)], axis=0).astype(BF16)
        sc_s[slot * 24:slot * 24 + 24, :] = nn(lhs, kt)

    def dec_mix(c, k, vt, pos, slot):
        e = c * ES + k
        selfcol = jnp.sum(jnp.where(lane_iota((24, LN)) == k, self_s[c], 0.0), axis=-1, keepdims=True)
        s = jnp.where(lane_iota((24, CL)) < pos, sc_s[slot * 24:slot * 24 + 24, :], NEG)
        mx = jnp.maximum(jnp.max(s, axis=-1, keepdims=True), selfcol)
        p = jnp.exp(s - mx)
        ps = jnp.exp(selfcol - mx)
        rl = 1.0 / (jnp.sum(p, axis=-1, keepdims=True) + ps)
        o = nt((p * rl).astype(BF16), vt)
        o = o + (ps * rl).astype(BF16).astype(F32) * vn_s[e:e + 1, :]
        acc = jnp.where(lgrp == 0, o[0:8], 0.0)
        for g in range(1, NKV):
            acc = jnp.where(lgrp == g, o[8 * g:8 * g + 8], acc)
        oa_s[e * 8:e * 8 + 8, :] = acc[:, :LN]
        ob_s[e * 8:e * 8 + 8, :HD] = acc[:, LN:]

    def dec_out(e, n):
        return jnp.concatenate([x for r in range(GRP) for x in
                                (oa_s[pl.ds(e * 8 + r, n, stride=8), :], ob_s[pl.ds(e * 8 + r, n, stride=8), :][:, :HD])], axis=1)

    def wo_perm():
        return jnp.concatenate([wo_s[(g * GRP + r) * HD:(g * GRP + r + 1) * HD, :] for r in range(GRP) for g in range(NKV)], axis=0)

    def mlp(x, rows):
        h2 = rms(x, gm_s[...].astype(F32))
        step = 512
        for c in range(FFN // step):
            gt = nn(h2, wg_s[:, c * step:(c + 1) * step])
            up = nn(h2, wu_s[:, c * step:(c + 1) * step])
            act_s[:rows, c * step:(c + 1) * step] = (gt * (1.0 / (1.0 + jnp.exp(-gt))) * up).astype(BF16)
        return (x + nt(act_s[:rows, :], wd_s[...])).astype(BF16)

    def round32(x):
        return x.astype(BF16).astype(F32)

    def hop(c):
        return pltpu.make_async_remote_copy(so_s.at[c], xc_s.at[c], ssem.at[c], rsem.at[c],
                                            device_id={'stage': jnp.minimum(st + 1, LAST)}, device_id_type=MESH)

    def last_rows(x):
        return [x[k * SEG + SEG - 1:k * SEG + SEG] for k in range(2)]

    for c in range(2):
        lim = CL - CP if c == 0 else CL

        @pl.when(st == 0)
        def _():
            wait('p%d' % c, 'd%d' % c)

        @pl.when(st > 0)
        def _():
            hop(c).wait_recv()

        x = xc_s[c].astype(F32)
        h = x * lax.rsqrt(jnp.mean(x * x, axis=-1, keepdims=True) + NORM_EPS) * gat
        h = jnp.concatenate([h] + last_rows(h) + [jnp.zeros((2 * LN - CR - 2, HID), F32)], axis=0).astype(BF16)
        qkv = nt(w3_s[...], h)
        cos, sin = cos_s[c], sin_s[c]
        qt = round32(rope_t(qkv[:HID], cos, sin)) * (HD ** -0.5)
        kt = round32(rope_t(qkv[HID:HID + KVW], cos, sin))
        vt = round32(qkv[HID + KVW:])
        qt_s[...] = qt[:, :LN].astype(BF16)
        qe, ke, ve = qt[:, LN:], kt[:, LN:], vt[:, LN:]
        row = lax.broadcasted_iota(jnp.int32, (24, LN), 0)
        sf = jnp.zeros((24, LN), F32)
        for g in range(NKV):
            for r in range(GRP):
                j = g * GRP + r
                v = jnp.sum(qe[j * HD:(j + 1) * HD] * ke[g * HD:(g + 1) * HD], axis=0, keepdims=True)
                sf = jnp.where(row == 8 * g + r, v, sf)
        self_s[c] = sf
        n = CD + 8
        e0 = c * ES
        pad = jnp.zeros((HD, LN), F32)
        for r in range(GRP):
            qr = [qe[(g * GRP + r) * HD:(g * GRP + r + 1) * HD] for g in range(NKV)]
            qa_s[pl.ds(e0 * 8 + r, n, stride=8), :] = jnp.concatenate(qr[:2], axis=0).T[:n]
            qb_s[pl.ds(e0 * 8 + r, n, stride=8), :] = jnp.concatenate([qr[2], pad], axis=0).T[:n]
        vn_s[e0:e0 + n, :LN] = ve[:LN].T[:n]
        vn_s[e0:e0 + n, LN:] = jnp.concatenate([ve[LN:], pad], axis=0).T[:n, :HD]
        kdn_s[c] = ke
        vdn_s[c] = ve
        pltpu.make_async_copy(kdn_s.at[c], kdn.at[c], out_sem.at[c]).start()
        pltpu.make_async_copy(vdn_s.at[c], vdn.at[c], out_sem.at[2 + c]).start()

        if c == 0:
            wait('kp', 'vp')
            start('wg', 'wu', 'wd', 'gf')
        off = p0 + c * CP
        place = jnp.where(lax.broadcasted_iota(jnp.int32, (CP, CL), 0) + off == lane_iota((CP, CL)), 1.0, 0.0).astype(BF16)
        lp = lane_iota((KVW, CL)) - off
        fresh = (lp >= 0) & (lp < CP)
        kpu = jnp.where(fresh, nn(kt[:, :LN].astype(BF16), place), kp_s[...].reshape(KVW, CL).astype(F32))
        vpu = jnp.where(fresh, nn(vt[:, :LN].astype(BF16), place), vp_s[...].reshape(KVW, CL).astype(F32))
        kp_s[...] = kpu.astype(BF16).reshape(NKV, HD, CL)
        vp_s[...] = vpu.astype(BF16).reshape(NKV, HD, CL)
        if c == 1:
            pltpu.make_async_copy(kp_s, kpn, out_sem.at[4]).start()
            pltpu.make_async_copy(vp_s, vpn, out_sem.at[5]).start()

        for m in (2 * c, 2 * c + 1):
            kcp[m].wait()
            vcp[m].wait()
        if c == 0:
            @pl.when(st == 0)
            def _():
                start('p1', 'd1')
            for m in (2, 3):
                kcp[m].start()
                vcp[m].start()
            wait('wo', 'gm')

        def dqk(i):
            for k in range(DR):
                dec_scores(c * ES + i * DR + k, kd_s[2 * c + i, k].reshape(KVW, CL), i * DR + k)

        def dmix(i):
            for k in range(DR):
                dec_mix(c, i * DR + k, vd_s[2 * c + i, k].reshape(KVW, CL), dl_s[2 * c + i, k], i * DR + k)

        @pl.when(st < LAST)
        def _():
            kfull = kpu[:, :lim].T.astype(BF16)
            bias_s[:lim, :] = jnp.where(lax.broadcasted_iota(jnp.int32, (lim, LN), 0) <= lane_iota((lim, LN)) + off, 0.0, NEG)

            def heads(t):
                return [j for j in (2 * t, 2 * t + 1) if j < NQ]

            def scores(t):
                cols = []
                for j in heads(t):
                    g = j // GRP
                    parts = [jnp.zeros((g * HD, LN), BF16)] * (g > 0) + [qt_s[j * HD:(j + 1) * HD, :]]
                    parts += [jnp.zeros(((NKV - 1 - g) * HD, LN), BF16)] * (g < NKV - 1)
                    cols.append(jnp.concatenate(parts, axis=0))
                w = len(cols) * LN
                ps_s[t % 2, :lim, :w] = nn(kfull, jnp.concatenate(cols, axis=1))

            def fold(v, op):
                return op(v.reshape(v.shape[0] // 8, 8, v.shape[1]), axis=0)

            def mix(t):
                sl = t % 2
                ck = 64
                hs = heads(t)
                for i, j in enumerate(hs):
                    ln = slice(i * LN, (i + 1) * LN)
                    mx = jnp.full((8, LN), NEG, F32)
                    for q in range(0, lim, ck):
                        mx = jnp.maximum(mx, fold(ps_s[sl, q:q + ck, ln] + bias_s[q:q + ck, :], jnp.max))
                    mx = jnp.max(mx, axis=0, keepdims=True)
                    sm = jnp.zeros((8, LN), F32)
                    for q in range(0, lim, ck):
                        p = jnp.exp(ps_s[sl, q:q + ck, ln] + bias_s[q:q + ck, :] - mx)
                        ps_s[sl, q:q + ck, ln] = p
                        sm = sm + fold(p, jnp.sum)
                    rl = 1.0 / jnp.sum(sm, axis=0, keepdims=True)
                    for q in range(0, lim, ck):
                        pb_s[sl, q:q + ck, ln] = (ps_s[sl, q:q + ck, ln] * rl).astype(BF16)
                g0, g1 = hs[0] // GRP, hs[-1] // GRP
                o = nn(vp_s[...].reshape(KVW, CL)[g0 * HD:(g1 + 1) * HD, :lim], pb_s[sl, :lim, :len(hs) * LN])
                for i, j in enumerate(hs):
                    g, r = j // GRP, j % GRP
                    d = (r * NKV + g) * HD
                    ot_s[d:d + HD, :] = o[(g - g0) * HD:(g - g0 + 1) * HD, i * LN:(i + 1) * LN]

            scores(0)
            dqk(0)
            scores(1)
            mix(0)
            dmix(0)
            scores(2)
            dqk(1)
            mix(1)
            scores(3)
            mix(2)
            dmix(1)
            scores(4)
            mix(3)
            mix(4)
            a = jnp.concatenate([ot_s[...].T, dec_out(e0, CD)], axis=0).astype(BF16)
            x1 = round32(xc_s[c].astype(F32) + nn(a, wo_perm()))
            if c == 0:
                wait('wg', 'wu', 'wd')
            so_s[c] = mlp(x1, CR)
            if c == 0:
                @pl.when(st == 0)
                def _():
                    pl.semaphore_wait(bar, 1)

                @pl.when(st > 0)
                def _():
                    pl.semaphore_wait(bar, 2)
            hop(c).start()

        @pl.when(st == LAST)
        def _():
            for k in range(2):
                dec_scores(e0 + CD + k, kp_s[...].reshape(KVW, CL), 2 * DR + k)
            dqk(0)
            dqk(1)
            for k in range(2):
                dec_mix(c, CD + k, vp_s[...].reshape(KVW, CL), off + k * SEG + SEG - 1, 2 * DR + k)
            dmix(0)
            dmix(1)
            if c == 0:
                wait('wg', 'wu', 'wd', 'gf')
                pl.semaphore_wait(bar, 1)
            else:
                ls = [dec_out(k * ES + CD, 8)[:2] for k in range(2)]
                a = jnp.concatenate([dec_out(0, CD), dec_out(ES, CD)] + ls + [jnp.zeros((4, HID), F32)], axis=0).astype(BF16)
                xs = [xc_s[k].astype(F32) for k in range(2)]
                xf = jnp.concatenate([xs[0][CP:], xs[1][CP:]] + last_rows(xs[0]) + last_rows(xs[1]) + [jnp.zeros((4, HID), F32)], axis=0)
                x2 = mlp(round32(xf + nn(a, wo_perm())), FR)
                fh = rms(x2.astype(F32), gf_s[...].astype(F32).reshape(1, HID))
                ri = lax.broadcasted_iota(jnp.int32, (FR, FR), 0)
                src = jnp.where(ri < ND, (ri % NM) * DR + ri // NM, ri)
                fh_s[...] = nn(jnp.where(lane_iota((FR, FR)) == src, 1.0, 0.0).astype(BF16), fh).astype(BF16)
                ofh = pltpu.make_async_copy(fh_s, fh_o, out_sem.at[6])
                ofh.start()
                ofh.wait()

    for c in range(2):
        pltpu.make_async_copy(kdn_s.at[c], kdn.at[c], out_sem.at[c]).wait()
        pltpu.make_async_copy(vdn_s.at[c], vdn.at[c], out_sem.at[2 + c]).wait()
    pltpu.make_async_copy(kp_s, kpn, out_sem.at[4]).wait()
    pltpu.make_async_copy(vp_s, vpn, out_sem.at[5]).wait()

    @pl.when(st < LAST)
    def _():
        wait('gf')
        for c in range(2):
            hop(c).wait_send()


def head_kernel(fh, wh, tok, logits, fh_s, fr_s, wh_s, lsem, ssem, rsem):
    st = lax.axis_index('stage')
    lfh = pltpu.make_async_copy(fh, fh_s, lsem.at[0])
    lwh = pltpu.make_async_copy(wh, wh_s, lsem.at[1])

    @pl.when(st == LAST)
    def _():
        lfh.start()

    lwh.start()
    bar = pltpu.get_barrier_semaphore()

    def send(k):
        return pltpu.make_async_remote_copy(fh_s, fr_s, ssem.at[k], rsem, device_id={'stage': k}, device_id_type=MESH)

    def head(ref):
        lwh.wait()
        lg = nn(ref[...], wh_s[...])
        for i in range(DR + 1):
            logits[i] = lg[i * NM:(i + 1) * NM]

    @pl.when(st < LAST)
    def _():
        pl.semaphore_signal(bar, inc=1, device_id={'stage': LAST}, device_id_type=MESH)

    @pl.when(st == LAST)
    def _():
        for k in range(LAST):
            pl.semaphore_signal(bar, inc=1, device_id={'stage': k}, device_id_type=MESH)
        pl.semaphore_wait(bar, LAST)
        lfh.wait()
        for k in range(LAST):
            send(k).start()
        head(fh_s)
        for k in range(LAST):
            send(k).wait_send()

    @pl.when(st < LAST)
    def _():
        pl.semaphore_wait(bar, 1)
        send(0).wait_recv()
        head(fr_s)


def tile_start(pos):
    return pl.ds(pl.multiple_of((pos // LN) * LN, LN), LN)


def copy_all(kd, vd, ko, vo, ks, vs, ksem, vsem, edit):
    ins = [(pltpu.make_async_copy(kd.at[m], ks.at[m], ksem.at[m]), pltpu.make_async_copy(vd.at[m], vs.at[m], vsem.at[m])) for m in range(NM)]
    for a, b in ins:
        a.start()
        b.start()
    outs = []
    for m in range(NM):
        for c, scr, out, sem, w in ((ins[m][0], ks, ko, ksem, 0), (ins[m][1], vs, vo, vsem, 1)):
            c.wait()
            if edit is not None:
                edit(m, scr, w)
            o = pltpu.make_async_copy(scr.at[m], out.at[m], sem.at[m])
            o.start()
            outs.append(o)
    for o in outs:
        o.wait()


def pre_kernel(kd, vd, ko, vo, tok, ks, vs, ksem, vsem):
    st = lax.axis_index('stage')

    @pl.when(st >= 2)
    def _():
        copy_all(kd, vd, ko, vo, ks, vs, ksem, vsem, None)


def load_new(srcs, dsts, sem):
    cs = [pltpu.make_async_copy(a, b, sem.at[i]) for i, (a, b) in enumerate(zip(srcs, dsts))]
    for c in cs:
        c.start()
    return cs


def update_tiles(dlen, bk, bv, ko, vo, kpo, vpo, kt, vt, new, cs, ksem, vsem, nsem):
    lane = lane_iota((HD, LN))

    def cp(hbm, scr, sem, m, i, out):
        h = hbm.at[m, i, :, :, tile_start(dlen[m, i])]
        v = scr.at[m, i]
        return pltpu.make_async_copy(v, h, sem.at[m]) if out else pltpu.make_async_copy(h, v, sem.at[m])

    cs[4].wait()
    for m in range(NM):
        for i in range(DR):
            cp(bk, kt, ksem, m, i, False).start()
            cp(bv, vt, vsem, m, i, False).start()
    for c in cs[:4]:
        c.wait()
    po = [pltpu.make_async_copy(new[2], kpo, nsem.at[2]), pltpu.make_async_copy(new[3], vpo, nsem.at[3])]
    for o in po:
        o.start()
    for m in range(NM):
        for hbm, scr, sem, nw in ((ko, kt, ksem, new[0]), (vo, vt, vsem, new[1])):
            for i in range(DR):
                cp(hbm, scr, sem, m, i, False).wait()
            for i in range(DR):
                pos = dlen[m, i]
                for g in range(NKV):
                    col = nw[m // 2, g * HD:(g + 1) * HD, m % 2 * DR + i:m % 2 * DR + i + 1]
                    scr[m, i, g] = jnp.where(lane == pos % LN, col, scr[m, i, g].astype(F32)).astype(BF16)
            for i in range(DR):
                cp(hbm, scr, sem, m, i, True).start()
    for m in range(NM):
        for i in range(DR):
            cp(ko, kt, ksem, m, i, True).wait()
            cp(vo, vt, vsem, m, i, True).wait()
    for o in po:
        o.wait()


def mid_kernel(dlen_h, kd, vd, bk, bv, kdn, vdn, kpn, vpn, ko, vo, kpo, vpo, tok, ks, vs, kt, vt, kn_s, vn_s, kp_s, vp_s, dlen, ksem, vsem, nsem):
    st = lax.axis_index('stage')
    new = (kn_s, vn_s, kp_s, vp_s)

    @pl.when(st < 2)
    def _():
        cs = load_new((kdn, vdn, kpn, vpn, dlen_h), new + (dlen,), nsem)
        for c in cs:
            c.wait()
        po = [pltpu.make_async_copy(kp_s, kpo, nsem.at[2]), pltpu.make_async_copy(vp_s, vpo, nsem.at[3])]
        for o in po:
            o.start()
        lane = lane_iota((HD, LN))

        def edit(m, scr, w):
            for i in range(DR):
                pos = dlen[m, i]
                sl = tile_start(pos)
                for g in range(NKV):
                    col = new[w][m // 2, g * HD:(g + 1) * HD, m % 2 * DR + i:m % 2 * DR + i + 1]
                    scr[m, i, g, :, sl] = jnp.where(lane == pos % LN, col, scr[m, i, g, :, sl].astype(F32)).astype(BF16)

        copy_all(kd, vd, ko, vo, ks, vs, ksem, vsem, edit)
        for o in po:
            o.wait()

    @pl.when(st == 2)
    def _():
        cs = load_new((kdn, vdn, kpn, vpn, dlen_h), new + (dlen,), nsem)
        update_tiles(dlen, bk, bv, ko, vo, kpo, vpo, kt, vt, new, cs, ksem, vsem, nsem)


def post_kernel(dlen_h, kdn, vdn, kpn, vpn, lg, bk, bv, bkp, bvp, ko, vo, kpo, vpo, kt, vt, kn_s, vn_s, kp_s, vp_s, dlen, ksem, vsem, nsem):
    st = lax.axis_index('stage')

    @pl.when(st == LAST)
    def _():
        new = (kn_s, vn_s, kp_s, vp_s)
        cs = load_new((kdn, vdn, kpn, vpn, dlen_h), new + (dlen,), nsem)
        update_tiles(dlen, bk, bv, ko, vo, kpo, vpo, kt, vt, new, cs, ksem, vsem, nsem)


ANY = pl.BlockSpec(memory_space=pltpu.HBM)


def solution(mesh):
    part = P('replica')
    layer = P('stage')
    cache = P('stage', 'replica')
    in_specs = (part,) * 4 + (layer,) * 9 + (P(), P()) + (cache,) * 4
    out_specs = (part,) + (cache,) * 4
    inv_freq = np.float32(ROPE_BASE) ** (-np.arange(HALF, dtype=np.float32) * np.float32(2.0 / HD))
    ifr_c = np.broadcast_to(inv_freq[:, None], (HALF, NP)).astype(np.float32)

    def device_fn(x_dec, x_pre, dec_len, pre_len, g_attn, w_q, w_k, w_v, w_o, g_mlp, w_gate, w_up, w_down, g_final, w_head, k_dec, v_dec, k_pre, v_pre):
        kd = jnp.transpose(k_dec[0], (0, 1, 3, 4, 2))
        vd = jnp.transpose(v_dec[0], (0, 1, 3, 4, 2))
        kp = jnp.transpose(k_pre[0], (1, 2, 0))
        vp = jnp.transpose(v_pre[0], (1, 2, 0))
        args = (x_dec.reshape(ND, HID), x_pre.reshape(NP, HID), dec_len, pre_len, g_attn, w_q[0], w_k[0].T, w_v[0].T, w_o[0], g_mlp,
                w_gate[0], w_up[0], w_down[0].T, g_final, kd, vd, kp, vp, jnp.asarray(ifr_c))
        vm = lambda shape, dt: pltpu.VMEM(shape, dt)
        scratch = [
            vm((2, CR, HID), BF16), pltpu.SMEM((NM, DR), jnp.int32), pltpu.SMEM((1,), jnp.int32), vm((1, HID), BF16),
            vm((HID, HID), BF16), vm((HID + 2 * KVW, HID), BF16), vm((HID, HID), BF16), vm((1, HID), BF16),
            vm((HID, FFN), BF16), vm((HID, FFN), BF16), vm((HID, FFN), BF16), vm((HID,), BF16),
            vm(kd.shape, BF16), vm(vd.shape, BF16), vm(kp.shape, BF16), vm(vp.shape, BF16), vm((HALF, 2 * LN), F32),
            vm((2, HALF, 2 * LN), F32), vm((2, HALF, 2 * LN), F32), vm((HID, LN), BF16),
            vm((2 * ES * 8, LN), F32), vm((2 * ES * 8, LN), F32), vm((2, 24, LN), F32), vm((2 * ES, KVW), F32),
            vm((2 * ES * 8, LN), F32), vm((2 * ES * 8, LN), F32),
            vm((2, KVW, LN), F32), vm((2, KVW, LN), F32), vm(((2 * DR + 2) * 24, CL), F32), vm((2, CL, 2 * LN), F32), vm((2, CL, 2 * LN), BF16),
            vm((CL, LN), F32), vm((HID, LN), F32), vm((CR, FFN), BF16), vm((2, CR, HID), BF16), vm((FR, HID), BF16),
            pltpu.SemaphoreType.DMA((19,)), pltpu.SemaphoreType.DMA((NM,)), pltpu.SemaphoreType.DMA((NM,)), pltpu.SemaphoreType.DMA((7,)),
            pltpu.SemaphoreType.DMA((2,)), pltpu.SemaphoreType.DMA((2,)),
        ]
        sds = jax.ShapeDtypeStruct
        big = pltpu.CompilerParams(vmem_limit_bytes=62 * 1024 * 1024)
        cshape = sds(kd.shape, BF16)
        pshape = sds(kp.shape, BF16)
        nsems = [pltpu.SemaphoreType.DMA((NM,)), pltpu.SemaphoreType.DMA((NM,))]
        tile = vm((NM, DR, NKV, HD, LN), BF16)
        news = [vm((2, KVW, LN), F32), vm((2, KVW, LN), F32), vm(kp.shape, BF16), vm(vp.shape, BF16), pltpu.SMEM((NM, DR), jnp.int32)]
        vmem = pl.BlockSpec(memory_space=pltpu.VMEM)
        tshape = sds((8, LN), F32)
        bk, bv, tok = pl.pallas_call(
            pre_kernel, out_shape=(cshape, cshape, tshape), in_specs=[ANY, ANY], out_specs=(ANY, ANY, ANY),
            scratch_shapes=[vm(kd.shape, BF16), vm(vd.shape, BF16)] + nsems, name='pre', compiler_params=big)(kd, vd)
        args = args + (tok,)
        kdn, vdn, kpn, vpn, fh = pl.pallas_call(
            pipe_kernel,
            out_shape=(sds((2, KVW, LN), F32), sds((2, KVW, LN), F32), pshape, pshape, sds((ND + 8, HID), BF16)),
            in_specs=[ANY] * len(args),
            out_specs=(ANY,) * 5,
            scratch_shapes=scratch,
            name='pipe',
            compiler_params=pltpu.CompilerParams(collective_id=0, has_side_effects=True, vmem_limit_bytes=62 * 1024 * 1024),
        )(*args)
        bk, bv, bkp, bvp, tok2 = pl.pallas_call(
            mid_kernel, out_shape=(cshape, cshape, pshape, pshape, tshape), in_specs=[ANY] * 9, out_specs=(ANY,) * 5,
            input_output_aliases={3: 0, 4: 1},
            scratch_shapes=[vm(kd.shape, BF16), vm(vd.shape, BF16), tile, tile] + news + nsems + [pltpu.SemaphoreType.DMA((5,))],
            name='mid', compiler_params=big)(dec_len, kd, vd, bk, bv, kdn, vdn, kpn, vpn)
        logits = pl.pallas_call(
            head_kernel, out_shape=sds((DR + 1, NM, VOC), F32), in_specs=[ANY] * 3, out_specs=vmem,
            scratch_shapes=[vm((ND + 8, HID), BF16), vm((ND + 8, HID), BF16), vm((HID, VOC), BF16),
                            pltpu.SemaphoreType.DMA((2,)), pltpu.SemaphoreType.DMA((LAST,)), pltpu.SemaphoreType.DMA],
            name='head', compiler_params=pltpu.CompilerParams(collective_id=1, has_side_effects=True))(fh, w_head, tok2)
        ko, vo, kpo, vpo = pl.pallas_call(
            post_kernel, out_shape=(cshape, cshape, pshape, pshape), in_specs=[ANY] * 10, out_specs=(ANY,) * 4,
            input_output_aliases={6: 0, 7: 1, 8: 2, 9: 3},
            scratch_shapes=[tile, tile] + news + nsems + [pltpu.SemaphoreType.DMA((5,))],
            name='post', compiler_params=big)(dec_len, kdn, vdn, kpn, vpn, logits, bk, bv, bkp, bvp)
        back = lambda a: jnp.transpose(a, (0, 1, 4, 2, 3))[None]
        backp = lambda a: jnp.transpose(a, (2, 0, 1))[None]
        return jnp.transpose(logits, (1, 0, 2)), back(ko), back(vo), backp(kpo), backp(vpo)

    return jax.shard_map(device_fn, mesh=mesh, in_specs=in_specs, out_specs=out_specs, check_vma=False)
```

time: 65.1 us -> 47.5 us (0.73)
  Pallas kernels: 61.7 us -> 45.3 us
  local copies, waits for them, and re-layouts: 1.93 us -> 0.67 us
    pallas_call x1, Pallas kernels: 41.6 us -> 28.4 us  [device_fn(): pl.pallas_call(pipe_kernel, out_shape=(sds((2, KVW, LN), F32), sds((2, KV...]
    pallas_call x1, Pallas kernels: 1.6 us -> 0.14 us  [device_fn(): pl.pallas_call(mid_kernel, out_shape=(cshape, cshape, pshape, pshape, tsh...]
    reshape x1 -> x0, local copies, waits for them, and re-layouts: 1.26 us -> none  [device_fn(): g_final.reshape(1, HID)]
    pallas_call x1, Pallas kernels: 5.37 us -> 4.31 us  [device_fn(): pl.pallas_call(post_kernel, out_shape=(cshape, cshape, pshape, pshape), i...]
where the time goes in v4:
time: 47.5 us; the launch traced here: 47.3 us
  Pallas kernels  45.3 us (95%)
  between operations  1.33 us (3%)
  local copies, waits for them, and re-layouts  0.67 us (1%)
    pallas_call x1, Pallas kernels, device_fn(): pl.pallas_call(pipe_kernel, out_shape=(sds((2, KVW, LN), F32), sds((2, KV...  28.4 us
    pallas_call x1, Pallas kernels, device_fn(): pl.pallas_call(pre_kernel, out_shape=(cshape, cshape, tshape), in_specs=[...  9.26 us
    pallas_call x1, Pallas kernels, device_fn(): pl.pallas_call(post_kernel, out_shape=(cshape, cshape, pshape, pshape), i...  4.31 us
    pallas_call x1, Pallas kernels, device_fn(): pl.pallas_call(head_kernel, out_shape=sds((DR + 1, NM, VOC), F32), in_spe...  3.2 us

profile of v4, /device:TPU:7, one launch (start us, length us, event | category | flops | bytes accessed | tf_op | source)
XLA Modules:
  0.0 47.3 jit_solution(123029057266692883)
XLA Ops:
  1.3 9.3 %pre.1 = (bf16[4,8,3,64,512]{4,3,2,1,0:T(8,128)(2,1)}, bf16[4,8,3,64,512]{4,3,2,1,0:T(8,128)(2,1)}, f32[8,128]{1,0:T(8,128)}) custom-call(bf16[4,8,3,64,512]{4,3,2,1,0:T(8,128)(2,1)} %bitcast.40, bf16[4,8,3,64,512]{4,3,2,1,0:T(8,128)(2,1)} %bitcast.43), custom_call_target="tpu_custom_call" | custom-call | tf_op jit(solution)/shard_map/pre/pallas_call | solution.py:581
  10.5 28.4 %pipe.1 = (f32[2,192,128]{2,1,0:T(8,128)}, f32[2,192,128]{2,1,0:T(8,128)}, bf16[3,64,512]{2,1,0:T(8,128)(2,1)}, bf16[3,64,512]{2,1,0:T(8,128)(2,1)}, bf16[40,576]{1,0:T(8,128)(2,1)}) custom-call(bf16[32,576]{1,0:T(8,128)(2,1)} %bitcast.61, bf16[256,576]{1,0:T(8,128)(2,1)} %bitcast.54, s32[4,8]{1,0:T(4,128)} %dlen_h.3, s32[1]{0:T(128)S(6)} %copy.38.plen, ...), custom_call_target="tpu_custom_call" | custom-call | tf_op jit(solution)/shard_map/pipe/pallas_call | solution.py:585
  39.0 0.1 mid.1
  39.1 3.2 %head.1.lg = f32[9,4,1024]{2,1,0:T(4,128)} custom-call(bf16[40,576]{1,0:T(8,128)(2,1)} %get-tuple-element.23.fh, bf16[576,1024]{1,0:T(8,128)(2,1)} %wh.1, f32[8,128]{1,0:T(8,128)} %get-tuple-element.30.tok), custom_call_target="tpu_custom_call" | custom-call | tf_op jit(solution)/shard_map/head/pallas_call | solution.py:599
  42.3 0.0 copy-start
  42.3 4.3 %post.1 = (bf16[4,8,3,64,512]{4,3,2,1,0:T(8,128)(2,1)}, bf16[4,8,3,64,512]{4,3,2,1,0:T(8,128)(2,1)}, bf16[3,64,512]{2,1,0:T(8,128)(2,1)}, bf16[3,64,512]{2,1,0:T(8,128)(2,1)}) custom-call(s32[4,8]{1,0:T(4,128)} %dlen_h.3, f32[2,192,128]{2,1,0:T(8,128)} %get-tuple-element.26.kdn, ...), custom_call_target="tpu_custom_call", output_to_operand_aliasing={{0}: (6, {}), {1}: (7, {}), {2}: (8, {}), {3}: (9, {})} | custom-call | tf_op jit(solution)/shard_map/post/pallas_call | solution.py:604
  46.7 0.0 copy-done
  46.7 0.7 %copy.39 = f32[4,9,1024]{2,0,1:T(4,128)} copy(f32[4,9,1024]{2,0,1:T(4,128)S(1)} %bitcast.51) | data formatting | bytes 294912
Async XLA Ops:
  42.3 4.3 %copy-start = (f32[9,4,1024]{2,1,0:T(4,128)S(1)}, f32[9,4,1024]{2,1,0:T(4,128)}, u32[]{:S(2)}) copy-start(f32[9,4,1024]{2,1,0:T(4,128)} %head.1.lg) | copy-start | bytes 442372

commit v5 on v4

--- a/solution.py
+++ b/solution.py
@@ -67,7 +67,7 @@
 
 def pipe_kernel(xd, xp, dlen, plen, ga, wq, wk, wv, wo, gm, wg, wu, wd, gf, kd, vd, kp, vp, ifr, tok,
                 kdn, vdn, kpn, vpn, fh_o,
-                xc_s, dl_s, pl_s, ga_s, wq_s, w3_s, wo_s, gm_s, wg_s, wu_s, wd_s, gf_s,
+                xc_s, dl_s, pl_s, ga_s, wq_s, w3_s, wo_s, gm_s, wg_s, wu_s, wd_s, wdt_s, gf_s,
                 kd_s, vd_s, kp_s, vp_s, ifr_s,
                 cos_s, sin_s, qt_s, qa_s, qb_s, self_s, vn_s, oa_s, ob_s,
                 kdn_s, vdn_s, sc_s, ps_s, pb_s, bias_s, ot_s, act_s, so_s, fh_s,
@@ -129,9 +129,21 @@
         kcp[m].start()
         vcp[m].start()
     start('wo', 'gm')
+
+    @pl.when(st > 0)
+    def _():
+        start('wg', 'wu', 'wd', 'gf')
+
     wait('ga', 'wq')
     w3_s[:HID, :] = wq_s[...].astype(F32).T.astype(BF16)
     wait('wk', 'wv')
+
+    @pl.when(st > 0)
+    def _():
+        wait('wd')
+        for k in range(0, FFN, LN):
+            wdt_s[k:k + LN, :] = wd_s[:, k:k + LN].astype(F32).T.astype(BF16)
+
     gat = ga_s[...].astype(F32)
 
     lgrp = lane_iota((8, KVW)) // HD
@@ -164,14 +176,14 @@
     def wo_perm():
         return jnp.concatenate([wo_s[(g * GRP + r) * HD:(g * GRP + r + 1) * HD, :] for r in range(GRP) for g in range(NKV)], axis=0)
 
-    def mlp(x, rows):
+    def mlp(x, rows, put):
         h2 = rms(x, gm_s[...].astype(F32))
         step = 512
         for c in range(FFN // step):
             gt = nn(h2, wg_s[:, c * step:(c + 1) * step])
             up = nn(h2, wu_s[:, c * step:(c + 1) * step])
             act_s[:rows, c * step:(c + 1) * step] = (gt * (1.0 / (1.0 + jnp.exp(-gt))) * up).astype(BF16)
-        return (x + nt(act_s[:rows, :], wd_s[...])).astype(BF16)
+        put(x, rows)
 
     def round32(x):
         return x.astype(BF16).astype(F32)
@@ -194,75 +206,94 @@
         def _():
             hop(c).wait_recv()
 
-        x = xc_s[c].astype(F32)
-        h = x * lax.rsqrt(jnp.mean(x * x, axis=-1, keepdims=True) + NORM_EPS) * gat
-        h = jnp.concatenate([h] + last_rows(h) + [jnp.zeros((2 * LN - CR - 2, HID), F32)], axis=0).astype(BF16)
-        qkv = nt(w3_s[...], h)
-        cos, sin = cos_s[c], sin_s[c]
-        qt = round32(rope_t(qkv[:HID], cos, sin)) * (HD ** -0.5)
-        kt = round32(rope_t(qkv[HID:HID + KVW], cos, sin))
-        vt = round32(qkv[HID + KVW:])
-        qt_s[...] = qt[:, :LN].astype(BF16)
-        qe, ke, ve = qt[:, LN:], kt[:, LN:], vt[:, LN:]
-        row = lax.broadcasted_iota(jnp.int32, (24, LN), 0)
-        sf = jnp.zeros((24, LN), F32)
-        for g in range(NKV):
-            for r in range(GRP):
-                j = g * GRP + r
-                v = jnp.sum(qe[j * HD:(j + 1) * HD] * ke[g * HD:(g + 1) * HD], axis=0, keepdims=True)
-                sf = jnp.where(row == 8 * g + r, v, sf)
-        self_s[c] = sf
-        n = CD + 8
-        e0 = c * ES
-        pad = jnp.zeros((HD, LN), F32)
-        for r in range(GRP):
-            qr = [qe[(g * GRP + r) * HD:(g * GRP + r + 1) * HD] for g in range(NKV)]
-            qa_s[pl.ds(e0 * 8 + r, n, stride=8), :] = jnp.concatenate(qr[:2], axis=0).T[:n]
-            qb_s[pl.ds(e0 * 8 + r, n, stride=8), :] = jnp.concatenate([qr[2], pad], axis=0).T[:n]
-        vn_s[e0:e0 + n, :LN] = ve[:LN].T[:n]
-        vn_s[e0:e0 + n, LN:] = jnp.concatenate([ve[LN:], pad], axis=0).T[:n, :HD]
-        kdn_s[c] = ke
-        vdn_s[c] = ve
-        pltpu.make_async_copy(kdn_s.at[c], kdn.at[c], out_sem.at[c]).start()
-        pltpu.make_async_copy(vdn_s.at[c], vdn.at[c], out_sem.at[2 + c]).start()
-
         if c == 0:
             wait('kp', 'vp')
-            start('wg', 'wu', 'wd', 'gf')
-        off = p0 + c * CP
-        place = jnp.where(lax.broadcasted_iota(jnp.int32, (CP, CL), 0) + off == lane_iota((CP, CL)), 1.0, 0.0).astype(BF16)
-        lp = lane_iota((KVW, CL)) - off
-        fresh = (lp >= 0) & (lp < CP)
-        kpu = jnp.where(fresh, nn(kt[:, :LN].astype(BF16), place), kp_s[...].reshape(KVW, CL).astype(F32))
-        vpu = jnp.where(fresh, nn(vt[:, :LN].astype(BF16), place), vp_s[...].reshape(KVW, CL).astype(F32))
-        kp_s[...] = kpu.astype(BF16).reshape(NKV, HD, CL)
-        vp_s[...] = vpu.astype(BF16).reshape(NKV, HD, CL)
-        if c == 1:
-            pltpu.make_async_copy(kp_s, kpn, out_sem.at[4]).start()
-            pltpu.make_async_copy(vp_s, vpn, out_sem.at[5]).start()
-
-        for m in (2 * c, 2 * c + 1):
-            kcp[m].wait()
-            vcp[m].wait()
-        if c == 0:
+
             @pl.when(st == 0)
             def _():
-                start('p1', 'd1')
+                start('wg', 'wu', 'wd', 'gf')
+        else:
             for m in (2, 3):
-                kcp[m].start()
-                vcp[m].start()
-            wait('wo', 'gm')
+                kcp[m].wait()
+                vcp[m].wait()
+        off = p0 + c * CP
+        e0 = c * ES
+
+        def project():
+            x = xc_s[c].astype(F32)
+            h = x * lax.rsqrt(jnp.mean(x * x, axis=-1, keepdims=True) + NORM_EPS) * gat
+            h = jnp.concatenate([h] + last_rows(h) + [jnp.zeros((2 * LN - CR - 2, HID), F32)], axis=0).astype(BF16)
+            half = (HID + 2 * KVW) // 2
+            qkv = jnp.concatenate([nt(w3_s[:half, :], h), nt(w3_s[half:, :], h)], axis=0)
+            cos, sin = cos_s[c], sin_s[c]
+            qt = round32(rope_t(qkv[:HID], cos, sin)) * (HD ** -0.5)
+            kt = round32(rope_t(qkv[HID:HID + KVW], cos, sin))
+            vt = round32(qkv[HID + KVW:])
+            qt_s[...] = qt[:, :LN].astype(BF16)
+            qe, ke, ve = qt[:, LN:], kt[:, LN:], vt[:, LN:]
+            row = lax.broadcasted_iota(jnp.int32, (24, LN), 0)
+            sf = jnp.zeros((24, LN), F32)
+            for g in range(NKV):
+                for r in range(GRP):
+                    j = g * GRP + r
+                    v = jnp.sum(qe[j * HD:(j + 1) * HD] * ke[g * HD:(g + 1) * HD], axis=0, keepdims=True)
+                    sf = jnp.where(row == 8 * g + r, v, sf)
+            self_s[c] = sf
+            n = CD + 8
+            pad = jnp.zeros((HD, LN), F32)
+            for r in range(GRP):
+                qr = [qe[(g * GRP + r) * HD:(g * GRP + r + 1) * HD] for g in range(NKV)]
+                qa_s[pl.ds(e0 * 8 + r, n, stride=8), :] = jnp.concatenate(qr[:2], axis=0).T[:n]
+                qb_s[pl.ds(e0 * 8 + r, n, stride=8), :] = jnp.concatenate([qr[2], pad], axis=0).T[:n]
+            vn_s[e0:e0 + n, :LN] = ve[:LN].T[:n]
+            vn_s[e0:e0 + n, LN:] = jnp.concatenate([ve[LN:], pad], axis=0).T[:n, :HD]
+            kdn_s[c] = ke
+            vdn_s[c] = ve
+            pltpu.make_async_copy(kdn_s.at[c], kdn.at[c], out_sem.at[c]).start()
+            pltpu.make_async_copy(vdn_s.at[c], vdn.at[c], out_sem.at[2 + c]).start()
+            return kt, vt
+
+        def put_prompt(kt, vt):
+            place = jnp.where(lax.broadcasted_iota(jnp.int32, (CP, CL), 0) + off == lane_iota((CP, CL)), 1.0, 0.0).astype(BF16)
+            lp = lane_iota((KVW, CL)) - off
+            fresh = (lp >= 0) & (lp < CP)
+            kpu = jnp.where(fresh, nn(kt[:, :LN].astype(BF16), place), kp_s[...].reshape(KVW, CL).astype(F32))
+            vpu = jnp.where(fresh, nn(vt[:, :LN].astype(BF16), place), vp_s[...].reshape(KVW, CL).astype(F32))
+            kp_s[...] = kpu.astype(BF16).reshape(NKV, HD, CL)
+            vp_s[...] = vpu.astype(BF16).reshape(NKV, HD, CL)
+            if c == 1:
+                pltpu.make_async_copy(kp_s, kpn, out_sem.at[4]).start()
+                pltpu.make_async_copy(vp_s, vpn, out_sem.at[5]).start()
+            return kpu
+
+        def loads():
+            if c == 0:
+                for m in (0, 1):
+                    kcp[m].wait()
+                    vcp[m].wait()
+
+                @pl.when(st == 0)
+                def _():
+                    start('p1', 'd1')
+                for m in (2, 3):
+                    kcp[m].start()
+                    vcp[m].start()
+                wait('wo', 'gm')
 
         def dqk(i):
             for k in range(DR):
                 dec_scores(c * ES + i * DR + k, kd_s[2 * c + i, k].reshape(KVW, CL), i * DR + k)
 
-        def dmix(i):
-            for k in range(DR):
-                dec_mix(c, i * DR + k, vd_s[2 * c + i, k].reshape(KVW, CL), dl_s[2 * c + i, k], i * DR + k)
+        def dmix(q):
+            for k in range(4 * q, 4 * q + 4):
+                m, i = 2 * c + k // DR, k % DR
+                dec_mix(c, k, vd_s[m, i].reshape(KVW, CL), dl_s[m, i], k)
 
         @pl.when(st < LAST)
         def _():
+            kt, vt = project()
+            loads()
+            kpu = put_prompt(kt, vt)
             kfull = kpu[:, :lim].T.astype(BF16)
             bias_s[:lim, :] = jnp.where(lax.broadcasted_iota(jnp.int32, (lim, LN), 0) <= lane_iota((lim, LN)) + off, 0.0, NEG)
 
@@ -277,7 +308,9 @@
                     parts += [jnp.zeros(((NKV - 1 - g) * HD, LN), BF16)] * (g < NKV - 1)
                     cols.append(jnp.concatenate(parts, axis=0))
                 w = len(cols) * LN
-                ps_s[t % 2, :lim, :w] = nn(kfull, jnp.concatenate(cols, axis=1))
+                rhs = jnp.concatenate(cols, axis=1)
+                for q in range(0, lim, lim // 2):
+                    ps_s[t % 2, q:q + lim // 2, :w] = nn(kfull[q:q + lim // 2], rhs)
 
             def fold(v, op):
                 return op(v.reshape(v.shape[0] // 8, 8, v.shape[1]), axis=0)
@@ -307,25 +340,41 @@
                     d = (r * NKV + g) * HD
                     ot_s[d:d + HD, :] = o[(g - g0) * HD:(g - g0 + 1) * HD, i * LN:(i + 1) * LN]
 
+            dqk(0)
             scores(0)
-            dqk(0)
             scores(1)
+            dmix(0)
             mix(0)
-            dmix(0)
             scores(2)
+            dmix(1)
+            mix(1)
             dqk(1)
-            mix(1)
             scores(3)
+            dmix(2)
             mix(2)
-            dmix(1)
             scores(4)
+            dmix(3)
             mix(3)
             mix(4)
             a = jnp.concatenate([ot_s[...].T, dec_out(e0, CD)], axis=0).astype(BF16)
             x1 = round32(xc_s[c].astype(F32) + nn(a, wo_perm()))
             if c == 0:
-                wait('wg', 'wu', 'wd')
-            so_s[c] = mlp(x1, CR)
+                wait('wg', 'wu')
+
+                @pl.when(st == 0)
+                def _():
+                    wait('wd')
+
+            def put(x, rows):
+                @pl.when(st == 0)
+                def _():
+                    so_s[c] = (x + nt(act_s[...], wd_s[...])).astype(BF16)
+
+                @pl.when(st > 0)
+                def _():
+                    so_s[c] = (x + nn(act_s[...], wdt_s[...])).astype(BF16)
+
+            mlp(x1, CR, put)
             if c == 0:
                 @pl.when(st == 0)
                 def _():
@@ -338,27 +387,34 @@
 
         @pl.when(st == LAST)
         def _():
+            kt, vt = project()
+            loads()
+            put_prompt(kt, vt)
             for k in range(2):
                 dec_scores(e0 + CD + k, kp_s[...].reshape(KVW, CL), 2 * DR + k)
             dqk(0)
             dqk(1)
             for k in range(2):
                 dec_mix(c, CD + k, vp_s[...].reshape(KVW, CL), off + k * SEG + SEG - 1, 2 * DR + k)
-            dmix(0)
-            dmix(1)
+            for q in range(4):
+                dmix(q)
             if c == 0:
-                wait('wg', 'wu', 'wd', 'gf')
+                wait('wg', 'wu', 'gf')
                 pl.semaphore_wait(bar, 1)
             else:
                 ls = [dec_out(k * ES + CD, 8)[:2] for k in range(2)]
                 a = jnp.concatenate([dec_out(0, CD), dec_out(ES, CD)] + ls + [jnp.zeros((4, HID), F32)], axis=0).astype(BF16)
                 xs = [xc_s[k].astype(F32) for k in range(2)]
                 xf = jnp.concatenate([xs[0][CP:], xs[1][CP:]] + last_rows(xs[0]) + last_rows(xs[1]) + [jnp.zeros((4, HID), F32)], axis=0)
-                x2 = mlp(round32(xf + nn(a, wo_perm())), FR)
-                fh = rms(x2.astype(F32), gf_s[...].astype(F32).reshape(1, HID))
-                ri = lax.broadcasted_iota(jnp.int32, (FR, FR), 0)
-                src = jnp.where(ri < ND, (ri % NM) * DR + ri // NM, ri)
-                fh_s[...] = nn(jnp.where(lane_iota((FR, FR)) == src, 1.0, 0.0).astype(BF16), fh).astype(BF16)
+
+                def put(x, rows):
+                    x2 = round32(x + nn(act_s[:rows, :], wdt_s[...]))
+                    fh = rms(x2, gf_s[...].astype(F32).reshape(1, HID))
+                    ri = lax.broadcasted_iota(jnp.int32, (FR, FR), 0)
+                    src = jnp.where(ri < ND, (ri % NM) * DR + ri // NM, ri)
+                    fh_s[...] = nn(jnp.where(lane_iota((FR, FR)) == src, 1.0, 0.0).astype(BF16), fh).astype(BF16)
+
+                mlp(round32(xf + nn(a, wo_perm())), FR, put)
                 ofh = pltpu.make_async_copy(fh_s, fh_o, out_sem.at[6])
                 ofh.start()
                 ofh.wait()
@@ -376,40 +432,28 @@
             hop(c).wait_send()
 
 
-def head_kernel(fh, wh, tok, logits, fh_s, fr_s, wh_s, lsem, ssem, rsem):
+def head_kernel(fh, tok, fo, fh_s, fr_s, lsem, ssem, rsem):
     st = lax.axis_index('stage')
-    lfh = pltpu.make_async_copy(fh, fh_s, lsem.at[0])
-    lwh = pltpu.make_async_copy(wh, wh_s, lsem.at[1])
-
-    @pl.when(st == LAST)
-    def _():
-        lfh.start()
-
-    lwh.start()
+    lfh = pltpu.make_async_copy(fh, fh_s, lsem)
     bar = pltpu.get_barrier_semaphore()
 
     def send(k):
         return pltpu.make_async_remote_copy(fh_s, fr_s, ssem.at[k], rsem, device_id={'stage': k}, device_id_type=MESH)
 
-    def head(ref):
-        lwh.wait()
-        lg = nn(ref[...], wh_s[...])
-        for i in range(DR + 1):
-            logits[i] = lg[i * NM:(i + 1) * NM]
-
     @pl.when(st < LAST)
     def _():
         pl.semaphore_signal(bar, inc=1, device_id={'stage': LAST}, device_id_type=MESH)
 
     @pl.when(st == LAST)
     def _():
+        lfh.start()
         for k in range(LAST):
             pl.semaphore_signal(bar, inc=1, device_id={'stage': k}, device_id_type=MESH)
         pl.semaphore_wait(bar, LAST)
         lfh.wait()
         for k in range(LAST):
             send(k).start()
-        head(fh_s)
+        fo[...] = fh_s[...]
         for k in range(LAST):
             send(k).wait_send()
 
@@ -417,7 +461,7 @@
     def _():
         pl.semaphore_wait(bar, 1)
         send(0).wait_recv()
-        head(fr_s)
+        fo[...] = fr_s[...]
 
 
 def tile_start(pos):
@@ -457,7 +501,7 @@
     return cs
 
 
-def update_tiles(dlen, bk, bv, ko, vo, kpo, vpo, kt, vt, new, cs, ksem, vsem, nsem):
+def update_tiles(dlen, bk, bv, ko, vo, kpo, vpo, kt, vt, new, cs, ksem, vsem, nsem, extra=None):
     lane = lane_iota((HD, LN))
 
     def cp(hbm, scr, sem, m, i, out):
@@ -475,6 +519,8 @@
     po = [pltpu.make_async_copy(new[2], kpo, nsem.at[2]), pltpu.make_async_copy(new[3], vpo, nsem.at[3])]
     for o in po:
         o.start()
+    if extra is not None:
+        extra()
     for m in range(NM):
         for hbm, scr, sem, nw in ((ko, kt, ksem, new[0]), (vo, vt, vsem, new[1])):
             for i in range(DR):
@@ -526,14 +572,32 @@
         update_tiles(dlen, bk, bv, ko, vo, kpo, vpo, kt, vt, new, cs, ksem, vsem, nsem)
 
 
-def post_kernel(dlen_h, kdn, vdn, kpn, vpn, lg, bk, bv, bkp, bvp, ko, vo, kpo, vpo, kt, vt, kn_s, vn_s, kp_s, vp_s, dlen, ksem, vsem, nsem):
+def post_kernel(dlen_h, kdn, vdn, kpn, vpn, fr, wh, bk, bv, bkp, bvp, ko, vo, kpo, vpo, logits,
+                kt, vt, fr_s, wh_s, kn_s, vn_s, kp_s, vp_s, dlen, ksem, vsem, nsem, hsem):
     st = lax.axis_index('stage')
+    lf = pltpu.make_async_copy(fr, fr_s, hsem.at[0])
+    lw = pltpu.make_async_copy(wh, wh_s, hsem.at[1])
+
+    def head():
+        lf.wait()
+        lw.wait()
+        lg = nn(fr_s[...], wh_s[...])
+        for i in range(DR + 1):
+            logits[i] = lg[i * NM:(i + 1) * NM]
 
     @pl.when(st == LAST)
     def _():
         new = (kn_s, vn_s, kp_s, vp_s)
         cs = load_new((kdn, vdn, kpn, vpn, dlen_h), new + (dlen,), nsem)
-        update_tiles(dlen, bk, bv, ko, vo, kpo, vpo, kt, vt, new, cs, ksem, vsem, nsem)
+        lf.start()
+        lw.start()
+        update_tiles(dlen, bk, bv, ko, vo, kpo, vpo, kt, vt, new, cs, ksem, vsem, nsem, head)
+
+    @pl.when(st < LAST)
+    def _():
+        lf.start()
+        lw.start()
+        head()
 
 
 ANY = pl.BlockSpec(memory_space=pltpu.HBM)
@@ -559,7 +623,7 @@
         scratch = [
             vm((2, CR, HID), BF16), pltpu.SMEM((NM, DR), jnp.int32), pltpu.SMEM((1,), jnp.int32), vm((1, HID), BF16),
             vm((HID, HID), BF16), vm((HID + 2 * KVW, HID), BF16), vm((HID, HID), BF16), vm((1, HID), BF16),
-            vm((HID, FFN), BF16), vm((HID, FFN), BF16), vm((HID, FFN), BF16), vm((HID,), BF16),
+            vm((HID, FFN), BF16), vm((HID, FFN), BF16), vm((HID, FFN), BF16), vm((FFN, HID), BF16), vm((HID,), BF16),
             vm(kd.shape, BF16), vm(vd.shape, BF16), vm(kp.shape, BF16), vm(vp.shape, BF16), vm((HALF, 2 * LN), F32),
             vm((2, HALF, 2 * LN), F32), vm((2, HALF, 2 * LN), F32), vm((HID, LN), BF16),
             vm((2 * ES * 8, LN), F32), vm((2 * ES * 8, LN), F32), vm((2, 24, LN), F32), vm((2 * ES, KVW), F32),
@@ -596,16 +660,16 @@
             input_output_aliases={3: 0, 4: 1},
             scratch_shapes=[vm(kd.shape, BF16), vm(vd.shape, BF16), tile, tile] + news + nsems + [pltpu.SemaphoreType.DMA((5,))],
             name='mid', compiler_params=big)(dec_len, kd, vd, bk, bv, kdn, vdn, kpn, vpn)
-        logits = pl.pallas_call(
-            head_kernel, out_shape=sds((DR + 1, NM, VOC), F32), in_specs=[ANY] * 3, out_specs=vmem,
-            scratch_shapes=[vm((ND + 8, HID), BF16), vm((ND + 8, HID), BF16), vm((HID, VOC), BF16),
-                            pltpu.SemaphoreType.DMA((2,)), pltpu.SemaphoreType.DMA((LAST,)), pltpu.SemaphoreType.DMA],
-            name='head', compiler_params=pltpu.CompilerParams(collective_id=1, has_side_effects=True))(fh, w_head, tok2)
-        ko, vo, kpo, vpo = pl.pallas_call(
-            post_kernel, out_shape=(cshape, cshape, pshape, pshape), in_specs=[ANY] * 10, out_specs=(ANY,) * 4,
-            input_output_aliases={6: 0, 7: 1, 8: 2, 9: 3},
-            scratch_shapes=[tile, tile] + news + nsems + [pltpu.SemaphoreType.DMA((5,))],
-            name='post', compiler_params=big)(dec_len, kdn, vdn, kpn, vpn, logits, bk, bv, bkp, bvp)
+        fr = pl.pallas_call(
+            head_kernel, out_shape=sds((FR, HID), BF16), in_specs=[ANY] * 2, out_specs=vmem,
+            scratch_shapes=[vm((FR, HID), BF16), vm((FR, HID), BF16),
+                            pltpu.SemaphoreType.DMA, pltpu.SemaphoreType.DMA((LAST,)), pltpu.SemaphoreType.DMA],
+            name='head', compiler_params=pltpu.CompilerParams(collective_id=1, has_side_effects=True))(fh, tok2)
+        ko, vo, kpo, vpo, logits = pl.pallas_call(
+            post_kernel, out_shape=(cshape, cshape, pshape, pshape, sds((DR + 1, NM, VOC), F32)), in_specs=[ANY] * 11,
+            out_specs=(ANY,) * 4 + (vmem,), input_output_aliases={7: 0, 8: 1, 9: 2, 10: 3},
+            scratch_shapes=[tile, tile, vm((FR, HID), BF16), vm((HID, VOC), BF16)] + news + nsems + [pltpu.SemaphoreType.DMA((5,)), pltpu.SemaphoreType.DMA((2,))],
+            name='post', compiler_params=big)(dec_len, kdn, vdn, kpn, vpn, fr, w_head, bk, bv, bkp, bvp)
         back = lambda a: jnp.transpose(a, (0, 1, 4, 2, 3))[None]
         backp = lambda a: jnp.transpose(a, (2, 0, 1))[None]
         return jnp.transpose(logits, (1, 0, 2)), back(ko), back(vo), backp(kpo), backp(vpo)

time: 47.5 us -> 46.1 us (0.971)
  Pallas kernels: 45.3 us -> 44.4 us
  local copies, waits for them, and re-layouts: 0.67 us -> 0 us
    pallas_call x1, Pallas kernels: 28.4 us -> 26.8 us  [device_fn(): pl.pallas_call(pipe_kernel, out_shape=(sds((2, KVW, LN), F32), sds((2, KV...]
    pallas_call x2, Pallas kernels: 7.51 us -> 8.22 us  [the longest x1 5.06 us: device_fn(): pl.pallas_call(post_kernel, out_shape=(cshape, cshape, pshape, pshape, sd...]
    unnamed x3 -> x0, local copies, waits for them, and re-layouts: 0.67 us -> none
where the time goes in v5:
time: 46.1 us; the launch traced here: 45.9 us
  Pallas kernels  44.4 us (96%)
  between operations  1.47 us (3%)
    pallas_call x1, Pallas kernels, device_fn(): pl.pallas_call(pipe_kernel, out_shape=(sds((2, KVW, LN), F32), sds((2, KV...  26.8 us
    pallas_call x1, Pallas kernels, device_fn(): pl.pallas_call(pre_kernel, out_shape=(cshape, cshape, tshape), in_specs=[...  9.26 us
    pallas_call x1, Pallas kernels, device_fn(): pl.pallas_call(post_kernel, out_shape=(cshape, cshape, pshape, pshape, sd...  5.06 us
    pallas_call x1, Pallas kernels, device_fn(): pl.pallas_call(head_kernel, out_shape=sds((FR, HID), BF16), in_specs=[ANY...  3.16 us

profile of v5, /device:TPU:7, one launch (start us, length us, event | category | flops | bytes accessed | tf_op | source)
XLA Modules:
  0.0 45.9 jit_solution(9150216210559458470)
XLA Ops:
  1.3 9.3 %pre.1 = (bf16[4,8,3,64,512]{4,3,2,1,0:T(8,128)(2,1)}, bf16[4,8,3,64,512]{4,3,2,1,0:T(8,128)(2,1)}, f32[8,128]{1,0:T(8,128)}) custom-call(bf16[4,8,3,64,512]{4,3,2,1,0:T(8,128)(2,1)} %bitcast.40, bf16[4,8,3,64,512]{4,3,2,1,0:T(8,128)(2,1)} %bitcast.43), custom_call_target="tpu_custom_call" | custom-call | tf_op jit(solution)/shard_map/pre/pallas_call | solution.py:645
  10.5 26.8 %pipe.1 = (f32[2,192,128]{2,1,0:T(8,128)}, f32[2,192,128]{2,1,0:T(8,128)}, bf16[3,64,512]{2,1,0:T(8,128)(2,1)}, bf16[3,64,512]{2,1,0:T(8,128)(2,1)}, bf16[40,576]{1,0:T(8,128)(2,1)}) custom-call(bf16[32,576]{1,0:T(8,128)(2,1)} %bitcast.60, bf16[256,576]{1,0:T(8,128)(2,1)} %bitcast.53, s32[4,8]{1,0:T(4,128)} %dlen_h.3, s32[1]{0:T(128)S(6)} %copy.37.plen, ...), custom_call_target="tpu_custom_call" | custom-call | tf_op jit(solution)/shard_map/pipe/pallas_call | solution.py:649
  37.3 0.1 mid.1
  37.5 3.2 %head.1.fr = bf16[40,576]{1,0:T(8,128)(2,1)} custom-call(bf16[40,576]{1,0:T(8,128)(2,1)} %get-tuple-element.28.fh, f32[8,128]{1,0:T(8,128)} %get-tuple-element.31.tok), custom_call_target="tpu_custom_call" | custom-call | tf_op jit(solution)/shard_map/head/pallas_call | solution.py:663
  40.6 5.1 %post.1 = (bf16[4,8,3,64,512]{4,3,2,1,0:T(8,128)(2,1)}, bf16[4,8,3,64,512]{4,3,2,1,0:T(8,128)(2,1)}, bf16[3,64,512]{2,1,0:T(8,128)(2,1)}, bf16[3,64,512]{2,1,0:T(8,128)(2,1)}, f32[9,4,1024]{2,1,0:T(4,128)}) custom-call(s32[4,8]{1,0:T(4,128)} %dlen_h.3, ...), custom_call_target="tpu_custom_call", output_to_operand_aliasing={{0}: (7, {}), {1}: (8, {}), {2}: (9, {}), {3}: (10, {})} | custom-call | tf_op jit(solution)/shard_map/post/pallas_call | solution.py:668

commit v6 on v5

--- a/solution.py
+++ b/solution.py
@@ -106,6 +106,18 @@
         pl.semaphore_signal(bar, inc=1, device_id={'stage': jnp.minimum(st + 1, LAST)}, device_id_type=MESH)
 
     wait('dl', 'pl', 'ifr')
+    for m in range(2):
+        kcp[m].start()
+        vcp[m].start()
+    start('kp', 'vp')
+
+    @pl.when(st > 0)
+    def _():
+        start('wo', 'gm', 'wg', 'wu', 'wd', 'gf')
+        for m in (2, 3):
+            kcp[m].start()
+            vcp[m].start()
+
     p0 = pl_s[0]
     li = lane_iota((1, 2 * LN))
     fr = ifr_s[...]
@@ -124,16 +136,6 @@
     for k in range(2):
         pb_s[k] = jnp.zeros((CL, 2 * LN), BF16)
 
-    start('kp', 'vp')
-    for m in range(2):
-        kcp[m].start()
-        vcp[m].start()
-    start('wo', 'gm')
-
-    @pl.when(st > 0)
-    def _():
-        start('wg', 'wu', 'wd', 'gf')
-
     wait('ga', 'wq')
     w3_s[:HID, :] = wq_s[...].astype(F32).T.astype(BF16)
     wait('wk', 'wv')
@@ -208,10 +210,6 @@
 
         if c == 0:
             wait('kp', 'vp')
-
-            @pl.when(st == 0)
-            def _():
-                start('wg', 'wu', 'wd', 'gf')
         else:
             for m in (2, 3):
                 kcp[m].wait()
@@ -274,11 +272,7 @@
 
                 @pl.when(st == 0)
                 def _():
-                    start('p1', 'd1')
-                for m in (2, 3):
-                    kcp[m].start()
-                    vcp[m].start()
-                wait('wo', 'gm')
+                    start('wo', 'gm', 'wg', 'wu', 'wd', 'gf', 'p1', 'd1')
 
         def dqk(i):
             for k in range(DR):
@@ -357,14 +351,16 @@
             mix(3)
             mix(4)
             a = jnp.concatenate([ot_s[...].T, dec_out(e0, CD)], axis=0).astype(BF16)
-            x1 = round32(xc_s[c].astype(F32) + nn(a, wo_perm()))
             if c == 0:
-                wait('wg', 'wu')
+                wait('wo', 'gm', 'wg', 'wu')
 
                 @pl.when(st == 0)
                 def _():
                     wait('wd')
-
+                    for m in (2, 3):
+                        kcp[m].start()
+                        vcp[m].start()
+            x1 = round32(xc_s[c].astype(F32) + nn(a, wo_perm()))
             def put(x, rows):
                 @pl.when(st == 0)
                 def _():
@@ -399,7 +395,7 @@
             for q in range(4):
                 dmix(q)
             if c == 0:
-                wait('wg', 'wu', 'gf')
+                wait('wo', 'gm', 'wg', 'wu', 'gf')
                 pl.semaphore_wait(bar, 1)
             else:
                 ls = [dec_out(k * ES + CD, 8)[:2] for k in range(2)]
@@ -436,32 +432,51 @@
     st = lax.axis_index('stage')
     lfh = pltpu.make_async_copy(fh, fh_s, lsem)
     bar = pltpu.get_barrier_semaphore()
-
-    def send(k):
-        return pltpu.make_async_remote_copy(fh_s, fr_s, ssem.at[k], rsem, device_id={'stage': k}, device_id_type=MESH)
+    relay = LAST - 1
+
+    def send(src, k):
+        return pltpu.make_async_remote_copy(src, fr_s, ssem.at[k], rsem, device_id={'stage': k}, device_id_type=MESH)
+
+    def hello(k):
+        pl.semaphore_signal(bar, inc=1, device_id={'stage': k}, device_id_type=MESH)
+
+    @pl.when(st == LAST)
+    def _():
+        lfh.start()
+
+    @pl.when(st != relay)
+    def _():
+        hello(relay)
+        pl.semaphore_wait(bar, 1)
+
+    @pl.when(st == relay)
+    def _():
+        for k in (0, 1, LAST):
+            hello(k)
+        pl.semaphore_wait(bar, LAST)
+
+    @pl.when(st == LAST)
+    def _():
+        lfh.wait()
+        send(fh_s, relay).start()
+        fo[...] = fh_s[...]
+        send(fh_s, relay).wait_send()
 
     @pl.when(st < LAST)
     def _():
-        pl.semaphore_signal(bar, inc=1, device_id={'stage': LAST}, device_id_type=MESH)
-
-    @pl.when(st == LAST)
-    def _():
-        lfh.start()
-        for k in range(LAST):
-            pl.semaphore_signal(bar, inc=1, device_id={'stage': k}, device_id_type=MESH)
-        pl.semaphore_wait(bar, LAST)
-        lfh.wait()
-        for k in range(LAST):
-            send(k).start()
-        fo[...] = fh_s[...]
-        for k in range(LAST):
-            send(k).wait_send()
-
-    @pl.when(st < LAST)
-    def _():
-        pl.semaphore_wait(bar, 1)
-        send(0).wait_recv()
+        send(fh_s, 0).wait_recv()
+
+        @pl.when(st == relay)
+        def _():
+            for k in range(relay):
+                send(fr_s, k).start()
+
         fo[...] = fr_s[...]
+
+        @pl.when(st == relay)
+        def _():
+            for k in range(relay):
+                send(fr_s, k).wait_send()
 
 
 def tile_start(pos):
@@ -514,13 +529,13 @@
         for i in range(DR):
             cp(bk, kt, ksem, m, i, False).start()
             cp(bv, vt, vsem, m, i, False).start()
+    if extra is not None:
+        extra[0]()
     for c in cs[:4]:
         c.wait()
     po = [pltpu.make_async_copy(new[2], kpo, nsem.at[2]), pltpu.make_async_copy(new[3], vpo, nsem.at[3])]
     for o in po:
         o.start()
-    if extra is not None:
-        extra()
     for m in range(NM):
         for hbm, scr, sem, nw in ((ko, kt, ksem, new[0]), (vo, vt, vsem, new[1])):
             for i in range(DR):
@@ -532,6 +547,8 @@
                     scr[m, i, g] = jnp.where(lane == pos % LN, col, scr[m, i, g].astype(F32)).astype(BF16)
             for i in range(DR):
                 cp(hbm, scr, sem, m, i, True).start()
+    if extra is not None:
+        extra[1]()
     for m in range(NM):
         for i in range(DR):
             cp(ko, kt, ksem, m, i, True).wait()
@@ -578,6 +595,10 @@
     lf = pltpu.make_async_copy(fr, fr_s, hsem.at[0])
     lw = pltpu.make_async_copy(wh, wh_s, hsem.at[1])
 
+    def load():
+        lf.start()
+        lw.start()
+
     def head():
         lf.wait()
         lw.wait()
@@ -589,14 +610,11 @@
     def _():
         new = (kn_s, vn_s, kp_s, vp_s)
         cs = load_new((kdn, vdn, kpn, vpn, dlen_h), new + (dlen,), nsem)
-        lf.start()
-        lw.start()
-        update_tiles(dlen, bk, bv, ko, vo, kpo, vpo, kt, vt, new, cs, ksem, vsem, nsem, head)
+        update_tiles(dlen, bk, bv, ko, vo, kpo, vpo, kt, vt, new, cs, ksem, vsem, nsem, (load, head))
 
     @pl.when(st < LAST)
     def _():
-        lf.start()
-        lw.start()
+        load()
         head()
 
 

time: 46.1 us -> 47.2 us (1.024)
  Pallas kernels: 44.4 us -> 45.1 us
    pallas_call x1, Pallas kernels: 3.16 us -> 2.36 us  [device_fn(): pl.pallas_call(head_kernel, out_shape=sds((FR, HID), BF16), in_specs=[ANY...]
    pallas_call x1, Pallas kernels: 26.8 us -> 27.6 us  [device_fn(): pl.pallas_call(pipe_kernel, out_shape=(sds((2, KVW, LN), F32), sds((2, KV...]
    pallas_call x1, Pallas kernels: 5.06 us -> 5.74 us  [device_fn(): pl.pallas_call(post_kernel, out_shape=(cshape, cshape, pshape, pshape, sd...]
where the time goes in v6:
time: 47.2 us; the launch traced here: 46.5 us
  Pallas kernels  45.1 us (96%)
  between operations  1.47 us (3%)
    pallas_call x1, Pallas kernels, device_fn(): pl.pallas_call(pipe_kernel, out_shape=(sds((2, KVW, LN), F32), sds((2, KV...  27.6 us
    pallas_call x1, Pallas kernels, device_fn(): pl.pallas_call(pre_kernel, out_shape=(cshape, cshape, tshape), in_specs=[...  9.26 us
    pallas_call x1, Pallas kernels, device_fn(): pl.pallas_call(post_kernel, out_shape=(cshape, cshape, pshape, pshape, sd...  5.74 us
    pallas_call x1, Pallas kernels, device_fn(): pl.pallas_call(head_kernel, out_shape=sds((FR, HID), BF16), in_specs=[ANY...  2.36 us

profile of v6, /device:TPU:7, one launch (start us, length us, event | category | flops | bytes accessed | tf_op | source)
XLA Modules:
  0.0 46.5 jit_solution(7046048105720829652)
XLA Ops:
  1.3 9.3 %pre.1 = (bf16[4,8,3,64,512]{4,3,2,1,0:T(8,128)(2,1)}, bf16[4,8,3,64,512]{4,3,2,1,0:T(8,128)(2,1)}, f32[8,128]{1,0:T(8,128)}) custom-call(bf16[4,8,3,64,512]{4,3,2,1,0:T(8,128)(2,1)} %bitcast.40, bf16[4,8,3,64,512]{4,3,2,1,0:T(8,128)(2,1)} %bitcast.43), custom_call_target="tpu_custom_call" | custom-call | tf_op jit(solution)/shard_map/pre/pallas_call | solution.py:663
  10.5 27.6 %pipe.1 = (f32[2,192,128]{2,1,0:T(8,128)}, f32[2,192,128]{2,1,0:T(8,128)}, bf16[3,64,512]{2,1,0:T(8,128)(2,1)}, bf16[3,64,512]{2,1,0:T(8,128)(2,1)}, bf16[40,576]{1,0:T(8,128)(2,1)}) custom-call(bf16[32,576]{1,0:T(8,128)(2,1)} %bitcast.60, bf16[256,576]{1,0:T(8,128)(2,1)} %bitcast.53, s32[4,8]{1,0:T(4,128)} %dlen_h.3, s32[1]{0:T(128)S(6)} %copy.37.plen, ...), custom_call_target="tpu_custom_call" | custom-call | tf_op jit(solution)/shard_map/pipe/pallas_call | solution.py:667
  38.1 0.1 mid.1
  38.3 2.4 %head.1.fr = bf16[40,576]{1,0:T(8,128)(2,1)} custom-call(bf16[40,576]{1,0:T(8,128)(2,1)} %get-tuple-element.28.fh, f32[8,128]{1,0:T(8,128)} %get-tuple-element.31.tok), custom_call_target="tpu_custom_call" | custom-call | tf_op jit(solution)/shard_map/head/pallas_call | solution.py:681
  40.6 5.7 %post.1 = (bf16[4,8,3,64,512]{4,3,2,1,0:T(8,128)(2,1)}, bf16[4,8,3,64,512]{4,3,2,1,0:T(8,128)(2,1)}, bf16[3,64,512]{2,1,0:T(8,128)(2,1)}, bf16[3,64,512]{2,1,0:T(8,128)(2,1)}, f32[9,4,1024]{2,1,0:T(4,128)}) custom-call(s32[4,8]{1,0:T(4,128)} %dlen_h.3, ...), custom_call_target="tpu_custom_call", output_to_operand_aliasing={{0}: (7, {}), {1}: (8, {}), {2}: (9, {}), {3}: (10, {})} | custom-call | tf_op jit(solution)/shard_map/post/pallas_call | solution.py:686

commit v7 on v5

--- a/solution.py
+++ b/solution.py
@@ -106,6 +106,11 @@
         pl.semaphore_signal(bar, inc=1, device_id={'stage': jnp.minimum(st + 1, LAST)}, device_id_type=MESH)
 
     wait('dl', 'pl', 'ifr')
+    for m in range(2):
+        kcp[m].start()
+        vcp[m].start()
+    start('kp', 'vp')
+
     p0 = pl_s[0]
     li = lane_iota((1, 2 * LN))
     fr = ifr_s[...]
@@ -124,17 +129,15 @@
     for k in range(2):
         pb_s[k] = jnp.zeros((CL, 2 * LN), BF16)
 
-    start('kp', 'vp')
-    for m in range(2):
-        kcp[m].start()
-        vcp[m].start()
-    start('wo', 'gm')
+    wait('ga', 'wq')
+    start('wo', 'gm', 'wg', 'wu', 'wd', 'gf')
 
     @pl.when(st > 0)
     def _():
-        start('wg', 'wu', 'wd', 'gf')
-
-    wait('ga', 'wq')
+        for m in (2, 3):
+            kcp[m].start()
+            vcp[m].start()
+
     w3_s[:HID, :] = wq_s[...].astype(F32).T.astype(BF16)
     wait('wk', 'wv')
 
@@ -208,10 +211,6 @@
 
         if c == 0:
             wait('kp', 'vp')
-
-            @pl.when(st == 0)
-            def _():
-                start('wg', 'wu', 'wd', 'gf')
         else:
             for m in (2, 3):
                 kcp[m].wait()
@@ -275,10 +274,9 @@
                 @pl.when(st == 0)
                 def _():
                     start('p1', 'd1')
-                for m in (2, 3):
-                    kcp[m].start()
-                    vcp[m].start()
-                wait('wo', 'gm')
+                    for m in (2, 3):
+                        kcp[m].start()
+                        vcp[m].start()
 
         def dqk(i):
             for k in range(DR):
@@ -315,19 +313,24 @@
             def fold(v, op):
                 return op(v.reshape(v.shape[0] // 8, 8, v.shape[1]), axis=0)
 
+            ck = 64
+
+            def masked(sl, q, ln):
+                v = ps_s[sl, q:q + ck, ln]
+                return v if q + ck <= 64 else v + bias_s[q:q + ck, :]
+
             def mix(t):
                 sl = t % 2
-                ck = 64
                 hs = heads(t)
                 for i, j in enumerate(hs):
                     ln = slice(i * LN, (i + 1) * LN)
                     mx = jnp.full((8, LN), NEG, F32)
                     for q in range(0, lim, ck):
-                        mx = jnp.maximum(mx, fold(ps_s[sl, q:q + ck, ln] + bias_s[q:q + ck, :], jnp.max))
+                        mx = jnp.maximum(mx, fold(masked(sl, q, ln), jnp.max))
                     mx = jnp.max(mx, axis=0, keepdims=True)
                     sm = jnp.zeros((8, LN), F32)
                     for q in range(0, lim, ck):
-                        p = jnp.exp(ps_s[sl, q:q + ck, ln] + bias_s[q:q + ck, :] - mx)
+                        p = jnp.exp(masked(sl, q, ln) - mx)
                         ps_s[sl, q:q + ck, ln] = p
                         sm = sm + fold(p, jnp.sum)
                     rl = 1.0 / jnp.sum(sm, axis=0, keepdims=True)
@@ -357,14 +360,13 @@
             mix(3)
             mix(4)
             a = jnp.concatenate([ot_s[...].T, dec_out(e0, CD)], axis=0).astype(BF16)
-            x1 = round32(xc_s[c].astype(F32) + nn(a, wo_perm()))
             if c == 0:
-                wait('wg', 'wu')
+                wait('wo', 'gm', 'wg', 'wu')
 
                 @pl.when(st == 0)
                 def _():
                     wait('wd')
-
+            x1 = round32(xc_s[c].astype(F32) + nn(a, wo_perm()))
             def put(x, rows):
                 @pl.when(st == 0)
                 def _():
@@ -399,7 +401,7 @@
             for q in range(4):
                 dmix(q)
             if c == 0:
-                wait('wg', 'wu', 'gf')
+                wait('wo', 'gm', 'wg', 'wu', 'gf')
                 pl.semaphore_wait(bar, 1)
             else:
                 ls = [dec_out(k * ES + CD, 8)[:2] for k in range(2)]
@@ -432,28 +434,40 @@
             hop(c).wait_send()
 
 
-def head_kernel(fh, tok, fo, fh_s, fr_s, lsem, ssem, rsem):
+def head_kernel(fh, wh, tok, logits, fh_s, fr_s, wh_s, lsem, ssem, rsem):
     st = lax.axis_index('stage')
-    lfh = pltpu.make_async_copy(fh, fh_s, lsem)
+    lfh = pltpu.make_async_copy(fh, fh_s, lsem.at[0])
+    lwh = pltpu.make_async_copy(wh, wh_s, lsem.at[1])
+
+    @pl.when(st == LAST)
+    def _():
+        lfh.start()
+
+    lwh.start()
     bar = pltpu.get_barrier_semaphore()
 
     def send(k):
         return pltpu.make_async_remote_copy(fh_s, fr_s, ssem.at[k], rsem, device_id={'stage': k}, device_id_type=MESH)
 
+    def head(ref):
+        lwh.wait()
+        lg = nn(ref[...], wh_s[...])
+        for i in range(DR + 1):
+            logits[i] = lg[i * NM:(i + 1) * NM]
+
     @pl.when(st < LAST)
     def _():
         pl.semaphore_signal(bar, inc=1, device_id={'stage': LAST}, device_id_type=MESH)
 
     @pl.when(st == LAST)
     def _():
-        lfh.start()
         for k in range(LAST):
             pl.semaphore_signal(bar, inc=1, device_id={'stage': k}, device_id_type=MESH)
         pl.semaphore_wait(bar, LAST)
         lfh.wait()
         for k in range(LAST):
             send(k).start()
-        fo[...] = fh_s[...]
+        head(fh_s)
         for k in range(LAST):
             send(k).wait_send()
 
@@ -461,7 +475,7 @@
     def _():
         pl.semaphore_wait(bar, 1)
         send(0).wait_recv()
-        fo[...] = fr_s[...]
+        head(fr_s)
 
 
 def tile_start(pos):
@@ -496,7 +510,7 @@
 
 def load_new(srcs, dsts, sem):
     cs = [pltpu.make_async_copy(a, b, sem.at[i]) for i, (a, b) in enumerate(zip(srcs, dsts))]
-    for c in cs:
+    for c in cs[4:] + cs[:4]:
         c.start()
     return cs
 
@@ -514,13 +528,13 @@
         for i in range(DR):
             cp(bk, kt, ksem, m, i, False).start()
             cp(bv, vt, vsem, m, i, False).start()
+    if extra is not None:
+        extra()
     for c in cs[:4]:
         c.wait()
     po = [pltpu.make_async_copy(new[2], kpo, nsem.at[2]), pltpu.make_async_copy(new[3], vpo, nsem.at[3])]
     for o in po:
         o.start()
-    if extra is not None:
-        extra()
     for m in range(NM):
         for hbm, scr, sem, nw in ((ko, kt, ksem, new[0]), (vo, vt, vsem, new[1])):
             for i in range(DR):
@@ -572,32 +586,29 @@
         update_tiles(dlen, bk, bv, ko, vo, kpo, vpo, kt, vt, new, cs, ksem, vsem, nsem)
 
 
-def post_kernel(dlen_h, kdn, vdn, kpn, vpn, fr, wh, bk, bv, bkp, bvp, ko, vo, kpo, vpo, logits,
-                kt, vt, fr_s, wh_s, kn_s, vn_s, kp_s, vp_s, dlen, ksem, vsem, nsem, hsem):
+def post_kernel(dlen_h, kdn, vdn, kpn, vpn, lg, bk, bv, bkp, bvp, ko, vo, kpo, vpo, logits,
+                kt, vt, lg_s, kn_s, vn_s, kp_s, vp_s, dlen, ksem, vsem, nsem, hsem):
     st = lax.axis_index('stage')
-    lf = pltpu.make_async_copy(fr, fr_s, hsem.at[0])
-    lw = pltpu.make_async_copy(wh, wh_s, hsem.at[1])
-
-    def head():
+    lf = pltpu.make_async_copy(lg, lg_s, hsem.at[0])
+    lo = pltpu.make_async_copy(lg_s, logits, hsem.at[1])
+
+    def turn():
         lf.wait()
-        lw.wait()
-        lg = nn(fr_s[...], wh_s[...])
-        for i in range(DR + 1):
-            logits[i] = lg[i * NM:(i + 1) * NM]
+        lo.start()
 
     @pl.when(st == LAST)
     def _():
         new = (kn_s, vn_s, kp_s, vp_s)
         cs = load_new((kdn, vdn, kpn, vpn, dlen_h), new + (dlen,), nsem)
         lf.start()
-        lw.start()
-        update_tiles(dlen, bk, bv, ko, vo, kpo, vpo, kt, vt, new, cs, ksem, vsem, nsem, head)
+        update_tiles(dlen, bk, bv, ko, vo, kpo, vpo, kt, vt, new, cs, ksem, vsem, nsem, turn)
 
     @pl.when(st < LAST)
     def _():
         lf.start()
-        lw.start()
-        head()
+        turn()
+
+    lo.wait()
 
 
 ANY = pl.BlockSpec(memory_space=pltpu.HBM)
@@ -660,16 +671,17 @@
             input_output_aliases={3: 0, 4: 1},
             scratch_shapes=[vm(kd.shape, BF16), vm(vd.shape, BF16), tile, tile] + news + nsems + [pltpu.SemaphoreType.DMA((5,))],
             name='mid', compiler_params=big)(dec_len, kd, vd, bk, bv, kdn, vdn, kpn, vpn)
-        fr = pl.pallas_call(
-            head_kernel, out_shape=sds((FR, HID), BF16), in_specs=[ANY] * 2, out_specs=vmem,
-            scratch_shapes=[vm((FR, HID), BF16), vm((FR, HID), BF16),
-                            pltpu.SemaphoreType.DMA, pltpu.SemaphoreType.DMA((LAST,)), pltpu.SemaphoreType.DMA],
-            name='head', compiler_params=pltpu.CompilerParams(collective_id=1, has_side_effects=True))(fh, tok2)
+        lgs = sds((DR + 1, NM, VOC), F32)
+        lg = pl.pallas_call(
+            head_kernel, out_shape=lgs, in_specs=[ANY] * 3, out_specs=vmem,
+            scratch_shapes=[vm((FR, HID), BF16), vm((FR, HID), BF16), vm((HID, VOC), BF16),
+                            pltpu.SemaphoreType.DMA((2,)), pltpu.SemaphoreType.DMA((LAST,)), pltpu.SemaphoreType.DMA],
+            name='head', compiler_params=pltpu.CompilerParams(collective_id=1, has_side_effects=True))(fh, w_head, tok2)
         ko, vo, kpo, vpo, logits = pl.pallas_call(
-            post_kernel, out_shape=(cshape, cshape, pshape, pshape, sds((DR + 1, NM, VOC), F32)), in_specs=[ANY] * 11,
-            out_specs=(ANY,) * 4 + (vmem,), input_output_aliases={7: 0, 8: 1, 9: 2, 10: 3},
-            scratch_shapes=[tile, tile, vm((FR, HID), BF16), vm((HID, VOC), BF16)] + news + nsems + [pltpu.SemaphoreType.DMA((5,)), pltpu.SemaphoreType.DMA((2,))],
-            name='post', compiler_params=big)(dec_len, kdn, vdn, kpn, vpn, fr, w_head, bk, bv, bkp, bvp)
+            post_kernel, out_shape=(cshape, cshape, pshape, pshape, lgs), in_specs=[ANY] * 10,
+            out_specs=(ANY,) * 5, input_output_aliases={6: 0, 7: 1, 8: 2, 9: 3},
+            scratch_shapes=[tile, tile, vm((DR + 1, NM, VOC), F32)] + news + nsems + [pltpu.SemaphoreType.DMA((5,)), pltpu.SemaphoreType.DMA((2,))],
+            name='post', compiler_params=big)(dec_len, kdn, vdn, kpn, vpn, lg, bk, bv, bkp, bvp)
         back = lambda a: jnp.transpose(a, (0, 1, 4, 2, 3))[None]
         backp = lambda a: jnp.transpose(a, (2, 0, 1))[None]
         return jnp.transpose(logits, (1, 0, 2)), back(ko), back(vo), backp(kpo), backp(vpo)

time: 46.1 us -> 45.7 us (level)
    pallas_call x2, Pallas kernels: 8.22 us -> 7.39 us  [the longest x1 4.19 us: device_fn(): pl.pallas_call(post_kernel, out_shape=(cshape, cshape, pshape, pshape, lg...]
    pallas_call x1, Pallas kernels: 26.8 us -> 27.3 us  [device_fn(): pl.pallas_call(pipe_kernel, out_shape=(sds((2, KVW, LN), F32), sds((2, KV...]
where the time goes in v7:
time: 45.7 us; the launch traced here: 45.5 us
  Pallas kernels  44.1 us (96%)
  between operations  1.47 us (3%)
    pallas_call x1, Pallas kernels, device_fn(): pl.pallas_call(pipe_kernel, out_shape=(sds((2, KVW, LN), F32), sds((2, KV...  27.3 us
    pallas_call x1, Pallas kernels, device_fn(): pl.pallas_call(pre_kernel, out_shape=(cshape, cshape, tshape), in_specs=[...  9.26 us
    pallas_call x1, Pallas kernels, device_fn(): pl.pallas_call(post_kernel, out_shape=(cshape, cshape, pshape, pshape, lg...  4.19 us
    pallas_call x1, Pallas kernels, device_fn(): pl.pallas_call(head_kernel, out_shape=lgs, in_specs=[ANY] * 3, out_specs=...  3.2 us

profile of v7, /device:TPU:7, one launch (start us, length us, event | category | flops | bytes accessed | tf_op | source)
XLA Modules:
  0.0 45.5 jit_solution(635476898270560120)
XLA Ops:
  1.3 9.3 %pre.1 = (bf16[4,8,3,64,512]{4,3,2,1,0:T(8,128)(2,1)}, bf16[4,8,3,64,512]{4,3,2,1,0:T(8,128)(2,1)}, f32[8,128]{1,0:T(8,128)}) custom-call(bf16[4,8,3,64,512]{4,3,2,1,0:T(8,128)(2,1)} %bitcast.40, bf16[4,8,3,64,512]{4,3,2,1,0:T(8,128)(2,1)} %bitcast.43), custom_call_target="tpu_custom_call" | custom-call | tf_op jit(solution)/shard_map/pre/pallas_call | solution.py:656
  10.5 27.3 %pipe.1 = (f32[2,192,128]{2,1,0:T(8,128)}, f32[2,192,128]{2,1,0:T(8,128)}, bf16[3,64,512]{2,1,0:T(8,128)(2,1)}, bf16[3,64,512]{2,1,0:T(8,128)(2,1)}, bf16[40,576]{1,0:T(8,128)(2,1)}) custom-call(bf16[32,576]{1,0:T(8,128)(2,1)} %bitcast.60, bf16[256,576]{1,0:T(8,128)(2,1)} %bitcast.53, s32[4,8]{1,0:T(4,128)} %dlen_h.3, s32[1]{0:T(128)S(6)} %copy.37.plen, ...), custom_call_target="tpu_custom_call" | custom-call | tf_op jit(solution)/shard_map/pipe/pallas_call | solution.py:660
  37.8 0.1 mid.1
  38.0 3.2 %head.1.lg = f32[9,4,1024]{2,1,0:T(4,128)} custom-call(bf16[40,576]{1,0:T(8,128)(2,1)} %get-tuple-element.28.fh, bf16[576,1024]{1,0:T(8,128)(2,1)} %wh.1, f32[8,128]{1,0:T(8,128)} %get-tuple-element.31.tok), custom_call_target="tpu_custom_call" | custom-call | tf_op jit(solution)/shard_map/head/pallas_call | solution.py:675
  41.2 4.2 %post.1 = (bf16[4,8,3,64,512]{4,3,2,1,0:T(8,128)(2,1)}, bf16[4,8,3,64,512]{4,3,2,1,0:T(8,128)(2,1)}, bf16[3,64,512]{2,1,0:T(8,128)(2,1)}, bf16[3,64,512]{2,1,0:T(8,128)(2,1)}, f32[9,4,1024]{2,1,0:T(4,128)}) custom-call(s32[4,8]{1,0:T(4,128)} %dlen_h.3, ...), custom_call_target="tpu_custom_call", output_to_operand_aliasing={{0}: (6, {}), {1}: (7, {}), {2}: (8, {}), {3}: (9, {})} | custom-call | tf_op jit(solution)/shard_map/post/pallas_call | solution.py:680

commit v8 on v7

--- a/solution.py
+++ b/solution.py
@@ -37,6 +37,7 @@
 CR = CP + CD
 ES = CD + 8
 FR = ND + 8
+PARTS = (slice(0, 256), slice(256, HID))
 
 
 def nt(a, b):
@@ -106,11 +107,6 @@
         pl.semaphore_signal(bar, inc=1, device_id={'stage': jnp.minimum(st + 1, LAST)}, device_id_type=MESH)
 
     wait('dl', 'pl', 'ifr')
-    for m in range(2):
-        kcp[m].start()
-        vcp[m].start()
-    start('kp', 'vp')
-
     p0 = pl_s[0]
     li = lane_iota((1, 2 * LN))
     fr = ifr_s[...]
@@ -129,11 +125,16 @@
     for k in range(2):
         pb_s[k] = jnp.zeros((CL, 2 * LN), BF16)
 
+    start('kp', 'vp')
+    for m in range(2):
+        kcp[m].start()
+        vcp[m].start()
+    start('wo', 'gm')
     wait('ga', 'wq')
-    start('wo', 'gm', 'wg', 'wu', 'wd', 'gf')
 
     @pl.when(st > 0)
     def _():
+        start('wg', 'wu', 'wd', 'gf')
         for m in (2, 3):
             kcp[m].start()
             vcp[m].start()
@@ -191,8 +192,8 @@
     def round32(x):
         return x.astype(BF16).astype(F32)
 
-    def hop(c):
-        return pltpu.make_async_remote_copy(so_s.at[c], xc_s.at[c], ssem.at[c], rsem.at[c],
+    def hop(c, i):
+        return pltpu.make_async_remote_copy(so_s.at[c, :, PARTS[i]], xc_s.at[c, :, PARTS[i]], ssem.at[c, i], rsem.at[c, i],
                                             device_id={'stage': jnp.minimum(st + 1, LAST)}, device_id_type=MESH)
 
     def last_rows(x):
@@ -207,7 +208,8 @@
 
         @pl.when(st > 0)
         def _():
-            hop(c).wait_recv()
+            for i in range(len(PARTS)):
+                hop(c, i).wait_recv()
 
         if c == 0:
             wait('kp', 'vp')
@@ -267,16 +269,23 @@
 
         def loads():
             if c == 0:
-                for m in (0, 1):
-                    kcp[m].wait()
-                    vcp[m].wait()
+                kcp[0].wait()
+
+                @pl.when(st == 0)
+                def _():
+                    start('wg', 'wu', 'wd', 'gf')
+
+                kcp[1].wait()
+                vcp[0].wait()
+                vcp[1].wait()
 
                 @pl.when(st == 0)
                 def _():
                     start('p1', 'd1')
-                    for m in (2, 3):
-                        kcp[m].start()
-                        vcp[m].start()
+                    kcp[2].start()
+                    vcp[2].start()
+
+                wait('wo', 'gm')
 
         def dqk(i):
             for k in range(DR):
@@ -360,32 +369,35 @@
             mix(3)
             mix(4)
             a = jnp.concatenate([ot_s[...].T, dec_out(e0, CD)], axis=0).astype(BF16)
+            x1 = round32(xc_s[c].astype(F32) + nn(a, wo_perm()))
             if c == 0:
-                wait('wo', 'gm', 'wg', 'wu')
+                wait('wg', 'wu')
 
                 @pl.when(st == 0)
                 def _():
                     wait('wd')
-            x1 = round32(xc_s[c].astype(F32) + nn(a, wo_perm()))
+                    kcp[3].start()
+                    vcp[3].start()
+                    pl.semaphore_wait(bar, 1)
+
+                @pl.when(st > 0)
+                def _():
+                    pl.semaphore_wait(bar, 2)
+
             def put(x, rows):
                 @pl.when(st == 0)
                 def _():
-                    so_s[c] = (x + nt(act_s[...], wd_s[...])).astype(BF16)
+                    for i, w in enumerate(PARTS):
+                        so_s[c, :, w] = (x[:, w] + nt(act_s[...], wd_s[w, :])).astype(BF16)
+                        hop(c, i).start()
 
                 @pl.when(st > 0)
                 def _():
-                    so_s[c] = (x + nn(act_s[...], wdt_s[...])).astype(BF16)
+                    for i, w in enumerate(PARTS):
+                        so_s[c, :, w] = (x[:, w] + nn(act_s[...], wdt_s[:, w])).astype(BF16)
+                        hop(c, i).start()
 
             mlp(x1, CR, put)
-            if c == 0:
-                @pl.when(st == 0)
-                def _():
-                    pl.semaphore_wait(bar, 1)
-
-                @pl.when(st > 0)
-                def _():
-                    pl.semaphore_wait(bar, 2)
-            hop(c).start()
 
         @pl.when(st == LAST)
         def _():
@@ -401,7 +413,7 @@
             for q in range(4):
                 dmix(q)
             if c == 0:
-                wait('wo', 'gm', 'wg', 'wu', 'gf')
+                wait('wg', 'wu', 'gf')
                 pl.semaphore_wait(bar, 1)
             else:
                 ls = [dec_out(k * ES + CD, 8)[:2] for k in range(2)]
@@ -431,7 +443,8 @@
     def _():
         wait('gf')
         for c in range(2):
-            hop(c).wait_send()
+            for i in range(len(PARTS)):
+                hop(c, i).wait_send()
 
 
 def head_kernel(fh, wh, tok, logits, fh_s, fr_s, wh_s, lsem, ssem, rsem):
@@ -642,7 +655,7 @@
             vm((2, KVW, LN), F32), vm((2, KVW, LN), F32), vm(((2 * DR + 2) * 24, CL), F32), vm((2, CL, 2 * LN), F32), vm((2, CL, 2 * LN), BF16),
             vm((CL, LN), F32), vm((HID, LN), F32), vm((CR, FFN), BF16), vm((2, CR, HID), BF16), vm((FR, HID), BF16),
             pltpu.SemaphoreType.DMA((19,)), pltpu.SemaphoreType.DMA((NM,)), pltpu.SemaphoreType.DMA((NM,)), pltpu.SemaphoreType.DMA((7,)),
-            pltpu.SemaphoreType.DMA((2,)), pltpu.SemaphoreType.DMA((2,)),
+            pltpu.SemaphoreType.DMA((2, 2)), pltpu.SemaphoreType.DMA((2, 2)),
         ]
         sds = jax.ShapeDtypeStruct
         big = pltpu.CompilerParams(vmem_limit_bytes=62 * 1024 * 1024)

time: 45.7 us -> 46.2 us (1.011)
  no operation moved by 1% of the time
where the time goes in v8:
time: 46.2 us; the launch traced here: 46 us
  Pallas kernels  44.5 us (96%)
  between operations  1.47 us (3%)
    pallas_call x1, Pallas kernels, device_fn(): pl.pallas_call(pipe_kernel, out_shape=(sds((2, KVW, LN), F32), sds((2, KV...  27.7 us
    pallas_call x1, Pallas kernels, device_fn(): pl.pallas_call(pre_kernel, out_shape=(cshape, cshape, tshape), in_specs=[...  9.26 us
    pallas_call x1, Pallas kernels, device_fn(): pl.pallas_call(post_kernel, out_shape=(cshape, cshape, pshape, pshape, lg...  4.19 us
    pallas_call x1, Pallas kernels, device_fn(): pl.pallas_call(head_kernel, out_shape=lgs, in_specs=[ANY] * 3, out_specs=...  3.2 us

profile of v8, /device:TPU:7, one launch (start us, length us, event | category | flops | bytes accessed | tf_op | source)
XLA Modules:
  0.0 46.0 jit_solution(11957509506653212759)
XLA Ops:
  1.3 9.3 %pre.1 = (bf16[4,8,3,64,512]{4,3,2,1,0:T(8,128)(2,1)}, bf16[4,8,3,64,512]{4,3,2,1,0:T(8,128)(2,1)}, f32[8,128]{1,0:T(8,128)}) custom-call(bf16[4,8,3,64,512]{4,3,2,1,0:T(8,128)(2,1)} %bitcast.40, bf16[4,8,3,64,512]{4,3,2,1,0:T(8,128)(2,1)} %bitcast.43), custom_call_target="tpu_custom_call" | custom-call | tf_op jit(solution)/shard_map/pre/pallas_call | solution.py:669
  10.5 27.7 %pipe.1 = (f32[2,192,128]{2,1,0:T(8,128)}, f32[2,192,128]{2,1,0:T(8,128)}, bf16[3,64,512]{2,1,0:T(8,128)(2,1)}, bf16[3,64,512]{2,1,0:T(8,128)(2,1)}, bf16[40,576]{1,0:T(8,128)(2,1)}) custom-call(bf16[32,576]{1,0:T(8,128)(2,1)} %bitcast.60, bf16[256,576]{1,0:T(8,128)(2,1)} %bitcast.53, s32[4,8]{1,0:T(4,128)} %dlen_h.3, s32[1]{0:T(128)S(6)} %copy.37.plen, ...), custom_call_target="tpu_custom_call" | custom-call | tf_op jit(solution)/shard_map/pipe/pallas_call | solution.py:673
  38.3 0.1 mid.1
  38.4 3.2 %head.1.lg = f32[9,4,1024]{2,1,0:T(4,128)} custom-call(bf16[40,576]{1,0:T(8,128)(2,1)} %get-tuple-element.28.fh, bf16[576,1024]{1,0:T(8,128)(2,1)} %wh.1, f32[8,128]{1,0:T(8,128)} %get-tuple-element.31.tok), custom_call_target="tpu_custom_call" | custom-call | tf_op jit(solution)/shard_map/head/pallas_call | solution.py:688
  41.6 4.2 %post.1 = (bf16[4,8,3,64,512]{4,3,2,1,0:T(8,128)(2,1)}, bf16[4,8,3,64,512]{4,3,2,1,0:T(8,128)(2,1)}, bf16[3,64,512]{2,1,0:T(8,128)(2,1)}, bf16[3,64,512]{2,1,0:T(8,128)(2,1)}, f32[9,4,1024]{2,1,0:T(4,128)}) custom-call(s32[4,8]{1,0:T(4,128)} %dlen_h.3, ...), custom_call_target="tpu_custom_call", output_to_operand_aliasing={{0}: (6, {}), {1}: (7, {}), {2}: (8, {}), {3}: (9, {})} | custom-call | tf_op jit(solution)/shard_map/post/pallas_call | solution.py:693

commit v9 on v7

--- a/solution.py
+++ b/solution.py
@@ -106,11 +106,6 @@
         pl.semaphore_signal(bar, inc=1, device_id={'stage': jnp.minimum(st + 1, LAST)}, device_id_type=MESH)
 
     wait('dl', 'pl', 'ifr')
-    for m in range(2):
-        kcp[m].start()
-        vcp[m].start()
-    start('kp', 'vp')
-
     p0 = pl_s[0]
     li = lane_iota((1, 2 * LN))
     fr = ifr_s[...]
@@ -129,15 +124,17 @@
     for k in range(2):
         pb_s[k] = jnp.zeros((CL, 2 * LN), BF16)
 
+    start('kp', 'vp')
+    for m in range(2):
+        kcp[m].start()
+        vcp[m].start()
+    start('wo', 'gm')
+
+    @pl.when(st > 0)
+    def _():
+        start('wg', 'wu', 'wd', 'gf')
+
     wait('ga', 'wq')
-    start('wo', 'gm', 'wg', 'wu', 'wd', 'gf')
-
-    @pl.when(st > 0)
-    def _():
-        for m in (2, 3):
-            kcp[m].start()
-            vcp[m].start()
-
     w3_s[:HID, :] = wq_s[...].astype(F32).T.astype(BF16)
     wait('wk', 'wv')
 
@@ -211,6 +208,10 @@
 
         if c == 0:
             wait('kp', 'vp')
+
+            @pl.when(st == 0)
+            def _():
+                start('wg', 'wu', 'wd', 'gf')
         else:
             for m in (2, 3):
                 kcp[m].wait()
@@ -274,9 +275,10 @@
                 @pl.when(st == 0)
                 def _():
                     start('p1', 'd1')
-                    for m in (2, 3):
-                        kcp[m].start()
-                        vcp[m].start()
+                for m in (2, 3):
+                    kcp[m].start()
+                    vcp[m].start()
+                wait('wo', 'gm')
 
         def dqk(i):
             for k in range(DR):
@@ -360,13 +362,14 @@
             mix(3)
             mix(4)
             a = jnp.concatenate([ot_s[...].T, dec_out(e0, CD)], axis=0).astype(BF16)
+            x1 = round32(xc_s[c].astype(F32) + nn(a, wo_perm()))
             if c == 0:
-                wait('wo', 'gm', 'wg', 'wu')
+                wait('wg', 'wu')
 
                 @pl.when(st == 0)
                 def _():
                     wait('wd')
-            x1 = round32(xc_s[c].astype(F32) + nn(a, wo_perm()))
+
             def put(x, rows):
                 @pl.when(st == 0)
                 def _():
@@ -401,7 +404,7 @@
             for q in range(4):
                 dmix(q)
             if c == 0:
-                wait('wo', 'gm', 'wg', 'wu', 'gf')
+                wait('wg', 'wu', 'gf')
                 pl.semaphore_wait(bar, 1)
             else:
                 ls = [dec_out(k * ES + CD, 8)[:2] for k in range(2)]

time: 45.7 us -> 45.2 us (0.989)
  Pallas kernels: 44.1 us -> 43.5 us
    pallas_call x1, Pallas kernels: 27.3 us -> 26.7 us  [device_fn(): pl.pallas_call(pipe_kernel, out_shape=(sds((2, KVW, LN), F32), sds((2, KV...]
where the time goes in v9:
time: 45.2 us; the launch traced here: 45 us
  Pallas kernels  43.5 us (96%)
  between operations  1.47 us (3%)
    pallas_call x1, Pallas kernels, device_fn(): pl.pallas_call(pipe_kernel, out_shape=(sds((2, KVW, LN), F32), sds((2, KV...  26.7 us
    pallas_call x1, Pallas kernels, device_fn(): pl.pallas_call(pre_kernel, out_shape=(cshape, cshape, tshape), in_specs=[...  9.26 us
    pallas_call x1, Pallas kernels, device_fn(): pl.pallas_call(post_kernel, out_shape=(cshape, cshape, pshape, pshape, lg...  4.19 us
    pallas_call x1, Pallas kernels, device_fn(): pl.pallas_call(head_kernel, out_shape=lgs, in_specs=[ANY] * 3, out_specs=...  3.2 us

profile of v9, /device:TPU:7, one launch (start us, length us, event | category | flops | bytes accessed | tf_op | source)
XLA Modules:
  0.0 45.0 jit_solution(7005860080968738483)
XLA Ops:
  1.3 9.3 %pre.1 = (bf16[4,8,3,64,512]{4,3,2,1,0:T(8,128)(2,1)}, bf16[4,8,3,64,512]{4,3,2,1,0:T(8,128)(2,1)}, f32[8,128]{1,0:T(8,128)}) custom-call(bf16[4,8,3,64,512]{4,3,2,1,0:T(8,128)(2,1)} %bitcast.40, bf16[4,8,3,64,512]{4,3,2,1,0:T(8,128)(2,1)} %bitcast.43), custom_call_target="tpu_custom_call" | custom-call | tf_op jit(solution)/shard_map/pre/pallas_call | solution.py:659
  10.5 26.7 %pipe.1 = (f32[2,192,128]{2,1,0:T(8,128)}, f32[2,192,128]{2,1,0:T(8,128)}, bf16[3,64,512]{2,1,0:T(8,128)(2,1)}, bf16[3,64,512]{2,1,0:T(8,128)(2,1)}, bf16[40,576]{1,0:T(8,128)(2,1)}) custom-call(bf16[32,576]{1,0:T(8,128)(2,1)} %bitcast.60, bf16[256,576]{1,0:T(8,128)(2,1)} %bitcast.53, s32[4,8]{1,0:T(4,128)} %dlen_h.3, s32[1]{0:T(128)S(6)} %copy.37.plen, ...), custom_call_target="tpu_custom_call" | custom-call | tf_op jit(solution)/shard_map/pipe/pallas_call | solution.py:663
  37.3 0.1 mid.1
  37.4 3.2 %head.1.lg = f32[9,4,1024]{2,1,0:T(4,128)} custom-call(bf16[40,576]{1,0:T(8,128)(2,1)} %get-tuple-element.28.fh, bf16[576,1024]{1,0:T(8,128)(2,1)} %wh.1, f32[8,128]{1,0:T(8,128)} %get-tuple-element.31.tok), custom_call_target="tpu_custom_call" | custom-call | tf_op jit(solution)/shard_map/head/pallas_call | solution.py:678
  40.6 4.2 %post.1 = (bf16[4,8,3,64,512]{4,3,2,1,0:T(8,128)(2,1)}, bf16[4,8,3,64,512]{4,3,2,1,0:T(8,128)(2,1)}, bf16[3,64,512]{2,1,0:T(8,128)(2,1)}, bf16[3,64,512]{2,1,0:T(8,128)(2,1)}, f32[9,4,1024]{2,1,0:T(4,128)}) custom-call(s32[4,8]{1,0:T(4,128)} %dlen_h.3, ...), custom_call_target="tpu_custom_call", output_to_operand_aliasing={{0}: (6, {}), {1}: (7, {}), {2}: (8, {}), {3}: (9, {})} | custom-call | tf_op jit(solution)/shard_map/post/pallas_call | solution.py:683

commit v10 on v9

--- a/solution.py
+++ b/solution.py
@@ -106,6 +106,10 @@
         pl.semaphore_signal(bar, inc=1, device_id={'stage': jnp.minimum(st + 1, LAST)}, device_id_type=MESH)
 
     wait('dl', 'pl', 'ifr')
+    start('kp', 'vp')
+    for m in range(2):
+        kcp[m].start()
+        vcp[m].start()
     p0 = pl_s[0]
     li = lane_iota((1, 2 * LN))
     fr = ifr_s[...]
@@ -124,10 +128,6 @@
     for k in range(2):
         pb_s[k] = jnp.zeros((CL, 2 * LN), BF16)
 
-    start('kp', 'vp')
-    for m in range(2):
-        kcp[m].start()
-        vcp[m].start()
     start('wo', 'gm')
 
     @pl.when(st > 0)

time: 45.2 us -> 45.2 us (level)
  no operation moved by 1% of the time
where the time goes in v10:
time: 45.2 us; the launch traced here: 45 us
  Pallas kernels  43.5 us (96%)
  between operations  1.47 us (3%)
    pallas_call x1, Pallas kernels, device_fn(): pl.pallas_call(pipe_kernel, out_shape=(sds((2, KVW, LN), F32), sds((2, KV...  26.7 us
    pallas_call x1, Pallas kernels, device_fn(): pl.pallas_call(pre_kernel, out_shape=(cshape, cshape, tshape), in_specs=[...  9.26 us
    pallas_call x1, Pallas kernels, device_fn(): pl.pallas_call(post_kernel, out_shape=(cshape, cshape, pshape, pshape, lg...  4.19 us
    pallas_call x1, Pallas kernels, device_fn(): pl.pallas_call(head_kernel, out_shape=lgs, in_specs=[ANY] * 3, out_specs=...  3.2 us

profile of v10, /device:TPU:7, one launch (start us, length us, event | category | flops | bytes accessed | tf_op | source)
XLA Modules:
  0.0 45.0 jit_solution(2936019204348834081)
XLA Ops:
  1.3 9.3 %pre.1 = (bf16[4,8,3,64,512]{4,3,2,1,0:T(8,128)(2,1)}, bf16[4,8,3,64,512]{4,3,2,1,0:T(8,128)(2,1)}, f32[8,128]{1,0:T(8,128)}) custom-call(bf16[4,8,3,64,512]{4,3,2,1,0:T(8,128)(2,1)} %bitcast.40, bf16[4,8,3,64,512]{4,3,2,1,0:T(8,128)(2,1)} %bitcast.43), custom_call_target="tpu_custom_call" | custom-call | tf_op jit(solution)/shard_map/pre/pallas_call | solution.py:659
  10.5 26.7 %pipe.1 = (f32[2,192,128]{2,1,0:T(8,128)}, f32[2,192,128]{2,1,0:T(8,128)}, bf16[3,64,512]{2,1,0:T(8,128)(2,1)}, bf16[3,64,512]{2,1,0:T(8,128)(2,1)}, bf16[40,576]{1,0:T(8,128)(2,1)}) custom-call(bf16[32,576]{1,0:T(8,128)(2,1)} %bitcast.60, bf16[256,576]{1,0:T(8,128)(2,1)} %bitcast.53, s32[4,8]{1,0:T(4,128)} %dlen_h.3, s32[1]{0:T(128)S(6)} %copy.37.plen, ...), custom_call_target="tpu_custom_call" | custom-call | tf_op jit(solution)/shard_map/pipe/pallas_call | solution.py:663
  37.3 0.1 mid.1
  37.4 3.2 %head.1.lg = f32[9,4,1024]{2,1,0:T(4,128)} custom-call(bf16[40,576]{1,0:T(8,128)(2,1)} %get-tuple-element.28.fh, bf16[576,1024]{1,0:T(8,128)(2,1)} %wh.1, f32[8,128]{1,0:T(8,128)} %get-tuple-element.31.tok), custom_call_target="tpu_custom_call" | custom-call | tf_op jit(solution)/shard_map/head/pallas_call | solution.py:678
  40.6 4.2 %post.1 = (bf16[4,8,3,64,512]{4,3,2,1,0:T(8,128)(2,1)}, bf16[4,8,3,64,512]{4,3,2,1,0:T(8,128)(2,1)}, bf16[3,64,512]{2,1,0:T(8,128)(2,1)}, bf16[3,64,512]{2,1,0:T(8,128)(2,1)}, f32[9,4,1024]{2,1,0:T(4,128)}) custom-call(s32[4,8]{1,0:T(4,128)} %dlen_h.3, ...), custom_call_target="tpu_custom_call", output_to_operand_aliasing={{0}: (6, {}), {1}: (7, {}), {2}: (8, {}), {3}: (9, {})} | custom-call | tf_op jit(solution)/shard_map/post/pallas_call | solution.py:683
